TPU v7x, 32 devices: a whole 2x2x4 slice. The times are simulated.
32 devices in a mesh: region: 8 (over z, core), feat: 4 (over y, x).
Axes of the slice: x: 2, y: 2, z: 4, core: 2. Of those that a mesh axis runs over, the one named last changes fastest.
Arguments:
- node_lat: bfloat16 [3072, 512], P(('region', 'feat')), may hold values from -6 to 6
- edge_lat: bfloat16 [24576, 512], P(('region', 'feat')), may hold values from -6 to 6
- receiver_row: int32 [24576], P('region'), may hold values from 0 to 383
- sender_slot: int32 [24576], P('region'), may hold values from 0 to 511, as said below
- send_rows: int32 [8, 8, 16], P('region'), may hold values from 0 to 383
- w_edge_in: bfloat16 [3, 512, 512], P(None, 'feat'), may hold values from -0.15625 to 0.15625
- w_edge_out: bfloat16 [512, 512], P('feat'), may hold values from -0.25 to 0.25
- w_node_in: bfloat16 [2, 512, 512], P(None, 'feat'), may hold values from -0.1875 to 0.1875
- w_node_out: bfloat16 [512, 512], P('feat'), may hold values from -0.25 to 0.25
- edge_gain: float32 [512], P('feat'), may hold values from 0.1 to 1.9
- node_gain: float32 [512], P('feat'), may hold values from 0.1 to 1.9
- node_cot: bfloat16 [3072, 512], P(('region', 'feat')), may hold values from -6 to 6
- edge_cot: bfloat16 [24576, 512], P(('region', 'feat')), may hold values from -6 to 6
Outputs:
- node_new: bfloat16 [3072, 512], P(('region', 'feat'))
- edge_new: bfloat16 [24576, 512], P(('region', 'feat'))
- node_grad: float32 [3072, 512], P(('region', 'feat'))
- edge_grad: float32 [24576, 512], P(('region', 'feat'))
- grad_edge_in: float32 [3, 512, 512], P(None, 'feat')
- grad_edge_out: float32 [512, 512], P('feat')
- grad_node_in: float32 [2, 512, 512], P(None, 'feat')
- grad_node_out: float32 [512, 512], P('feat')
Inputs may be any that keep to these rules, and one draw needn't show every extreme that they name: `receiver_row`: edge e lies in region e // 3072; its receiver is that row of the region's 384 nodes. `sender_slot`: A value below 384 is a row of the edge's own region; a value 384 + p * 16 + s names the node that region p lists in slot s for the edge's region, and p is never the edge's own region. send_rows[p, r, s] is a row of region p's 384 nodes.
All inputs are finite; a program needn't handle non-finite values.
Results may differ from a plain program's by a relative error of at most 0.02.
Values may be sent and summed in bfloat16 or wider, within the bound.
No kernel may reach another device: no remote copies, remote signals or barrier semaphores. Data moves between devices by JAX's collectives and lax.ppermute only.
A program may use at most 64 MiB of HBM per device.

v0:
```python
import functools

import jax
import jax.numpy as jnp
from jax import lax
from jax.experimental import pallas as pl
from jax.experimental.pallas import tpu as pltpu
from jax.sharding import PartitionSpec as P


EPSILON = 1e-05
F32 = jnp.float32
BF16 = jnp.bfloat16
VMEM_LIMIT = 36 * 1024 * 1024


def dot(a, b):
    return jnp.dot(a, b, preferred_element_type=F32)


def dot_t(a, b):
    return lax.dot_general(a, b, (((1,), (1,)), ((), ())), preferred_element_type=F32)


def t_dot(a, b):
    return lax.dot_general(a, b, (((0,), (0,)), ((), ())), preferred_element_type=F32)


def swap(x, axis, bits):
    n = lax.axis_size(axis)
    return lax.ppermute(x, axis, [(i, i ^ bits) for i in range(n)])


def feat_swaps(parts):
    return [parts[0]] + [swap(parts[b], "feat", b) for b in range(1, len(parts))]


def add_all(parts):
    total = parts[0].astype(F32)
    for part in parts[1:]:
        total = total + part.astype(F32)
    return total


def layer_norm(values):
    breadth = values.shape[1]
    average = jnp.sum(values, axis=1, keepdims=True) / breadth
    variance = jnp.sum(values * values, axis=1, keepdims=True) / breadth - average * average
    inverse = lax.rsqrt(variance + EPSILON)
    return (values - average) * inverse, inverse


def layer_norm_back(scaled, normed, inverse):
    breadth = scaled.shape[1]
    first = jnp.sum(scaled, axis=1, keepdims=True) / breadth
    second = jnp.sum(scaled * normed, axis=1, keepdims=True) / breadth
    return (inverse * (scaled - first - normed * second)).astype(BF16)


def swish_and_slope(values):
    s = 1.0 / (1.0 + jnp.exp(-values))
    return (values * s).astype(BF16), s * (1.0 + values * (1.0 - s))


def hot(column, width):
    at = lax.broadcasted_iota(jnp.int32, (column.shape[0], width), 1)
    return jnp.where(column == at, 1.0, 0.0).astype(BF16)


def hot_t(row, height):
    at = lax.broadcasted_iota(jnp.int32, (height, row.shape[1]), 0)
    return jnp.where(row == at, 1.0, 0.0).astype(BF16)


def tile_of(rows):
    for size in (256, 192, 128, 96, 64, 48, 32, 16):
        if rows % size == 0:
            return size
    return rows


def shape(dims, dtype=BF16):
    return jax.ShapeDtypeStruct(tuple(dims), dtype)


def whole_block(dims):
    return pl.BlockSpec(tuple(dims), lambda *_: (0,) * len(dims))


def call(kernel, ins, outs, scratch=(), flops=0):
    return pl.pallas_call(
        kernel,
        out_shape=tuple(outs),
        grid=(1,),
        in_specs=[whole_block(x.shape) for x in ins],
        out_specs=tuple(whole_block(x.shape) for x in outs),
        scratch_shapes=list(scratch),
        compiler_params=pltpu.CompilerParams(vmem_limit_bytes=VMEM_LIMIT),
        cost_estimate=pl.CostEstimate(
            flops=flops,
            bytes_accessed=sum(x.size * x.dtype.itemsize for x in (*ins, *outs)),
            transcendentals=0,
        ),
    )(*ins)


def fill_weights(w_ref, own_in, own_out, pieces, parity, here):
    m = w_ref.shape[0]
    portion = own_out.shape[0]
    half = portion // 2
    at = pl.multiple_of(here * portion, half)
    for k in range(m):
        w_ref[k, pl.ds(at, portion), :] = own_in[k] if k < m - 1 else own_out[...]
    for b, (got, other) in enumerate(pieces, start=1):
        start = (here ^ b) * portion
        first = pl.multiple_of(start + parity * half, half)
        second = pl.multiple_of(start + (1 - parity) * half, half)
        for k in range(m):
            w_ref[k, pl.ds(first, half), :] = got[k * half : (k + 1) * half, :]
            w_ref[k, pl.ds(second, half), :] = other[k * half : (k + 1) * half, :]


def split_grads(grads, n, keep, send, parity, here):
    m = grads.shape[0]
    portion = grads.shape[1] // n
    half = portion // 2
    block = m * half
    for side in range(2):

        @pl.when(parity == side)
        def _():
            for f in range(n):
                for u in range(2 * m):
                    out = keep if u // m == side else send
                    at = f * portion + (u % 2) * half
                    start = pl.multiple_of((f ^ here) * block + (u % m) * half, half)
                    out[pl.ds(start, half), :] = grads[u // 2, at : at + half, :].astype(BF16)


def pack_kernel(inner, outer, *refs):
    gains, pack, sems = refs[:-2], refs[-2], refs[-1]
    half = outer.shape[0] // 2
    m = inner.shape[0] + 1
    at = pl.multiple_of(lax.axis_index("region") % 2 * half, half)
    copies = []
    for k in range(m):
        source = inner.at[k, pl.ds(at, half)] if k < m - 1 else outer.at[pl.ds(at, half)]
        copies.append(pltpu.make_async_copy(source, pack.at[pl.ds(k * half, half)], sems.at[k]))
        copies[-1].start()
    if gains:
        parts = []
        for gain in gains:
            left = gain[...]
            for _ in range(3):
                part = left.astype(BF16)
                left = left - part.astype(F32)
                parts.append(part.astype(F32))
        parts.append(jnp.zeros((16 - len(parts), left.shape[1]), F32))
        pack[m * half :, :] = jnp.zeros((16, pack.shape[1]), BF16)
        pack[m * half :, : left.shape[1]] = jnp.concatenate(parts, axis=0).astype(BF16)
    for copy in copies:
        copy.wait()


def pack_halves(inner, outer, gains):
    m, d = inner.shape[0] + 1, inner.shape[2]
    rows = m * (outer.shape[0] // 2) + (16 if gains else 0)
    return pl.pallas_call(
        pack_kernel,
        out_shape=shape((rows, d)),
        grid=(1,),
        in_specs=[pl.BlockSpec(memory_space=pltpu.HBM)] * 2 + [whole_block(x.shape) for x in gains],
        out_specs=whole_block((rows, d)),
        scratch_shapes=[pltpu.SemaphoreType.DMA((m,))],
        compiler_params=pltpu.CompilerParams(vmem_limit_bytes=VMEM_LIMIT),
        cost_estimate=pl.CostEstimate(flops=rows * d, bytes_accessed=4 * rows * d, transcendentals=0),
    )(inner, outer, *gains)


def fill_gains(gain_ref, blocks, own, pieces, here):
    portion = blocks.shape[2]
    blocks[here, 0:1, :] = own[0][...]
    blocks[here, 1:2, :] = own[1][...]
    for b, (got, _) in enumerate(pieces, start=1):
        parts = got[got.shape[0] - 16 :, :portion].astype(F32)
        blocks[here ^ b, 0:1, :] = parts[0:1] + parts[1:2] + parts[2:3]
        blocks[here ^ b, 1:2, :] = parts[3:4] + parts[4:5] + parts[5:6]
    for f in range(blocks.shape[0]):
        gain_ref[0:2, f * portion : (f + 1) * portion] = blocks[f, 0:2, :]


def outgoing_kernel(n, at_ref, *refs):
    near, (keep, send) = refs[:n], refs[n : n + 2]
    own = near[0].shape[0]
    rows = jnp.zeros((at_ref.shape[0], near[0].shape[1]), F32)
    for b in range(n):
        rows = rows + dot(hot(at_ref[...] - b * own, own), near[b][...])
    rows = rows.astype(BF16)
    pairs, slots, _ = keep.shape
    for b in range(pairs):
        keep[b] = rows[(2 * b) * slots : (2 * b + 1) * slots]
        send[b] = rows[(2 * b + 1) * slots : (2 * b + 2) * slots]


def edge_forward_kernel(n, pairs, *refs):
    edge, s_at, r_at, r_row, edge_gain, node_gain, own_in, own_out = refs[:8]
    refs = refs[8:]
    tables, refs = refs[: n + pairs], refs[n + pairs :]
    pieces = [(refs[2 * b], refs[2 * b + 1]) for b in range(n - 1)]
    refs = refs[2 * (n - 1) :]
    new, hidden_ref, slope_ref, normed_ref, inverse_ref, table, w, gains = refs[:8]
    pooled, total, blocks = refs[8 : 8 + n], refs[8 + n], refs[9 + n]
    here = lax.axis_index("feat")
    parity = lax.axis_index("region") % 2
    own = tables[0].shape[0]
    nodes = own * n

    @pl.when(pl.program_id(0) == 0)
    def _():
        at = 0
        for piece in tables:
            table[at : at + piece.shape[0], :] = piece[...]
            at += piece.shape[0]
        fill_weights(w, own_in, own_out, pieces, parity, here)
        fill_gains(gains, blocks, (edge_gain, node_gain), pieces, here)
        total[...] = jnp.zeros_like(total)

    lat = edge[...]
    senders = dot(hot(s_at[...], table.shape[0]), table[...]).astype(BF16)
    receivers = dot(hot(r_at[...], nodes), table[:nodes, :]).astype(BF16)
    pre = dot(lat, w[0]) + dot(senders, w[1]) + dot(receivers, w[2])
    hidden, slope = swish_and_slope(pre)
    hidden_ref[...] = hidden
    slope_ref[...] = slope.astype(BF16)
    normed, inverse = layer_norm(dot(hidden, w[3]))
    normed_ref[...] = normed.astype(BF16)
    inverse_ref[...] = jnp.broadcast_to(inverse, inverse_ref.shape)
    updated = (lat.astype(F32) + normed * gains[0:1, :]).astype(BF16)
    new[...] = updated
    total[...] += dot(hot_t(r_row[...], nodes), updated)

    @pl.when(pl.program_id(0) == pl.num_programs(0) - 1)
    def _():
        for b in range(n):
            pooled[b][...] = total[b * own : (b + 1) * own, :].astype(BF16)


def node_kernel(n, lat_ref, cot_ref, gains, own_in, own_out, *refs):
    parts, refs = refs[:n], refs[n:]
    pieces = [(refs[2 * b], refs[2 * b + 1]) for b in range(n - 1)]
    refs = refs[2 * (n - 1) :]
    new, pooled_grad, base = refs[:3]
    messages, w = refs[3 : 3 + n], refs[3 + n]
    here = lax.axis_index("feat")
    parity = lax.axis_index("region") % 2
    gain = gains[1:2, :]
    fill_weights(w, own_in, own_out, pieces, parity, here)
    pooled = add_all([part[...] for part in parts]).astype(BF16)
    lat = lat_ref[...]
    pre = dot(lat, w[0]) + dot(pooled, w[1])
    hidden, slope = swish_and_slope(pre)
    normed, inverse = layer_norm(dot(hidden, w[2]))
    new[...] = (lat.astype(F32) + normed * gain).astype(BF16)
    cot = cot_ref[...].astype(F32)
    mix_grad = layer_norm_back(cot * gain, normed, inverse)
    pre_grad = (dot_t(mix_grad, w[2]) * slope).astype(BF16)
    pooled_grad[...] = dot_t(pre_grad, w[1]).astype(BF16)
    base[...] = cot + dot_t(pre_grad, w[0])
    d = lat.shape[1]
    portion = d // n
    for b in range(n):
        messages[b][:, :d] = pre_grad
        messages[b][:, d : 2 * d] = mix_grad
    for f in range(n):

        @pl.when(here == f)
        def _():
            for b in range(n):
                block = slice((f ^ b) * portion, ((f ^ b) + 1) * portion)
                messages[b][:, 2 * d : 2 * d + portion] = pooled[:, block]
                messages[b][:, 2 * d + portion :] = hidden[:, block]


def node_weight_kernel(n, *refs):
    near, messages, (keep, send, lat, grads) = refs[:n], refs[n : 2 * n], refs[2 * n :]
    here = lax.axis_index("feat")
    parity = lax.axis_index("region") % 2
    _, d = near[0].shape
    portion = d // n
    for f in range(n):

        @pl.when(here == f)
        def _():
            for b in range(n):
                lat[b] = near[b][:, f * portion : (f + 1) * portion]

    totals = [jnp.zeros((portion, d), F32)] * 3
    for b in range(n):
        pre_grad = messages[b][:, :d]
        mix_grad = messages[b][:, d : 2 * d]
        totals[0] = totals[0] + t_dot(lat[b], pre_grad)
        totals[1] = totals[1] + t_dot(messages[b][:, 2 * d : 2 * d + portion], pre_grad)
        totals[2] = totals[2] + t_dot(messages[b][:, 2 * d + portion :], mix_grad)
    for k in range(3):
        grads[k * portion : (k + 1) * portion, :] = totals[k]
    half = keep.shape[0]
    keep[...] = grads[pl.ds(pl.multiple_of(parity * half, 16), half), :].astype(BF16)
    send[...] = grads[pl.ds(pl.multiple_of((1 - parity) * half, 16), half), :].astype(BF16)


def edge_backward_kernel(n, slots, *refs):
    edge, cot, hidden, slope, normed, inverse, r_at, s_row, r_row, gains, table, w = refs[:12]
    near, refs = refs[12 : 12 + n], refs[12 + n :]
    edge_grad, keep, send, near_grad = refs[:4]
    near_all, grads, sent, received = refs[4:]
    here = lax.axis_index("feat")
    parity = lax.axis_index("region") % 2
    own = near[0].shape[0]
    nodes = own * n

    @pl.when(pl.program_id(0) == 0)
    def _():
        for b in range(n):
            near_all[b * own : (b + 1) * own, :] = near[b][...]
        grads[...] = jnp.zeros_like(grads)
        sent[...] = jnp.zeros_like(sent)
        received[...] = jnp.zeros_like(received)

    total = cot[...].astype(F32) + dot(hot(r_at[...], nodes), near_all[...])
    mix_grad = layer_norm_back(total * gains[0:1, :], normed[...].astype(F32), inverse[:, :1])
    pre_grad = (dot_t(mix_grad, w[3]) * slope[...].astype(F32)).astype(BF16)
    edge_grad[...] = total + dot_t(pre_grad, w[0])
    grads[0] += t_dot(edge[...], pre_grad)
    grads[3] += t_dot(hidden[...], mix_grad)
    sent[...] += dot(hot_t(s_row[...], table.shape[0]), pre_grad)
    received[...] += dot(hot_t(r_row[...], nodes), pre_grad)

    @pl.when(pl.program_id(0) == pl.num_programs(0) - 1)
    def _():
        from_senders = sent[...].astype(BF16)
        from_receivers = received[...].astype(BF16)
        grads[1] = t_dot(table[...], from_senders)
        grads[2] = t_dot(table[:nodes, :], from_receivers)
        split_grads(grads, n, keep, send, parity, here)
        to_table = dot_t(from_senders, w[1])
        near_grad[...] = to_table[:nodes] + dot_t(from_receivers, w[2])
        back = to_table[nodes:].astype(BF16)
        at = n * grads.shape[0] * (grads.shape[1] // n // 2)
        count = (keep.shape[0] - at) // slots
        for b in range(count):
            rows = slice(at + b * slots, at + (b + 1) * slots)
            keep[rows, :] = back[(2 * b) * slots : (2 * b + 1) * slots]
            send[rows, :] = back[(2 * b + 1) * slots : (2 * b + 2) * slots]


def return_kernel(n, pairs, near_grad, at_row, *refs):
    blocks, outs = refs[:pairs], refs[pairs:]
    nodes, _ = near_grad.shape
    own = nodes // n
    rows = blocks[0].shape[0]
    total = near_grad[...]
    for b in range(pairs):
        total = total + dot(hot_t(at_row[:, b * rows : (b + 1) * rows], nodes), blocks[b][...])
    for b in range(n):
        outs[b][...] = total[b * own : (b + 1) * own, :].astype(BF16)


def pair_sum_kernel(n, slots, keep, got, *outs):
    block = outs[0].shape[0]
    for b in range(n):
        rows = slice(b * block, (b + 1) * block)
        outs[b][...] = (keep[rows, :].astype(F32) + got[rows, :].astype(F32)).astype(BF16)
    for b, out in enumerate(outs[n:]):
        rows = slice(n * block + b * slots, n * block + (b + 1) * slots)
        out[:slots, :] = keep[rows, :]
        out[slots:, :] = got[rows, :]


def scatter_sum_kernel(n, pairs, *refs):
    parts, node_parts = refs[:n], refs[n : n + 2]
    outs, total = refs[n + 2 : n + 2 + pairs], refs[n + 2 + pairs]
    z = lax.axis_index("region") // 2
    cut = parts[0].shape[0]
    total[:cut, :] = add_all([part[...] for part in parts])
    total[cut:, :] = add_all([part[...] for part in node_parts])
    rows = outs[0].shape[0]
    for b in range(pairs):
        outs[b][...] = total[pl.ds(pl.multiple_of((z ^ b) * rows, rows), rows), :].astype(BF16)


def sum_kernel(*refs):
    refs[-1][...] = add_all([part[...] for part in refs[:-1]]).astype(BF16)


def finish_kernel(pairs, edge_norm, node_norm, *refs):
    mine, theirs = refs[:pairs], refs[pairs : 2 * pairs]
    outs, total = refs[2 * pairs : -1], refs[-1]
    region = lax.axis_index("region")
    parity, z = region % 2, region // 2
    rows = mine[0].shape[0]
    for b in range(pairs):
        at = (z ^ b) * rows
        for side, ref in ((parity, mine[b]), (1 - parity, theirs[b])):
            start = pl.multiple_of(side * pairs * rows + at, rows)
            total[pl.ds(start, rows), :] = ref[...].astype(F32)
    spread(total, outs, edge_norm, node_norm)


def spread(total, outs, edge_norm, node_norm):
    portion = outs[1].shape[0]
    size = total.shape[0] // 2
    for norm, m, at, pair in ((edge_norm, 4, 0, outs[:2]), (node_norm, 3, 2 * portion, outs[2:])):
        half = m * portion // 2
        for u in range(2 * m):
            row = u * (portion // 2)
            source = (row // half) * size + at + row % half
            out, start = (pair[0], row) if u < 2 * m - 2 else (pair[1], row - (m - 1) * portion)
            out[start : start + portion // 2, :] = total[source : source + portion // 2, :] * norm


def gather_halves(mine):
    pieces = []
    for b in range(1, lax.axis_size("feat")):
        got = swap(mine, "feat", b)
        pieces += [got, swap(got, "region", 1)]
    return pieces


def chip_exchange(blocks):
    return [blocks[0]] + [swap(blocks[b], "region", 2 * b) for b in range(1, len(blocks))]


def reduce_grads(parts, node_parts, portion, edge_norm, node_norm):
    n = len(parts)
    half, d = parts[0].shape
    pairs = lax.axis_size("region") // 2
    z = lax.axis_index("region") // 2
    parity = lax.axis_index("region") % 2
    size = half + node_parts[0].shape[0]
    rows = size // pairs
    outs = [shape((k * portion, d), F32) for k in (3, 1, 2, 1)]
    if rows % 16 == 0:
        parts = call(
            functools.partial(scatter_sum_kernel, n, pairs),
            [*parts, *node_parts],
            [shape((rows, d))] * pairs,
            [pltpu.VMEM((size, d), F32)],
        )
    else:
        mine = jnp.concatenate([add_all(parts), add_all(node_parts)]).astype(BF16).reshape(pairs, rows, d)
        parts = [lax.dynamic_index_in_dim(mine, z ^ b, 0, keepdims=False) for b in range(pairs)]
    parts = chip_exchange(parts)
    if rows % 16 == 0:
        (chunk,) = call(sum_kernel, parts, [shape((rows, d))])
    else:
        chunk = add_all(parts).astype(BF16)
    mine = chip_exchange([chunk] * pairs)
    theirs = [swap(piece, "region", 1) for piece in mine]
    if rows % 16 == 0:
        return call(
            functools.partial(finish_kernel, pairs, edge_norm, node_norm),
            mine + theirs,
            outs,
            [pltpu.VMEM((2 * size, d), F32)],
        )
    order = jnp.arange(pairs) ^ z
    sides = [jnp.stack(side)[order].reshape(size, d) for side in (mine, theirs)]
    total = jnp.where(parity == 0, jnp.concatenate(sides), jnp.concatenate(sides[::-1])).astype(F32)

    def from_total(*refs):
        spread(refs[0], refs[1:], edge_norm, node_norm)

    return call(from_total, [total], outs)


def layer(
    node_lat,
    edge_lat,
    receiver_row,
    sender_slot,
    send_rows,
    w_edge_in,
    w_edge_out,
    w_node_in,
    w_node_out,
    edge_gain,
    node_gain,
    node_cot,
    edge_cot,
):
    n = lax.axis_size("feat")
    regions = lax.axis_size("region")
    pairs = regions // 2
    here = lax.axis_index("feat")
    region = lax.axis_index("region")
    own, d = node_lat.shape
    nodes = own * n
    share = edge_lat.shape[0]
    slots = send_rows.shape[2]
    table_size = nodes + regions * slots

    def relative(row):
        return ((row // own) ^ here) * own + row % own

    local_receivers = lax.dynamic_slice_in_dim(receiver_row, here * share, share)
    local_senders = lax.dynamic_slice_in_dim(sender_slot, here * share, share)
    remote = jnp.maximum(local_senders - nodes, 0)
    sender_at = jnp.where(
        local_senders < nodes,
        relative(local_senders),
        nodes + ((remote // slots) ^ region) * slots + remote % slots,
    )
    receiver_at = relative(local_receivers)
    send_at = relative(send_rows[0])[jnp.arange(regions) ^ region].reshape(-1)

    portion = d // n
    half = portion // 2
    gain_rows = [edge_gain[None], node_gain[None]]
    near = feat_swaps([node_lat] * n)
    edge_pack = pack_halves(w_edge_in, w_edge_out, gain_rows)
    node_pack = pack_halves(w_node_in, w_node_out, [])
    w_edge = gather_halves(edge_pack)

    square = 2 * d * d
    keep, send = call(
        functools.partial(outgoing_kernel, n),
        [send_at[:, None], *near],
        [shape((pairs, slots, d))] * 2,
        flops=2 * regions * slots * nodes * d,
    )
    other = swap(send, "region", 1)
    remote_rows = chip_exchange([jnp.concatenate([keep[b], other[b]], axis=0) for b in range(pairs)])
    w_node = gather_halves(node_pack)

    tile = tile_of(share)
    steps = share // tile
    by_rows = lambda width: pl.BlockSpec((tile, width), lambda i: (i, 0))
    by_columns = pl.BlockSpec((1, tile), lambda i: (0, i))
    edge_params = pltpu.CompilerParams(
        dimension_semantics=("arbitrary",), vmem_limit_bytes=VMEM_LIMIT
    )
    ins = [edge_lat, sender_at[:, None], receiver_at[:, None], receiver_at[None]]
    rest = [*gain_rows, w_edge_in, w_edge_out, *near, *remote_rows, *w_edge]
    outs = [shape((share, d))] * 4 + [shape((share, 128), F32)]
    kept = [shape((table_size, d)), shape((4, d, d)), shape((8, d), F32)] + [shape((own, d))] * n
    edge_new, hidden, slope, normed, inverse, table, w_full, gains, *pooled_parts = pl.pallas_call(
        functools.partial(edge_forward_kernel, n, pairs),
        out_shape=tuple(outs + kept),
        grid=(steps,),
        in_specs=[by_rows(d), by_rows(1), by_rows(1), by_columns]
        + [whole_block(x.shape) for x in rest],
        out_specs=tuple([by_rows(d)] * 4 + [by_rows(128)] + [whole_block(x.shape) for x in kept]),
        scratch_shapes=[pltpu.VMEM((nodes, d), F32), pltpu.VMEM((n, 8, portion), F32)],
        compiler_params=edge_params,
        cost_estimate=pl.CostEstimate(
            flops=7 * share * square, bytes_accessed=8 * share * d, transcendentals=share * d
        ),
        name="edge_forward",
    )(*ins, *rest)

    parts = feat_swaps(pooled_parts)
    node_new, pooled_grad, node_base, *messages = call(
        functools.partial(node_kernel, n),
        [node_lat, node_cot, gains, w_node_in, w_node_out, *parts, *w_node],
        [shape((own, d)), shape((own, d)), shape((own, d), F32)]
        + [shape((own, 2 * d + 2 * portion))] * n,
        [pltpu.VMEM((3, d, d), BF16)],
        flops=6 * own * square,
    )
    grad_near = feat_swaps([pooled_grad] * n)
    messages = feat_swaps(messages)

    ins = [edge_lat, edge_cot, hidden, slope, normed, inverse, receiver_at[:, None], sender_at[None], receiver_at[None]]
    rest = [gains, table, w_full, *grad_near]
    kept = [shape((n * 2 * portion + pairs * slots, d))] * 2 + [shape((nodes, d), F32)]
    edge_grad, keep, send, near_grad = pl.pallas_call(
        functools.partial(edge_backward_kernel, n, slots),
        out_shape=tuple([shape((share, d), F32)] + kept),
        grid=(steps,),
        in_specs=[by_rows(d)] * 5 + [by_rows(128), by_rows(1), by_columns, by_columns]
        + [whole_block(x.shape) for x in rest],
        out_specs=tuple([by_rows(d)] + [whole_block(x.shape) for x in kept]),
        scratch_shapes=[
            pltpu.VMEM((nodes, d), BF16),
            pltpu.VMEM((4, d, d), F32),
            pltpu.VMEM((table_size, d), F32),
            pltpu.VMEM((nodes, d), F32),
        ],
        compiler_params=edge_params,
        cost_estimate=pl.CostEstimate(
            flops=10 * share * square, bytes_accessed=16 * share * d, transcendentals=0
        ),
        name="edge_backward",
    )(*ins, *rest)
    got = swap(send, "region", 1)
    node_keep, node_send = call(
        functools.partial(node_weight_kernel, n),
        [*near, *messages],
        [shape((3 * half, d))] * 2,
        [pltpu.VMEM((n, own, portion), BF16), pltpu.VMEM((3 * portion, d), F32)],
        flops=3 * nodes * square // n,
    )
    node_got = swap(node_send, "region", 1)
    outs = call(
        functools.partial(pair_sum_kernel, n, slots),
        [keep, got],
        [shape((4 * half, d))] * n + [shape((2 * slots, d))] * pairs,
    )
    parts = feat_swaps(outs[:n])
    returned = chip_exchange(outs[n:])
    grad_edge_in, grad_edge_out, grad_node_in, grad_node_out = reduce_grads(
        parts,
        [node_keep, node_got],
        portion,
        float((share * n * regions) ** -0.5),
        float((nodes * regions) ** -0.5),
    )

    parts = call(
        functools.partial(return_kernel, n, pairs),
        [near_grad, send_at[None], *returned],
        [shape((own, d))] * n,
        flops=2 * regions * slots * nodes * d,
    )
    node_grad = node_base + add_all(feat_swaps(parts))

    return (
        node_new,
        edge_new,
        node_grad,
        edge_grad,
        grad_edge_in.reshape(w_edge_in.shape),
        grad_edge_out,
        grad_node_in.reshape(w_node_in.shape),
        grad_node_out,
    )


def solution(mesh):
    rows = P(("region", "feat"), None)
    in_specs = (
        rows,
        rows,
        P("region"),
        P("region"),
        P("region", None, None),
        P(None, "feat", None),
        P("feat", None),
        P(None, "feat", None),
        P("feat", None),
        P("feat"),
        P("feat"),
        rows,
        rows,
    )
    out_specs = (
        rows,
        rows,
        rows,
        rows,
        P(None, "feat", None),
        P("feat", None),
        P(None, "feat", None),
        P("feat", None),
    )
    return jax.shard_map(layer, mesh=mesh, in_specs=in_specs, out_specs=out_specs, check_vma=False)
```

profile of v0, /device:TPU:0, one launch (start us, length us, event | category | flops | bytes accessed | tf_op | source)
XLA Modules:
  0.0 130.4 jit_solution(451488523790076579)
XLA Ops:
  0.6 3.0 %collective-permute-start = (bf16[96,512]{1,0:T(8,128)(2,1)}, bf16[96,512]{1,0:T(8,128)(2,1)S(1)}, u32[]{:S(2)}, u32[]{:S(2)}) collective-permute-start(bf16[96,512]{1,0:T(8,128)(2,1)} %refs_0_.7), channel_id=1, source_target_pairs={{0,1},{1,0},{2,3},{3,2},{4,5},{5,4},{6,7},{7,6},{8,9},{9,8},{10,11... | collective-permute-start | bytes 294920 | tf_op jit(solution)/shard_map/ppermute | solution.py:31
  3.7 1.5 %collective-permute-start.1 = (bf16[96,512]{1,0:T(8,128)(2,1)}, bf16[96,512]{1,0:T(8,128)(2,1)S(1)}, u32[]{:S(2)}, u32[]{:S(2)}) collective-permute-start(bf16[96,512]{1,0:T(8,128)(2,1)} %refs_0_.7), channel_id=1, source_target_pairs={{0,2},{1,3},{2,0},{3,1},{4,6},{5,7},{6,4},{7,5},{8,10},{9,11},{10,... | collective-permute-start | bytes 294920 | tf_op jit(solution)/shard_map/ppermute | solution.py:31
  5.2 1.0 copy-done.5
  8.8 2.0 %collective-permute-start.9 = (bf16[272,512]{1,0:T(8,128)(2,1)S(1)}, bf16[272,512]{1,0:T(8,128)(2,1)S(1)}, u32[]{:S(2)}, u32[]{:S(2)}) collective-permute-start(bf16[272,512]{1,0:T(8,128)(2,1)S(1)} %shard_map.189), channel_id=1, source_target_pairs={{0,2},{1,3},{2,0},{3,1},{4,6},{5,7},{6,4},{7,5},{8,10},{9,11},{10,... | collective-permute-start | bytes 835592 | tf_op jit(solution)/shard_map/ppermute | solution.py:31
  10.8 1.4 %collective-permute-start.11 = (bf16[272,512]{1,0:T(8,128)(2,1)S(1)}, bf16[272,512]{1,0:T(8,128)(2,1)S(1)}, u32[]{:S(2)}, u32[]{:S(2)}) collective-permute-start(bf16[272,512]{1,0:T(8,128)(2,1)S(1)} %shard_map.189), channel_id=1, source_target_pairs={{0,3},{1,2},{2,1},{3,0},{4,7},{5,6},{6,5},{7,4},{8,11},{9,10},{10,... | collective-permute-start | bytes 835592 | tf_op jit(solution)/shard_map/ppermute | solution.py:31
  16.0 1.9 %collective-permute-start.16 = (bf16[192,512]{1,0:T(8,128)(2,1)S(1)}, bf16[192,512]{1,0:T(8,128)(2,1)S(1)}, u32[]{:S(2)}, u32[]{:S(2)}) collective-permute-start(bf16[192,512]{1,0:T(8,128)(2,1)S(1)} %shard_map.190), channel_id=1, source_target_pairs={{0,1},{1,0},{2,3},{3,2},{4,5},{5,4},{6,7},{7,6},{8,9},{9,8},{10,11... | collective-permute-start | bytes 589832 | tf_op jit(solution)/shard_map/ppermute | solution.py:31
  18.4 1.2 collective-permute-done.3
  19.6 1.6 %collective-permute-start.4 = (bf16[32,512]{1,0:T(8,128)(2,1)S(1)}, bf16[32,512]{1,0:T(8,128)(2,1)S(1)}, u32[]{:S(2)}, u32[]{:S(2)}) collective-permute-start(bf16[32,512]{1,0:T(8,128)(2,1)S(1)} %pad_maximum_fusion.1), channel_id=1, source_target_pairs={{0,8},{4,12},{8,0},{12,4},{16,24},{20,28},{24,16},{28,20},{1,9},{5... | collective-permute-start | bytes 98312 | tf_op jit(solution)/shard_map/ppermute | solution.py:31
  21.3 2.3 %collective-permute-done.4.refs_13_ = bf16[32,512]{1,0:T(8,128)(2,1)S(1)} collective-permute-done((bf16[32,512]{1,0:T(8,128)(2,1)S(1)}, bf16[32,512]{1,0:T(8,128)(2,1)S(1)}, u32[]{:S(2)}, u32[]{:S(2)}) %collective-permute-start.4) | collective-permute-done | bytes 32800 | tf_op jit(solution)/shard_map/ppermute | solution.py:31
  23.6 2.6 %collective-permute-start.5 = (bf16[32,512]{1,0:T(8,128)(2,1)S(1)}, bf16[32,512]{1,0:T(8,128)(2,1)S(1)}, u32[]{:S(2)}, u32[]{:S(2)}) collective-permute-start(bf16[32,512]{1,0:T(8,128)(2,1)S(1)} %pad_maximum_fusion.2), channel_id=1, source_target_pairs={{0,16},{4,20},{8,24},{12,28},{16,0},{20,4},{24,8},{28,12},{1,17},{... | collective-permute-start | bytes 98312 | tf_op jit(solution)/shard_map/ppermute | solution.py:31
  26.8 1.6 %collective-permute-done.5.refs_14_ = bf16[32,512]{1,0:T(8,128)(2,1)S(1)} collective-permute-done((bf16[32,512]{1,0:T(8,128)(2,1)S(1)}, bf16[32,512]{1,0:T(8,128)(2,1)S(1)}, u32[]{:S(2)}, u32[]{:S(2)}) %collective-permute-start.5) | collective-permute-done | bytes 32800 | tf_op jit(solution)/shard_map/ppermute | solution.py:31
  28.4 3.8 %collective-permute-start.6 = (bf16[32,512]{1,0:T(8,128)(2,1)S(1)}, bf16[32,512]{1,0:T(8,128)(2,1)S(1)}, u32[]{:S(2)}, u32[]{:S(2)}) collective-permute-start(bf16[32,512]{1,0:T(8,128)(2,1)S(1)} %pad_maximum_fusion.3), channel_id=1, source_target_pairs={{0,24},{4,28},{8,16},{12,20},{16,8},{20,12},{24,0},{28,4},{1,25},{... | collective-permute-start | bytes 98312 | tf_op jit(solution)/shard_map/ppermute | solution.py:31
  32.2 1.9 %collective-permute-done.6.refs_15_ = bf16[32,512]{1,0:T(8,128)(2,1)S(1)} collective-permute-done((bf16[32,512]{1,0:T(8,128)(2,1)S(1)}, bf16[32,512]{1,0:T(8,128)(2,1)S(1)}, u32[]{:S(2)}, u32[]{:S(2)}) %collective-permute-start.6) | collective-permute-done | bytes 32800 | tf_op jit(solution)/shard_map/ppermute | solution.py:31
  34.1 1.5 %collective-permute-start.18 = (bf16[192,512]{1,0:T(8,128)(2,1)S(1)}, bf16[192,512]{1,0:T(8,128)(2,1)S(1)}, u32[]{:S(2)}, u32[]{:S(2)}) collective-permute-start(bf16[192,512]{1,0:T(8,128)(2,1)S(1)} %shard_map.190), channel_id=1, source_target_pairs={{0,2},{1,3},{2,0},{3,1},{4,6},{5,7},{6,4},{7,5},{8,10},{9,11},{10,... | collective-permute-start | bytes 589832 | tf_op jit(solution)/shard_map/ppermute | solution.py:31
  37.3 5.5 %collective-permute-done.18.refs_6_ = bf16[192,512]{1,0:T(8,128)(2,1)S(1)} collective-permute-done((bf16[192,512]{1,0:T(8,128)(2,1)S(1)}, bf16[192,512]{1,0:T(8,128)(2,1)S(1)}, u32[]{:S(2)}, u32[]{:S(2)}) %collective-permute-start.18) | collective-permute-done | bytes 196640 | tf_op jit(solution)/shard_map/ppermute | solution.py:31
  43.5 7.4 %edge_forward.1 = (bf16[768,512]{1,0:T(8,128)(2,1)}, bf16[768,512]{1,0:T(8,128)(2,1)S(1)}, bf16[768,512]{1,0:T(8,128)(2,1)S(1)}, bf16[768,512]{1,0:T(8,128)(2,1)...) custom-call(bf16[768,512]{1,0:T(8,128)(2,1)S(1)} %copy-done.14, ...), custom_call_target="tpu_custom_call" | custom-call | flops 2818572288 | bytes 3145728 | tf_op jit(solution)/shard_map/edge_forward/pallas_call | solution.py:546
  50.9 1.0 collective-permute-start.13
  52.0 1.5 %collective-permute-start.14 = (bf16[96,512]{1,0:T(8,128)(2,1)S(1)}, bf16[96,512]{1,0:T(8,128)(2,1)S(1)}, u32[]{:S(2)}, u32[]{:S(2)}) collective-permute-start(bf16[96,512]{1,0:T(8,128)(2,1)S(1)} %get-tuple-element.60), channel_id=1, source_target_pairs={{0,2},{1,3},{2,0},{3,1},{4,6},{5,7},{6,4},{7,5},{8,10},{9,11},{10,... | collective-permute-start | bytes 294920 | tf_op jit(solution)/shard_map/ppermute | solution.py:31
  54.4 1.8 %collective-permute-done.13.refs_1_ = bf16[96,512]{1,0:T(8,128)(2,1)S(1)} collective-permute-done((bf16[96,512]{1,0:T(8,128)(2,1)S(1)}, bf16[96,512]{1,0:T(8,128)(2,1)S(1)}, u32[]{:S(2)}, u32[]{:S(2)}) %collective-permute-start.13) | collective-permute-done | bytes 98336 | tf_op jit(solution)/shard_map/ppermute | solution.py:31
  56.2 1.7 %collective-permute-done.14.refs_2_ = bf16[96,512]{1,0:T(8,128)(2,1)S(1)} collective-permute-done((bf16[96,512]{1,0:T(8,128)(2,1)S(1)}, bf16[96,512]{1,0:T(8,128)(2,1)S(1)}, u32[]{:S(2)}, u32[]{:S(2)}) %collective-permute-start.14) | collective-permute-done | bytes 98336 | tf_op jit(solution)/shard_map/ppermute | solution.py:31
  57.9 1.1 collective-permute-done.15.refs_3_
  59.1 2.1 %shard_map.191 = (bf16[96,512]{1,0:T(8,128)(2,1)}, bf16[96,512]{1,0:T(8,128)(2,1)S(1)}, f32[96,512]{1,0:T(8,128)S(1)}, bf16[96,1280]{1,0:T(8,128)(2,1)S(1)}, bf1...) custom-call(bf16[96,512]{1,0:T(8,128)(2,1)S(1)} %copy-done.2, ...), custom_call_target="tpu_custom_call" | custom-call | flops 301989888 | bytes 3555328 | tf_op jit(solution)/shard_map/pallas_call | solution.py:91
  61.2 1.1 collective-permute-start.22
  62.3 1.3 collective-permute-start.23
  63.5 1.2 collective-permute-start.24
  64.7 2.0 %collective-permute-done.22.refs_13_ = bf16[96,512]{1,0:T(8,128)(2,1)S(1)} collective-permute-done((bf16[96,512]{1,0:T(8,128)(2,1)S(1)}, bf16[96,512]{1,0:T(8,128)(2,1)S(1)}, u32[]{:S(2)}, u32[]{:S(2)}) %collective-permute-start.22) | collective-permute-done | bytes 98336 | tf_op jit(solution)/shard_map/ppermute | solution.py:31
  67.3 1.8 %collective-permute-done.24.refs_15_ = bf16[96,512]{1,0:T(8,128)(2,1)S(1)} collective-permute-done((bf16[96,512]{1,0:T(8,128)(2,1)S(1)}, bf16[96,512]{1,0:T(8,128)(2,1)S(1)}, u32[]{:S(2)}, u32[]{:S(2)}) %collective-permute-start.24) | collective-permute-done | bytes 98336 | tf_op jit(solution)/shard_map/ppermute | solution.py:31
  69.1 7.4 %edge_backward.1 = (f32[768,512]{1,0:T(8,128)}, bf16[1088,512]{1,0:T(8,128)(2,1)S(1)}, bf16[1088,512]{1,0:T(8,128)(2,1)S(1)}, f32[384,512]{1,0:T(8,128)S(1)}) custom-call(bf16[768,512]{1,0:T(8,128)(2,1)S(1)} %copy-done.14, bf16[768,512]{1,0:T(8,128)(2,1)S(1)} %copy-done.15, bf16[768,512]{1,0:T(8,128)(2,1)S(1)} %get-tuple-element.65.refs_2_, ...), custom_call_target="tpu_custom_call" | custom-call | flops 4026531840 | bytes 6291456 | tf_op jit(solution)/shard_map/edge_backward/pallas_call | solution.py:576
  76.5 1.0 collective-permute-start.35
  78.4 1.6 %collective-permute-start.37 = (bf16[96,1280]{1,0:T(8,128)(2,1)S(1)}, bf16[96,1280]{1,0:T(8,128)(2,1)S(1)}, u32[]{:S(2)}, u32[]{:S(2)}) collective-permute-start(bf16[96,1280]{1,0:T(8,128)(2,1)S(1)} %get-tuple-element.91), channel_id=1, source_target_pairs={{0,3},{1,2},{2,1},{3,0},{4,7},{5,6},{6,5},{7,4},{8,11},{9,10},{10,... | collective-permute-start | bytes 737288 | tf_op jit(solution)/shard_map/ppermute | solution.py:31
  80.2 1.1 collective-permute-start.32
  82.2 3.1 %collective-permute-done.35.refs_5_ = bf16[96,1280]{1,0:T(8,128)(2,1)S(1)} collective-permute-done((bf16[96,1280]{1,0:T(8,128)(2,1)S(1)}, bf16[96,1280]{1,0:T(8,128)(2,1)S(1)}, u32[]{:S(2)}, u32[]{:S(2)}) %collective-permute-start.35) | collective-permute-done | bytes 245792 | tf_op jit(solution)/shard_map/ppermute | solution.py:31
  85.3 1.4 %collective-permute-start.34 = (bf16[256,512]{1,0:T(8,128)(2,1)S(1)}, bf16[256,512]{1,0:T(8,128)(2,1)S(1)}, u32[]{:S(2)}, u32[]{:S(2)}) collective-permute-start(bf16[256,512]{1,0:T(8,128)(2,1)S(1)} %get-tuple-element.87), channel_id=1, source_target_pairs={{0,3},{1,2},{2,1},{3,0},{4,7},{5,6},{6,5},{7,4},{8,11},{9,10},{10,... | collective-permute-start | bytes 786440 | tf_op jit(solution)/shard_map/ppermute | solution.py:31
  86.6 5.0 %collective-permute-done.36.refs_6_ = bf16[96,1280]{1,0:T(8,128)(2,1)S(1)} collective-permute-done((bf16[96,1280]{1,0:T(8,128)(2,1)S(1)}, bf16[96,1280]{1,0:T(8,128)(2,1)S(1)}, u32[]{:S(2)}, u32[]{:S(2)}) %collective-permute-start.36) | collective-permute-done | bytes 245792 | tf_op jit(solution)/shard_map/ppermute | solution.py:31
  92.6 1.3 %collective-permute-done.38.refs_5_ = bf16[192,512]{1,0:T(8,128)(2,1)S(1)} collective-permute-done((bf16[192,512]{1,0:T(8,128)(2,1)S(1)}, bf16[192,512]{1,0:T(8,128)(2,1)S(1)}, u32[]{:S(2)}, u32[]{:S(2)}) %collective-permute-start.38) | collective-permute-done | bytes 196640 | tf_op jit(solution)/shard_map/ppermute | solution.py:31
  94.0 2.9 %collective-permute-start.27 = (bf16[32,512]{1,0:T(8,128)(2,1)S(1)}, bf16[32,512]{1,0:T(8,128)(2,1)S(1)}, u32[]{:S(2)}, u32[]{:S(2)}) collective-permute-start(bf16[32,512]{1,0:T(8,128)(2,1)S(1)} %get-tuple-element.77), channel_id=1, source_target_pairs={{0,16},{4,20},{8,24},{12,28},{16,0},{20,4},{24,8},{28,12},{1,17},{... | collective-permute-start | bytes 98312 | tf_op jit(solution)/shard_map/ppermute | solution.py:31
  96.8 2.6 %collective-permute-start.28 = (bf16[32,512]{1,0:T(8,128)(2,1)S(1)}, bf16[32,512]{1,0:T(8,128)(2,1)S(1)}, u32[]{:S(2)}, u32[]{:S(2)}) collective-permute-start(bf16[32,512]{1,0:T(8,128)(2,1)S(1)} %get-tuple-element.78), channel_id=1, source_target_pairs={{0,24},{4,28},{8,16},{12,20},{16,8},{20,12},{24,0},{28,4},{1,25},{... | collective-permute-start | bytes 98312 | tf_op jit(solution)/shard_map/ppermute | solution.py:31
  99.4 2.7 %collective-permute-done.33.refs_2_ = bf16[256,512]{1,0:T(8,128)(2,1)S(1)} collective-permute-done((bf16[256,512]{1,0:T(8,128)(2,1)S(1)}, bf16[256,512]{1,0:T(8,128)(2,1)S(1)}, u32[]{:S(2)}, u32[]{:S(2)}) %collective-permute-start.33) | collective-permute-done | bytes 262176 | tf_op jit(solution)/shard_map/ppermute | solution.py:31
  102.5 4.2 %collective-permute-start.40 = (bf16[112,512]{1,0:T(8,128)(2,1)S(1)}, bf16[112,512]{1,0:T(8,128)(2,1)S(1)}, u32[]{:S(2)}, u32[]{:S(2)}) collective-permute-start(bf16[112,512]{1,0:T(8,128)(2,1)S(1)} %get-tuple-element.96), channel_id=1, source_target_pairs={{0,16},{4,20},{8,24},{12,28},{16,0},{20,4},{24,8},{28,12},{1,17},{... | collective-permute-start | bytes 344072 | tf_op jit(solution)/shard_map/ppermute | solution.py:31
  107.5 1.0 collective-permute-start.29
  108.6 6.4 %collective-permute-done.40.refs_2_ = bf16[112,512]{1,0:T(8,128)(2,1)S(1)} collective-permute-done((bf16[112,512]{1,0:T(8,128)(2,1)S(1)}, bf16[112,512]{1,0:T(8,128)(2,1)S(1)}, u32[]{:S(2)}, u32[]{:S(2)}) %collective-permute-start.40) | collective-permute-done | bytes 114720 | tf_op jit(solution)/shard_map/ppermute | solution.py:31
  115.1 1.9 %collective-permute-start.42 = (bf16[112,512]{1,0:T(8,128)(2,1)S(1)}, bf16[112,512]{1,0:T(8,128)(2,1)S(1)}, u32[]{:S(2)}, u32[]{:S(2)}) collective-permute-start(bf16[112,512]{1,0:T(8,128)(2,1)S(1)} %shard_map.196.refs_0_), channel_id=1, source_target_pairs={{0,8},{4,12},{8,0},{12,4},{16,24},{20,28},{24,16},{28,20},{1,9},{5... | collective-permute-start | bytes 344072 | tf_op jit(solution)/shard_map/ppermute | solution.py:31
  116.9 1.2 collective-permute-start.43
  118.1 1.4 %collective-permute-start.44 = (bf16[112,512]{1,0:T(8,128)(2,1)S(1)}, bf16[112,512]{1,0:T(8,128)(2,1)S(1)}, u32[]{:S(2)}, u32[]{:S(2)}) collective-permute-start(bf16[112,512]{1,0:T(8,128)(2,1)S(1)} %shard_map.196.refs_0_), channel_id=1, source_target_pairs={{0,24},{4,28},{8,16},{12,20},{16,8},{20,12},{24,0},{28,4},{1,25},{... | collective-permute-start | bytes 344072 | tf_op jit(solution)/shard_map/ppermute | solution.py:31
  120.4 1.6 %collective-permute-start.31 = (bf16[96,512]{1,0:T(8,128)(2,1)S(1)}, bf16[96,512]{1,0:T(8,128)(2,1)S(1)}, u32[]{:S(2)}, u32[]{:S(2)}) collective-permute-start(bf16[96,512]{1,0:T(8,128)(2,1)S(1)} %get-tuple-element.82), channel_id=1, source_target_pairs={{0,3},{1,2},{2,1},{3,0},{4,7},{5,6},{6,5},{7,4},{8,11},{9,10},{10,... | collective-permute-start | bytes 294920 | tf_op jit(solution)/shard_map/ppermute | solution.py:31
  121.9 2.2 %collective-permute-done.30 = bf16[96,512]{1,0:T(8,128)(2,1)S(1)} collective-permute-done((bf16[96,512]{1,0:T(8,128)(2,1)S(1)}, bf16[96,512]{1,0:T(8,128)(2,1)S(1)}, u32[]{:S(2)}, u32[]{:S(2)}) %collective-permute-start.30) | collective-permute-done | bytes 98336 | tf_op jit(solution)/shard_map/ppermute | solution.py:31
  124.7 2.9 %collective-permute-done.43.refs_2_ = bf16[112,512]{1,0:T(8,128)(2,1)S(1)} collective-permute-done((bf16[112,512]{1,0:T(8,128)(2,1)S(1)}, bf16[112,512]{1,0:T(8,128)(2,1)S(1)}, u32[]{:S(2)}, u32[]{:S(2)}) %collective-permute-start.43) | collective-permute-done | bytes 114720 | tf_op jit(solution)/shard_map/ppermute | solution.py:31
  129.0 1.4 %shard_map.197 = (f32[384,512]{1,0:T(8,128)}, f32[128,512]{1,0:T(8,128)}, f32[256,512]{1,0:T(8,128)}, f32[128,512]{1,0:T(8,128)}) custom-call(bf16[112,512]{1,0:T(8,128)(2,1)S(1)} %shard_map.196.refs_0_, bf16[112,512]{1,0:T(8,128)(2,1)S(1)} %collective-permute-done.42.refs_1_, bf16[112,512]{1,0:T(8,128)(2,1)S(1)} %collective-permute-done.43.refs_2_, ...), custom_call_target="tpu_custom_call" | custom-call | bytes 2752512 | tf_op jit(solution)/shard_map/pallas_call | solution.py:91
  (112 shorter events, 18.2 us)
Async XLA Ops:
  0.6 15.2 %collective-permute-start = (bf16[96,512]{1,0:T(8,128)(2,1)}, bf16[96,512]{1,0:T(8,128)(2,1)S(1)}, u32[]{:S(2)}, u32[]{:S(2)}) collective-permute-start(bf16[96,512]{1,0:T(8,128)(2,1)} %refs_0_.7), channel_id=1, source_target_pairs={{0,1},{1,0},{2,3},{3,2},{4,5},{5,4},{6,7},{7,6},{8,9},{9,8},{10,11... | collective-permute-start | bytes 294920 | tf_op jit(solution)/shard_map/ppermute | solution.py:31
  3.7 12.3 %collective-permute-start.1 = (bf16[96,512]{1,0:T(8,128)(2,1)}, bf16[96,512]{1,0:T(8,128)(2,1)S(1)}, u32[]{:S(2)}, u32[]{:S(2)}) collective-permute-start(bf16[96,512]{1,0:T(8,128)(2,1)} %refs_0_.7), channel_id=1, source_target_pairs={{0,2},{1,3},{2,0},{3,1},{4,6},{5,7},{6,4},{7,5},{8,10},{9,11},{10,... | collective-permute-start | bytes 294920 | tf_op jit(solution)/shard_map/ppermute | solution.py:31
  5.2 12.7 %collective-permute-start.2 = (bf16[96,512]{1,0:T(8,128)(2,1)}, bf16[96,512]{1,0:T(8,128)(2,1)S(1)}, u32[]{:S(2)}, u32[]{:S(2)}) collective-permute-start(bf16[96,512]{1,0:T(8,128)(2,1)} %refs_0_.7), channel_id=1, source_target_pairs={{0,3},{1,2},{2,1},{3,0},{4,7},{5,6},{6,5},{7,4},{8,11},{9,10},{10,... | collective-permute-start | bytes 294920 | tf_op jit(solution)/shard_map/ppermute | solution.py:31
  8.8 17.4 %collective-permute-start.9 = (bf16[272,512]{1,0:T(8,128)(2,1)S(1)}, bf16[272,512]{1,0:T(8,128)(2,1)S(1)}, u32[]{:S(2)}, u32[]{:S(2)}) collective-permute-start(bf16[272,512]{1,0:T(8,128)(2,1)S(1)} %shard_map.189), channel_id=1, source_target_pairs={{0,2},{1,3},{2,0},{3,1},{4,6},{5,7},{6,4},{7,5},{8,10},{9,11},{10,... | collective-permute-start | bytes 835592 | tf_op jit(solution)/shard_map/ppermute | solution.py:31
  10.8 15.4 %collective-permute-start.11 = (bf16[272,512]{1,0:T(8,128)(2,1)S(1)}, bf16[272,512]{1,0:T(8,128)(2,1)S(1)}, u32[]{:S(2)}, u32[]{:S(2)}) collective-permute-start(bf16[272,512]{1,0:T(8,128)(2,1)S(1)} %shard_map.189), channel_id=1, source_target_pairs={{0,3},{1,2},{2,1},{3,0},{4,7},{5,6},{6,5},{7,4},{8,11},{9,10},{10,... | collective-permute-start | bytes 835592 | tf_op jit(solution)/shard_map/ppermute | solution.py:31
  15.8 10.9 %collective-permute-start.7 = (bf16[272,512]{1,0:T(8,128)(2,1)S(1)}, bf16[272,512]{1,0:T(8,128)(2,1)S(1)}, u32[]{:S(2)}, u32[]{:S(2)}) collective-permute-start(bf16[272,512]{1,0:T(8,128)(2,1)S(1)} %shard_map.189), channel_id=1, source_target_pairs={{0,1},{1,0},{2,3},{3,2},{4,5},{5,4},{6,7},{7,6},{8,9},{9,8},{10,11... | collective-permute-start | bytes 835592 | tf_op jit(solution)/shard_map/ppermute | solution.py:31
  16.0 19.7 %collective-permute-start.16 = (bf16[192,512]{1,0:T(8,128)(2,1)S(1)}, bf16[192,512]{1,0:T(8,128)(2,1)S(1)}, u32[]{:S(2)}, u32[]{:S(2)}) collective-permute-start(bf16[192,512]{1,0:T(8,128)(2,1)S(1)} %shard_map.190), channel_id=1, source_target_pairs={{0,1},{1,0},{2,3},{3,2},{4,5},{5,4},{6,7},{7,6},{8,9},{9,8},{10,11... | collective-permute-start | bytes 589832 | tf_op jit(solution)/shard_map/ppermute | solution.py:31
  19.6 4.0 %collective-permute-start.4 = (bf16[32,512]{1,0:T(8,128)(2,1)S(1)}, bf16[32,512]{1,0:T(8,128)(2,1)S(1)}, u32[]{:S(2)}, u32[]{:S(2)}) collective-permute-start(bf16[32,512]{1,0:T(8,128)(2,1)S(1)} %pad_maximum_fusion.1), channel_id=1, source_target_pairs={{0,8},{4,12},{8,0},{12,4},{16,24},{20,28},{24,16},{28,20},{1,9},{5... | collective-permute-start | bytes 98312 | tf_op jit(solution)/shard_map/ppermute | solution.py:31
  23.6 4.8 %collective-permute-start.5 = (bf16[32,512]{1,0:T(8,128)(2,1)S(1)}, bf16[32,512]{1,0:T(8,128)(2,1)S(1)}, u32[]{:S(2)}, u32[]{:S(2)}) collective-permute-start(bf16[32,512]{1,0:T(8,128)(2,1)S(1)} %pad_maximum_fusion.2), channel_id=1, source_target_pairs={{0,16},{4,20},{8,24},{12,28},{16,0},{20,4},{24,8},{28,12},{1,17},{... | collective-permute-start | bytes 98312 | tf_op jit(solution)/shard_map/ppermute | solution.py:31
  26.2 17.2 %collective-permute-start.10 = (bf16[272,512]{1,0:T(8,128)(2,1)S(1)}, bf16[272,512]{1,0:T(8,128)(2,1)}, u32[]{:S(2)}, u32[]{:S(2)}) collective-permute-start(bf16[272,512]{1,0:T(8,128)(2,1)S(1)} %collective-permute-done.9.refs_18_), channel_id=1, source_target_pairs={{0,4},{4,0},{8,12},{12,8},{16,20},{20,16},{24,28},{28,24},{1,5},{5... | collective-permute-start | bytes 835592 | tf_op jit(solution)/shard_map/ppermute | solution.py:31
  26.2 17.2 %collective-permute-start.12 = (bf16[272,512]{1,0:T(8,128)(2,1)S(1)}, bf16[272,512]{1,0:T(8,128)(2,1)}, u32[]{:S(2)}, u32[]{:S(2)}) collective-permute-start(bf16[272,512]{1,0:T(8,128)(2,1)S(1)} %collective-permute-done.11.refs_20_), channel_id=1, source_target_pairs={{0,4},{4,0},{8,12},{12,8},{16,20},{20,16},{24,28},{28,24},{1,5},{5... | collective-permute-start | bytes 835592 | tf_op jit(solution)/shard_map/ppermute | solution.py:31
  26.7 16.7 %collective-permute-start.8 = (bf16[272,512]{1,0:T(8,128)(2,1)S(1)}, bf16[272,512]{1,0:T(8,128)(2,1)}, u32[]{:S(2)}, u32[]{:S(2)}) collective-permute-start(bf16[272,512]{1,0:T(8,128)(2,1)S(1)} %collective-permute-done.7.refs_16_), channel_id=1, source_target_pairs={{0,4},{4,0},{8,12},{12,8},{16,20},{20,16},{24,28},{28,24},{1,5},{5... | collective-permute-start | bytes 835592 | tf_op jit(solution)/shard_map/ppermute | solution.py:31
  28.4 5.7 %collective-permute-start.6 = (bf16[32,512]{1,0:T(8,128)(2,1)S(1)}, bf16[32,512]{1,0:T(8,128)(2,1)S(1)}, u32[]{:S(2)}, u32[]{:S(2)}) collective-permute-start(bf16[32,512]{1,0:T(8,128)(2,1)S(1)} %pad_maximum_fusion.3), channel_id=1, source_target_pairs={{0,24},{4,28},{8,16},{12,20},{16,8},{20,12},{24,0},{28,4},{1,25},{... | collective-permute-start | bytes 98312 | tf_op jit(solution)/shard_map/ppermute | solution.py:31
  34.1 8.7 %collective-permute-start.18 = (bf16[192,512]{1,0:T(8,128)(2,1)S(1)}, bf16[192,512]{1,0:T(8,128)(2,1)S(1)}, u32[]{:S(2)}, u32[]{:S(2)}) collective-permute-start(bf16[192,512]{1,0:T(8,128)(2,1)S(1)} %shard_map.190), channel_id=1, source_target_pairs={{0,2},{1,3},{2,0},{3,1},{4,6},{5,7},{6,4},{7,5},{8,10},{9,11},{10,... | collective-permute-start | bytes 589832 | tf_op jit(solution)/shard_map/ppermute | solution.py:31
  35.7 7.2 %collective-permute-start.20 = (bf16[192,512]{1,0:T(8,128)(2,1)S(1)}, bf16[192,512]{1,0:T(8,128)(2,1)S(1)}, u32[]{:S(2)}, u32[]{:S(2)}) collective-permute-start(bf16[192,512]{1,0:T(8,128)(2,1)S(1)} %shard_map.190), channel_id=1, source_target_pairs={{0,3},{1,2},{2,1},{3,0},{4,7},{5,6},{6,5},{7,4},{8,11},{9,10},{10,... | collective-permute-start | bytes 589832 | tf_op jit(solution)/shard_map/ppermute | solution.py:31
  42.8 10.6 %collective-permute-start.17 = (bf16[192,512]{1,0:T(8,128)(2,1)S(1)}, bf16[192,512]{1,0:T(8,128)(2,1)S(1)}, u32[]{:S(2)}, u32[]{:S(2)}) collective-permute-start(bf16[192,512]{1,0:T(8,128)(2,1)S(1)} %collective-permute-done.16.refs_4_), channel_id=1, source_target_pairs={{0,4},{4,0},{8,12},{12,8},{16,20},{20,16},{24,28},{28,24},{1,5},{5... | collective-permute-start | bytes 589832 | tf_op jit(solution)/shard_map/ppermute | solution.py:31
  42.8 11.6 %collective-permute-start.19 = (bf16[192,512]{1,0:T(8,128)(2,1)S(1)}, bf16[192,512]{1,0:T(8,128)(2,1)S(1)}, u32[]{:S(2)}, u32[]{:S(2)}) collective-permute-start(bf16[192,512]{1,0:T(8,128)(2,1)S(1)} %collective-permute-done.18.refs_6_), channel_id=1, source_target_pairs={{0,4},{4,0},{8,12},{12,8},{16,20},{20,16},{24,28},{28,24},{1,5},{5... | collective-permute-start | bytes 589832 | tf_op jit(solution)/shard_map/ppermute | solution.py:31
  43.4 11.1 %collective-permute-start.21 = (bf16[192,512]{1,0:T(8,128)(2,1)S(1)}, bf16[192,512]{1,0:T(8,128)(2,1)S(1)}, u32[]{:S(2)}, u32[]{:S(2)}) collective-permute-start(bf16[192,512]{1,0:T(8,128)(2,1)S(1)} %collective-permute-done.20.refs_8_), channel_id=1, source_target_pairs={{0,4},{4,0},{8,12},{12,8},{16,20},{20,16},{24,28},{28,24},{1,5},{5... | collective-permute-start | bytes 589832 | tf_op jit(solution)/shard_map/ppermute | solution.py:31
  50.9 5.3 %collective-permute-start.13 = (bf16[96,512]{1,0:T(8,128)(2,1)S(1)}, bf16[96,512]{1,0:T(8,128)(2,1)S(1)}, u32[]{:S(2)}, u32[]{:S(2)}) collective-permute-start(bf16[96,512]{1,0:T(8,128)(2,1)S(1)} %get-tuple-element.59), channel_id=1, source_target_pairs={{0,1},{1,0},{2,3},{3,2},{4,5},{5,4},{6,7},{7,6},{8,9},{9,8},{10,11... | collective-permute-start | bytes 294920 | tf_op jit(solution)/shard_map/ppermute | solution.py:31
  52.0 6.0 %collective-permute-start.14 = (bf16[96,512]{1,0:T(8,128)(2,1)S(1)}, bf16[96,512]{1,0:T(8,128)(2,1)S(1)}, u32[]{:S(2)}, u32[]{:S(2)}) collective-permute-start(bf16[96,512]{1,0:T(8,128)(2,1)S(1)} %get-tuple-element.60), channel_id=1, source_target_pairs={{0,2},{1,3},{2,0},{3,1},{4,6},{5,7},{6,4},{7,5},{8,10},{9,11},{10,... | collective-permute-start | bytes 294920 | tf_op jit(solution)/shard_map/ppermute | solution.py:31
  53.4 5.6 %collective-permute-start.15 = (bf16[96,512]{1,0:T(8,128)(2,1)S(1)}, bf16[96,512]{1,0:T(8,128)(2,1)S(1)}, u32[]{:S(2)}, u32[]{:S(2)}) collective-permute-start(bf16[96,512]{1,0:T(8,128)(2,1)S(1)} %get-tuple-element.61), channel_id=1, source_target_pairs={{0,3},{1,2},{2,1},{3,0},{4,7},{5,6},{6,5},{7,4},{8,11},{9,10},{10,... | collective-permute-start | bytes 294920 | tf_op jit(solution)/shard_map/ppermute | solution.py:31
  61.2 5.5 %collective-permute-start.22 = (bf16[96,512]{1,0:T(8,128)(2,1)S(1)}, bf16[96,512]{1,0:T(8,128)(2,1)S(1)}, u32[]{:S(2)}, u32[]{:S(2)}) collective-permute-start(bf16[96,512]{1,0:T(8,128)(2,1)S(1)} %get-tuple-element.71.refs_12_), channel_id=1, source_target_pairs={{0,1},{1,0},{2,3},{3,2},{4,5},{5,4},{6,7},{7,6},{8,9},{9,8},{10,11... | collective-permute-start | bytes 294920 | tf_op jit(solution)/shard_map/ppermute | solution.py:31
  62.3 5.0 %collective-permute-start.23 = (bf16[96,512]{1,0:T(8,128)(2,1)S(1)}, bf16[96,512]{1,0:T(8,128)(2,1)S(1)}, u32[]{:S(2)}, u32[]{:S(2)}) collective-permute-start(bf16[96,512]{1,0:T(8,128)(2,1)S(1)} %get-tuple-element.71.refs_12_), channel_id=1, source_target_pairs={{0,2},{1,3},{2,0},{3,1},{4,6},{5,7},{6,4},{7,5},{8,10},{9,11},{10,... | collective-permute-start | bytes 294920 | tf_op jit(solution)/shard_map/ppermute | solution.py:31
  63.5 5.5 %collective-permute-start.24 = (bf16[96,512]{1,0:T(8,128)(2,1)S(1)}, bf16[96,512]{1,0:T(8,128)(2,1)S(1)}, u32[]{:S(2)}, u32[]{:S(2)}) collective-permute-start(bf16[96,512]{1,0:T(8,128)(2,1)S(1)} %get-tuple-element.71.refs_12_), channel_id=1, source_target_pairs={{0,3},{1,2},{2,1},{3,0},{4,7},{5,6},{6,5},{7,4},{8,11},{9,10},{10,... | collective-permute-start | bytes 294920 | tf_op jit(solution)/shard_map/ppermute | solution.py:31
  76.4 3.5 %collective-permute-start.25 = (bf16[1088,512]{1,0:T(8,128)(2,1)S(1)}, bf16[1088,512]{1,0:T(8,128)(2,1)S(1)}, u32[]{:S(2)}, u32[]{:S(2)}) collective-permute-start(bf16[1088,512]{1,0:T(8,128)(2,1)S(1)} %get-tuple-element.74), channel_id=1, source_target_pairs={{0,4},{4,0},{8,12},{12,8},{16,20},{20,16},{24,28},{28,24},{1,5},{5... | collective-permute-start | bytes 3342344 | tf_op jit(solution)/shard_map/ppermute | solution.py:31
  76.5 8.8 %collective-permute-start.35 = (bf16[96,1280]{1,0:T(8,128)(2,1)S(1)}, bf16[96,1280]{1,0:T(8,128)(2,1)S(1)}, u32[]{:S(2)}, u32[]{:S(2)}) collective-permute-start(bf16[96,1280]{1,0:T(8,128)(2,1)S(1)} %get-tuple-element.89), channel_id=1, source_target_pairs={{0,1},{1,0},{2,3},{3,2},{4,5},{5,4},{6,7},{7,6},{8,9},{9,8},{10,11... | collective-permute-start | bytes 737288 | tf_op jit(solution)/shard_map/ppermute | solution.py:31
  77.5 14.1 %collective-permute-start.36 = (bf16[96,1280]{1,0:T(8,128)(2,1)S(1)}, bf16[96,1280]{1,0:T(8,128)(2,1)S(1)}, u32[]{:S(2)}, u32[]{:S(2)}) collective-permute-start(bf16[96,1280]{1,0:T(8,128)(2,1)S(1)} %get-tuple-element.90), channel_id=1, source_target_pairs={{0,2},{1,3},{2,0},{3,1},{4,6},{5,7},{6,4},{7,5},{8,10},{9,11},{10,... | collective-permute-start | bytes 737288 | tf_op jit(solution)/shard_map/ppermute | solution.py:31
  78.4 13.2 %collective-permute-start.37 = (bf16[96,1280]{1,0:T(8,128)(2,1)S(1)}, bf16[96,1280]{1,0:T(8,128)(2,1)S(1)}, u32[]{:S(2)}, u32[]{:S(2)}) collective-permute-start(bf16[96,1280]{1,0:T(8,128)(2,1)S(1)} %get-tuple-element.91), channel_id=1, source_target_pairs={{0,3},{1,2},{2,1},{3,0},{4,7},{5,6},{6,5},{7,4},{8,11},{9,10},{10,... | collective-permute-start | bytes 737288 | tf_op jit(solution)/shard_map/ppermute | solution.py:31
  80.2 16.6 %collective-permute-start.32 = (bf16[256,512]{1,0:T(8,128)(2,1)S(1)}, bf16[256,512]{1,0:T(8,128)(2,1)S(1)}, u32[]{:S(2)}, u32[]{:S(2)}) collective-permute-start(bf16[256,512]{1,0:T(8,128)(2,1)S(1)} %get-tuple-element.85), channel_id=1, source_target_pairs={{0,1},{1,0},{2,3},{3,2},{4,5},{5,4},{6,7},{7,6},{8,9},{9,8},{10,11... | collective-permute-start | bytes 786440 | tf_op jit(solution)/shard_map/ppermute | solution.py:31
  81.3 20.8 %collective-permute-start.33 = (bf16[256,512]{1,0:T(8,128)(2,1)S(1)}, bf16[256,512]{1,0:T(8,128)(2,1)S(1)}, u32[]{:S(2)}, u32[]{:S(2)}) collective-permute-start(bf16[256,512]{1,0:T(8,128)(2,1)S(1)} %get-tuple-element.86), channel_id=1, source_target_pairs={{0,2},{1,3},{2,0},{3,1},{4,6},{5,7},{6,4},{7,5},{8,10},{9,11},{10,... | collective-permute-start | bytes 786440 | tf_op jit(solution)/shard_map/ppermute | solution.py:31
  85.3 16.8 %collective-permute-start.34 = (bf16[256,512]{1,0:T(8,128)(2,1)S(1)}, bf16[256,512]{1,0:T(8,128)(2,1)S(1)}, u32[]{:S(2)}, u32[]{:S(2)}) collective-permute-start(bf16[256,512]{1,0:T(8,128)(2,1)S(1)} %get-tuple-element.87), channel_id=1, source_target_pairs={{0,3},{1,2},{2,1},{3,0},{4,7},{5,6},{6,5},{7,4},{8,11},{9,10},{10,... | collective-permute-start | bytes 786440 | tf_op jit(solution)/shard_map/ppermute | solution.py:31
  92.5 1.5 %collective-permute-start.38 = (bf16[192,512]{1,0:T(8,128)(2,1)S(1)}, bf16[192,512]{1,0:T(8,128)(2,1)S(1)}, u32[]{:S(2)}, u32[]{:S(2)}) collective-permute-start(bf16[192,512]{1,0:T(8,128)(2,1)S(1)} %get-tuple-element.93), channel_id=1, source_target_pairs={{0,4},{4,0},{8,12},{12,8},{16,20},{20,16},{24,28},{28,24},{1,5},{5... | collective-permute-start | bytes 589832 | tf_op jit(solution)/shard_map/ppermute | solution.py:31
  92.6 14.1 %collective-permute-start.26 = (bf16[32,512]{1,0:T(8,128)(2,1)S(1)}, bf16[32,512]{1,0:T(8,128)(2,1)S(1)}, u32[]{:S(2)}, u32[]{:S(2)}) collective-permute-start(bf16[32,512]{1,0:T(8,128)(2,1)S(1)} %get-tuple-element.76), channel_id=1, source_target_pairs={{0,8},{4,12},{8,0},{12,4},{16,24},{20,28},{24,16},{28,20},{1,9},{5... | collective-permute-start | bytes 98312 | tf_op jit(solution)/shard_map/ppermute | solution.py:31
  94.0 12.9 %collective-permute-start.27 = (bf16[32,512]{1,0:T(8,128)(2,1)S(1)}, bf16[32,512]{1,0:T(8,128)(2,1)S(1)}, u32[]{:S(2)}, u32[]{:S(2)}) collective-permute-start(bf16[32,512]{1,0:T(8,128)(2,1)S(1)} %get-tuple-element.77), channel_id=1, source_target_pairs={{0,16},{4,20},{8,24},{12,28},{16,0},{20,4},{24,8},{28,12},{1,17},{... | collective-permute-start | bytes 98312 | tf_op jit(solution)/shard_map/ppermute | solution.py:31
  96.8 10.1 %collective-permute-start.28 = (bf16[32,512]{1,0:T(8,128)(2,1)S(1)}, bf16[32,512]{1,0:T(8,128)(2,1)S(1)}, u32[]{:S(2)}, u32[]{:S(2)}) collective-permute-start(bf16[32,512]{1,0:T(8,128)(2,1)S(1)} %get-tuple-element.78), channel_id=1, source_target_pairs={{0,24},{4,28},{8,16},{12,20},{16,8},{20,12},{24,0},{28,4},{1,25},{... | collective-permute-start | bytes 98312 | tf_op jit(solution)/shard_map/ppermute | solution.py:31
  102.4 6.2 %collective-permute-start.39 = (bf16[112,512]{1,0:T(8,128)(2,1)S(1)}, bf16[112,512]{1,0:T(8,128)(2,1)S(1)}, u32[]{:S(2)}, u32[]{:S(2)}) collective-permute-start(bf16[112,512]{1,0:T(8,128)(2,1)S(1)} %get-tuple-element.95), channel_id=1, source_target_pairs={{0,8},{4,12},{8,0},{12,4},{16,24},{20,28},{24,16},{28,20},{1,9},{5... | collective-permute-start | bytes 344072 | tf_op jit(solution)/shard_map/ppermute | solution.py:31
  102.5 12.5 %collective-permute-start.40 = (bf16[112,512]{1,0:T(8,128)(2,1)S(1)}, bf16[112,512]{1,0:T(8,128)(2,1)S(1)}, u32[]{:S(2)}, u32[]{:S(2)}) collective-permute-start(bf16[112,512]{1,0:T(8,128)(2,1)S(1)} %get-tuple-element.96), channel_id=1, source_target_pairs={{0,16},{4,20},{8,24},{12,28},{16,0},{20,4},{24,8},{28,12},{1,17},{... | collective-permute-start | bytes 344072 | tf_op jit(solution)/shard_map/ppermute | solution.py:31
  106.7 8.3 %collective-permute-start.41 = (bf16[112,512]{1,0:T(8,128)(2,1)S(1)}, bf16[112,512]{1,0:T(8,128)(2,1)S(1)}, u32[]{:S(2)}, u32[]{:S(2)}) collective-permute-start(bf16[112,512]{1,0:T(8,128)(2,1)S(1)} %get-tuple-element.97), channel_id=1, source_target_pairs={{0,24},{4,28},{8,16},{12,20},{16,8},{20,12},{24,0},{28,4},{1,25},{... | collective-permute-start | bytes 344072 | tf_op jit(solution)/shard_map/ppermute | solution.py:31
  107.5 12.9 %collective-permute-start.29 = (bf16[96,512]{1,0:T(8,128)(2,1)S(1)}, bf16[96,512]{1,0:T(8,128)(2,1)S(1)}, u32[]{:S(2)}, u32[]{:S(2)}) collective-permute-start(bf16[96,512]{1,0:T(8,128)(2,1)S(1)} %get-tuple-element.80), channel_id=1, source_target_pairs={{0,1},{1,0},{2,3},{3,2},{4,5},{5,4},{6,7},{7,6},{8,9},{9,8},{10,11... | collective-permute-start | bytes 294920 | tf_op jit(solution)/shard_map/ppermute | solution.py:31
  115.1 9.1 %collective-permute-start.42 = (bf16[112,512]{1,0:T(8,128)(2,1)S(1)}, bf16[112,512]{1,0:T(8,128)(2,1)S(1)}, u32[]{:S(2)}, u32[]{:S(2)}) collective-permute-start(bf16[112,512]{1,0:T(8,128)(2,1)S(1)} %shard_map.196.refs_0_), channel_id=1, source_target_pairs={{0,8},{4,12},{8,0},{12,4},{16,24},{20,28},{24,16},{28,20},{1,9},{5... | collective-permute-start | bytes 344072 | tf_op jit(solution)/shard_map/ppermute | solution.py:31
  116.9 10.6 %collective-permute-start.43 = (bf16[112,512]{1,0:T(8,128)(2,1)S(1)}, bf16[112,512]{1,0:T(8,128)(2,1)S(1)}, u32[]{:S(2)}, u32[]{:S(2)}) collective-permute-start(bf16[112,512]{1,0:T(8,128)(2,1)S(1)} %shard_map.196.refs_0_), channel_id=1, source_target_pairs={{0,16},{4,20},{8,24},{12,28},{16,0},{20,4},{24,8},{28,12},{1,17},{... | collective-permute-start | bytes 344072 | tf_op jit(solution)/shard_map/ppermute | solution.py:31
  118.1 9.4 %collective-permute-start.44 = (bf16[112,512]{1,0:T(8,128)(2,1)S(1)}, bf16[112,512]{1,0:T(8,128)(2,1)S(1)}, u32[]{:S(2)}, u32[]{:S(2)}) collective-permute-start(bf16[112,512]{1,0:T(8,128)(2,1)S(1)} %shard_map.196.refs_0_), channel_id=1, source_target_pairs={{0,24},{4,28},{8,16},{12,20},{16,8},{20,12},{24,0},{28,4},{1,25},{... | collective-permute-start | bytes 344072 | tf_op jit(solution)/shard_map/ppermute | solution.py:31
  119.5 4.6 %collective-permute-start.30 = (bf16[96,512]{1,0:T(8,128)(2,1)S(1)}, bf16[96,512]{1,0:T(8,128)(2,1)S(1)}, u32[]{:S(2)}, u32[]{:S(2)}) collective-permute-start(bf16[96,512]{1,0:T(8,128)(2,1)S(1)} %get-tuple-element.81), channel_id=1, source_target_pairs={{0,2},{1,3},{2,0},{3,1},{4,6},{5,7},{6,4},{7,5},{8,10},{9,11},{10,... | collective-permute-start | bytes 294920 | tf_op jit(solution)/shard_map/ppermute | solution.py:31
  120.4 7.7 %collective-permute-start.31 = (bf16[96,512]{1,0:T(8,128)(2,1)S(1)}, bf16[96,512]{1,0:T(8,128)(2,1)S(1)}, u32[]{:S(2)}, u32[]{:S(2)}) collective-permute-start(bf16[96,512]{1,0:T(8,128)(2,1)S(1)} %get-tuple-element.82), channel_id=1, source_target_pairs={{0,3},{1,2},{2,1},{3,0},{4,7},{5,6},{6,5},{7,4},{8,11},{9,10},{10,... | collective-permute-start | bytes 294920 | tf_op jit(solution)/shard_map/ppermute | solution.py:31
  124.1 4.7 %collective-permute-start.45 = (bf16[112,512]{1,0:T(8,128)(2,1)S(1)}, bf16[112,512]{1,0:T(8,128)(2,1)S(1)}, u32[]{:S(2)}, u32[]{:S(2)}) collective-permute-start(bf16[112,512]{1,0:T(8,128)(2,1)S(1)} %shard_map.196.refs_0_), channel_id=1, source_target_pairs={{0,4},{4,0},{8,12},{12,8},{16,20},{20,16},{24,28},{28,24},{1,5},{5... | collective-permute-start | bytes 344072 | tf_op jit(solution)/shard_map/ppermute | solution.py:31
  124.1 4.6 %collective-permute-start.46 = (bf16[112,512]{1,0:T(8,128)(2,1)S(1)}, bf16[112,512]{1,0:T(8,128)(2,1)S(1)}, u32[]{:S(2)}, u32[]{:S(2)}) collective-permute-start(bf16[112,512]{1,0:T(8,128)(2,1)S(1)} %collective-permute-done.42.refs_1_), channel_id=1, source_target_pairs={{0,4},{4,0},{8,12},{12,8},{16,20},{20,16},{24,28},{28,24},{1,5},{5... | collective-permute-start | bytes 344072 | tf_op jit(solution)/shard_map/ppermute | solution.py:31
  127.5 1.3 %collective-permute-start.47 = (bf16[112,512]{1,0:T(8,128)(2,1)S(1)}, bf16[112,512]{1,0:T(8,128)(2,1)S(1)}, u32[]{:S(2)}, u32[]{:S(2)}) collective-permute-start(bf16[112,512]{1,0:T(8,128)(2,1)S(1)} %collective-permute-done.43.refs_2_), channel_id=1, source_target_pairs={{0,4},{4,0},{8,12},{12,8},{16,20},{20,16},{24,28},{28,24},{1,5},{5... | collective-permute-start | bytes 344072 | tf_op jit(solution)/shard_map/ppermute | solution.py:31
  127.5 1.5 %collective-permute-start.48 = (bf16[112,512]{1,0:T(8,128)(2,1)S(1)}, bf16[112,512]{1,0:T(8,128)(2,1)S(1)}, u32[]{:S(2)}, u32[]{:S(2)}) collective-permute-start(bf16[112,512]{1,0:T(8,128)(2,1)S(1)} %collective-permute-done.44.refs_3_), channel_id=1, source_target_pairs={{0,4},{4,0},{8,12},{12,8},{16,20},{20,16},{24,28},{28,24},{1,5},{5... | collective-permute-start | bytes 344072 | tf_op jit(solution)/shard_map/ppermute | solution.py:31
  (17 other events, 248.8 us)
where the time goes:
time: 131 us; the launch traced here: 130 us
  starting transfers between devices  54.2 us (41%)
  waiting for transfers between devices  45.5 us (35%)
  Pallas kernels  21.3 us (16%)
  local copies, waits for them, and re-layouts  6.16 us (5%)
  other arithmetic  2.27 us (2%)
    ppermute x49, starting transfers between devices, swap(): return lax.ppermute(x, axis, [(i, i ^ bits) for i in range(n)])  54.2 us
    ppermute x49, waiting for transfers between devices, swap(): return lax.ppermute(x, axis, [(i, i ^ bits) for i in range(n)])  45.5 us
    pallas_call x1, Pallas kernels, layer(): pl.pallas_call(functools.partial(edge_forward_kernel, n, pairs), out_shap...  7.44 us
    pallas_call x1, Pallas kernels, layer(): pl.pallas_call(functools.partial(edge_backward_kernel, n, slots), out_sha...  7.38 us
    pallas_call x8, Pallas kernels, call(): pl.pallas_call(kernel, out_shape=tuple(outs), grid=(1,), in_specs=[whole_...  5.89 us
    unnamed x32, local copies, waits for them, and re-layouts  5.11 us
  transfers between devices with their start and end apart: 49, of which 20 were waited for; matrix products, arithmetic and copies ran while one was open for 3% of the time, Pallas kernels for 8%

commit v1 on v0

--- a/solution.py
+++ b/solution.py
@@ -58,7 +58,7 @@
 
 
 def swish_and_slope(values):
-    s = 1.0 / (1.0 + jnp.exp(-values))
+    s = 0.5 * jnp.tanh(0.5 * values) + 0.5
     return (values * s).astype(BF16), s * (1.0 + values * (1.0 - s))
 
 
@@ -138,19 +138,23 @@
 
 
 def pack_kernel(inner, outer, *refs):
-    gains, pack, sems = refs[:-2], refs[-2], refs[-1]
+    m = inner.shape[0] + 1
     half = outer.shape[0] // 2
-    m = inner.shape[0] + 1
+    count = (len(refs) - 2) // 2
+    gains, pack, sems, held = refs[:count], refs[count], refs[count + 1], refs[count + 2 :]
     at = pl.multiple_of(lax.axis_index("region") % 2 * half, half)
-    copies = []
+    copies = [pltpu.make_async_copy(gain, ref, sems.at[m + k]) for k, (gain, ref) in enumerate(zip(gains, held))]
     for k in range(m):
         source = inner.at[k, pl.ds(at, half)] if k < m - 1 else outer.at[pl.ds(at, half)]
         copies.append(pltpu.make_async_copy(source, pack.at[pl.ds(k * half, half)], sems.at[k]))
-        copies[-1].start()
+    for copy in copies:
+        copy.start()
+    for copy in copies:
+        copy.wait()
     if gains:
         parts = []
-        for gain in gains:
-            left = gain[...]
+        for ref in held:
+            left = ref[...]
             for _ in range(3):
                 part = left.astype(BF16)
                 left = left - part.astype(F32)
@@ -158,23 +162,22 @@
         parts.append(jnp.zeros((16 - len(parts), left.shape[1]), F32))
         pack[m * half :, :] = jnp.zeros((16, pack.shape[1]), BF16)
         pack[m * half :, : left.shape[1]] = jnp.concatenate(parts, axis=0).astype(BF16)
-    for copy in copies:
-        copy.wait()
 
 
 def pack_halves(inner, outer, gains):
     m, d = inner.shape[0] + 1, inner.shape[2]
     rows = m * (outer.shape[0] // 2) + (16 if gains else 0)
+    ins = [pltpu.with_memory_space_constraint(x, pltpu.HBM) for x in (inner, outer, *gains)]
     return pl.pallas_call(
         pack_kernel,
         out_shape=shape((rows, d)),
         grid=(1,),
-        in_specs=[pl.BlockSpec(memory_space=pltpu.HBM)] * 2 + [whole_block(x.shape) for x in gains],
+        in_specs=[pl.BlockSpec(memory_space=pltpu.HBM)] * len(ins),
         out_specs=whole_block((rows, d)),
-        scratch_shapes=[pltpu.SemaphoreType.DMA((m,))],
+        scratch_shapes=[pltpu.SemaphoreType.DMA((m + len(gains),))] + [pltpu.VMEM(x.shape, F32) for x in gains],
         compiler_params=pltpu.CompilerParams(vmem_limit_bytes=VMEM_LIMIT),
         cost_estimate=pl.CostEstimate(flops=rows * d, bytes_accessed=4 * rows * d, transcendentals=0),
-    )(inner, outer, *gains)
+    )(*ins)
 
 
 def fill_gains(gain_ref, blocks, own, pieces, here):
@@ -189,17 +192,34 @@
         gain_ref[0:2, f * portion : (f + 1) * portion] = blocks[f, 0:2, :]
 
 
-def outgoing_kernel(n, at_ref, *refs):
-    near, (keep, send) = refs[:n], refs[n : n + 2]
+def outgoing_kernel(n, rows_ref, *refs):
+    near, (keep, send, at_ref) = refs[:n], refs[n:]
     own = near[0].shape[0]
-    rows = jnp.zeros((at_ref.shape[0], near[0].shape[1]), F32)
+    here = lax.axis_index("feat")
+    region = lax.axis_index("region")
+    regions, slots = rows_ref.shape
+    for b in range(regions):
+        row = rows_ref[pl.ds(region ^ b, 1), :]
+        feat = jnp.zeros_like(row)
+        for k in range(1, n):
+            feat = feat + jnp.where(row >= k * own, 1, 0)
+        at_ref[0:1, b * slots : (b + 1) * slots] = (feat ^ here) * own + row - feat * own
+    at = at_ref[0:1, :]
+    rows = jnp.zeros((at.shape[1], near[0].shape[1]), F32)
     for b in range(n):
-        rows = rows + dot(hot(at_ref[...] - b * own, own), near[b][...])
+        rows = rows + t_dot(hot_t(at - b * own, own), near[b][...])
     rows = rows.astype(BF16)
     pairs, slots, _ = keep.shape
     for b in range(pairs):
         keep[b] = rows[(2 * b) * slots : (2 * b + 1) * slots]
         send[b] = rows[(2 * b + 1) * slots : (2 * b + 2) * slots]
+
+
+def join_kernel(keep, other, *outs):
+    slots = keep.shape[1]
+    for b, out in enumerate(outs):
+        out[:slots, :] = keep[b]
+        out[slots:, :] = other[b]
 
 
 def edge_forward_kernel(n, pairs, *refs):
@@ -311,8 +331,8 @@
 def edge_backward_kernel(n, slots, *refs):
     edge, cot, hidden, slope, normed, inverse, r_at, s_row, r_row, gains, table, w = refs[:12]
     near, refs = refs[12 : 12 + n], refs[12 + n :]
-    edge_grad, keep, send, near_grad = refs[:4]
-    near_all, grads, sent, received = refs[4:]
+    pre_grad_ref, keep, send, sent_ref, received_ref, near_all = refs[:6]
+    grads, sent, received = refs[6:]
     here = lax.axis_index("feat")
     parity = lax.axis_index("region") % 2
     own = near[0].shape[0]
@@ -329,7 +349,7 @@
     total = cot[...].astype(F32) + dot(hot(r_at[...], nodes), near_all[...])
     mix_grad = layer_norm_back(total * gains[0:1, :], normed[...].astype(F32), inverse[:, :1])
     pre_grad = (dot_t(mix_grad, w[3]) * slope[...].astype(F32)).astype(BF16)
-    edge_grad[...] = total + dot_t(pre_grad, w[0])
+    pre_grad_ref[...] = pre_grad
     grads[0] += t_dot(edge[...], pre_grad)
     grads[3] += t_dot(hidden[...], mix_grad)
     sent[...] += dot(hot_t(s_row[...], table.shape[0]), pre_grad)
@@ -342,9 +362,9 @@
         grads[1] = t_dot(table[...], from_senders)
         grads[2] = t_dot(table[:nodes, :], from_receivers)
         split_grads(grads, n, keep, send, parity, here)
-        to_table = dot_t(from_senders, w[1])
-        near_grad[...] = to_table[:nodes] + dot_t(from_receivers, w[2])
-        back = to_table[nodes:].astype(BF16)
+        sent_ref[...] = from_senders
+        received_ref[...] = from_receivers
+        back = dot_t(from_senders[nodes:], w[1]).astype(BF16)
         at = n * grads.shape[0] * (grads.shape[1] // n // 2)
         count = (keep.shape[0] - at) // slots
         for b in range(count):
@@ -353,14 +373,19 @@
             send[rows, :] = back[(2 * b + 1) * slots : (2 * b + 2) * slots]
 
 
-def return_kernel(n, pairs, near_grad, at_row, *refs):
+def edge_grad_kernel(cot, r_at, near, pre_grad, w, out):
+    total = cot[...].astype(F32) + dot(hot(r_at[...], near.shape[0]), near[...])
+    out[...] = total + dot_t(pre_grad[...], w[0])
+
+
+def return_kernel(n, pairs, sent, received, w, at_ref, *refs):
     blocks, outs = refs[:pairs], refs[pairs:]
-    nodes, _ = near_grad.shape
+    nodes = received.shape[0]
     own = nodes // n
     rows = blocks[0].shape[0]
-    total = near_grad[...]
+    total = dot_t(sent[:nodes, :], w[1]) + dot_t(received[...], w[2])
     for b in range(pairs):
-        total = total + dot(hot_t(at_row[:, b * rows : (b + 1) * rows], nodes), blocks[b][...])
+        total = total + dot(hot_t(at_ref[0:1, b * rows : (b + 1) * rows], nodes), blocks[b][...])
     for b in range(n):
         outs[b][...] = total[b * own : (b + 1) * own, :].astype(BF16)
 
@@ -377,32 +402,34 @@
 
 
 def scatter_sum_kernel(n, pairs, *refs):
-    parts, node_parts = refs[:n], refs[n : n + 2]
-    outs, total = refs[n + 2 : n + 2 + pairs], refs[n + 2 + pairs]
+    parts, outs, total = refs[:n], refs[n : n + pairs], refs[n + pairs]
     z = lax.axis_index("region") // 2
-    cut = parts[0].shape[0]
-    total[:cut, :] = add_all([part[...] for part in parts])
-    total[cut:, :] = add_all([part[...] for part in node_parts])
+    total[...] = add_all([part[...] for part in parts])
     rows = outs[0].shape[0]
     for b in range(pairs):
         outs[b][...] = total[pl.ds(pl.multiple_of((z ^ b) * rows, rows), rows), :].astype(BF16)
 
 
-def sum_kernel(*refs):
-    refs[-1][...] = add_all([part[...] for part in refs[:-1]]).astype(BF16)
-
-
-def finish_kernel(pairs, edge_norm, node_norm, *refs):
+def sum_kernel(pairs, *refs):
+    edge, node, out = refs[:pairs], refs[pairs : 2 * pairs], refs[2 * pairs]
+    cut = edge[0].shape[0]
+    out[:cut, :] = add_all([part[...] for part in edge]).astype(BF16)
+    out[cut:, :] = add_all([part[...] for part in node]).astype(BF16)
+
+
+def finish_kernel(pairs, cut, edge_norm, node_norm, *refs):
     mine, theirs = refs[:pairs], refs[pairs : 2 * pairs]
     outs, total = refs[2 * pairs : -1], refs[-1]
     region = lax.axis_index("region")
     parity, z = region % 2, region // 2
     rows = mine[0].shape[0]
     for b in range(pairs):
-        at = (z ^ b) * rows
         for side, ref in ((parity, mine[b]), (1 - parity, theirs[b])):
-            start = pl.multiple_of(side * pairs * rows + at, rows)
-            total[pl.ds(start, rows), :] = ref[...].astype(F32)
+            base = side * pairs * rows
+            start = pl.multiple_of(base + (z ^ b) * cut, 16)
+            total[pl.ds(start, cut), :] = ref[:cut, :].astype(F32)
+            start = pl.multiple_of(base + pairs * cut + (z ^ b) * (rows - cut), 16)
+            total[pl.ds(start, rows - cut), :] = ref[cut:, :].astype(F32)
     spread(total, outs, edge_norm, node_norm)
 
 
@@ -431,41 +458,54 @@
 
 
 def reduce_grads(parts, node_parts, portion, edge_norm, node_norm):
-    n = len(parts)
     half, d = parts[0].shape
     pairs = lax.axis_size("region") // 2
     z = lax.axis_index("region") // 2
     parity = lax.axis_index("region") % 2
-    size = half + node_parts[0].shape[0]
-    rows = size // pairs
+    node_half = node_parts[0].shape[0]
+    size = half + node_half
+    rows, cut = size // pairs, half // pairs
+    aligned = cut % 16 == 0 and rows % 16 == 0
     outs = [shape((k * portion, d), F32) for k in (3, 1, 2, 1)]
-    if rows % 16 == 0:
-        parts = call(
-            functools.partial(scatter_sum_kernel, n, pairs),
-            [*parts, *node_parts],
-            [shape((rows, d))] * pairs,
-            [pltpu.VMEM((size, d), F32)],
+
+    def scattered(parts, total):
+        rows = total // pairs
+        if aligned:
+            parts = call(
+                functools.partial(scatter_sum_kernel, len(parts), pairs),
+                parts,
+                [shape((rows, d))] * pairs,
+                [pltpu.VMEM((total, d), F32)],
+            )
+        else:
+            mine = add_all(parts).astype(BF16).reshape(pairs, rows, d)
+            parts = [lax.dynamic_index_in_dim(mine, z ^ b, 0, keepdims=False) for b in range(pairs)]
+        return chip_exchange(parts)
+
+    node_parts = scattered(node_parts, node_half)
+    parts = scattered(parts, half)
+    if aligned:
+        (chunk,) = call(
+            functools.partial(sum_kernel, pairs), [*parts, *node_parts], [shape((rows, d))]
         )
     else:
-        mine = jnp.concatenate([add_all(parts), add_all(node_parts)]).astype(BF16).reshape(pairs, rows, d)
-        parts = [lax.dynamic_index_in_dim(mine, z ^ b, 0, keepdims=False) for b in range(pairs)]
-    parts = chip_exchange(parts)
-    if rows % 16 == 0:
-        (chunk,) = call(sum_kernel, parts, [shape((rows, d))])
-    else:
-        chunk = add_all(parts).astype(BF16)
+        chunk = jnp.concatenate([add_all(parts), add_all(node_parts)]).astype(BF16)
     mine = chip_exchange([chunk] * pairs)
     theirs = [swap(piece, "region", 1) for piece in mine]
-    if rows % 16 == 0:
+    if aligned:
         return call(
-            functools.partial(finish_kernel, pairs, edge_norm, node_norm),
+            functools.partial(finish_kernel, pairs, cut, edge_norm, node_norm),
             mine + theirs,
             outs,
             [pltpu.VMEM((2 * size, d), F32)],
         )
     order = jnp.arange(pairs) ^ z
-    sides = [jnp.stack(side)[order].reshape(size, d) for side in (mine, theirs)]
-    total = jnp.where(parity == 0, jnp.concatenate(sides), jnp.concatenate(sides[::-1])).astype(F32)
+    sides = []
+    for side in (mine, theirs):
+        side = jnp.stack(side)[order]
+        sides += [side[:, :cut].reshape(half, d), side[:, cut:].reshape(node_half, d)]
+    swapped = sides[2:] + sides[:2]
+    total = jnp.where(parity == 0, jnp.concatenate(sides), jnp.concatenate(swapped)).astype(F32)
 
     def from_total(*refs):
         spread(refs[0], refs[1:], edge_norm, node_norm)
@@ -511,7 +551,6 @@
         nodes + ((remote // slots) ^ region) * slots + remote % slots,
     )
     receiver_at = relative(local_receivers)
-    send_at = relative(send_rows[0])[jnp.arange(regions) ^ region].reshape(-1)
 
     portion = d // n
     half = portion // 2
@@ -522,14 +561,14 @@
     w_edge = gather_halves(edge_pack)
 
     square = 2 * d * d
-    keep, send = call(
+    keep, send, send_at = call(
         functools.partial(outgoing_kernel, n),
-        [send_at[:, None], *near],
-        [shape((pairs, slots, d))] * 2,
+        [send_rows[0], *near],
+        [shape((pairs, slots, d))] * 2 + [shape((8, regions * slots), jnp.int32)],
         flops=2 * regions * slots * nodes * d,
     )
     other = swap(send, "region", 1)
-    remote_rows = chip_exchange([jnp.concatenate([keep[b], other[b]], axis=0) for b in range(pairs)])
+    remote_rows = chip_exchange(call(join_kernel, [keep, other], [shape((2 * slots, d))] * pairs))
     w_node = gather_halves(node_pack)
 
     tile = tile_of(share)
@@ -572,16 +611,16 @@
 
     ins = [edge_lat, edge_cot, hidden, slope, normed, inverse, receiver_at[:, None], sender_at[None], receiver_at[None]]
     rest = [gains, table, w_full, *grad_near]
-    kept = [shape((n * 2 * portion + pairs * slots, d))] * 2 + [shape((nodes, d), F32)]
-    edge_grad, keep, send, near_grad = pl.pallas_call(
+    kept = [shape((n * 2 * portion + pairs * slots, d))] * 2
+    kept += [shape((table_size, d)), shape((nodes, d)), shape((nodes, d))]
+    edge_pre_grad, keep, send, sent, received, near_grad = pl.pallas_call(
         functools.partial(edge_backward_kernel, n, slots),
-        out_shape=tuple([shape((share, d), F32)] + kept),
+        out_shape=tuple([shape((share, d))] + kept),
         grid=(steps,),
         in_specs=[by_rows(d)] * 5 + [by_rows(128), by_rows(1), by_columns, by_columns]
         + [whole_block(x.shape) for x in rest],
         out_specs=tuple([by_rows(d)] + [whole_block(x.shape) for x in kept]),
         scratch_shapes=[
-            pltpu.VMEM((nodes, d), BF16),
             pltpu.VMEM((4, d, d), F32),
             pltpu.VMEM((table_size, d), F32),
             pltpu.VMEM((nodes, d), F32),
@@ -616,11 +655,21 @@
         float((nodes * regions) ** -0.5),
     )
 
+    edge_grad = pl.pallas_call(
+        edge_grad_kernel,
+        out_shape=shape((share, d), F32),
+        grid=(steps,),
+        in_specs=[by_rows(d), by_rows(1), whole_block((nodes, d)), by_rows(d), whole_block((1, d, d))],
+        out_specs=by_rows(d),
+        compiler_params=edge_params,
+        cost_estimate=pl.CostEstimate(flops=2 * share * square, bytes_accessed=8 * share * d, transcendentals=0),
+        name="edge_grad",
+    )(edge_cot, receiver_at[:, None], near_grad, edge_pre_grad, w_full)
     parts = call(
         functools.partial(return_kernel, n, pairs),
-        [near_grad, send_at[None], *returned],
+        [sent, received, w_full, send_at, *returned],
         [shape((own, d))] * n,
-        flops=2 * regions * slots * nodes * d,
+        flops=4 * nodes * square,
     )
     node_grad = node_base + add_all(feat_swaps(parts))
 

time: 131 us -> 137 us (1.046)
  starting transfers between devices: 54.2 us -> 60.7 us
  local copies, waits for them, and re-layouts: 6.16 us -> 0.39 us
  waiting for transfers between devices: 45.5 us -> 48.7 us
  Pallas kernels: 21.3 us -> 24.3 us
    ppermute x49 -> x52, starting transfers between devices: 54.2 us -> 60.7 us  [swap(): return lax.ppermute(x, axis, [(i, i ^ bits) for i in range(n)])]
    unnamed x32 -> x22, local copies, waits for them, and re-layouts: 5.11 us -> 0.06 us
    ppermute x49 -> x52, waiting for transfers between devices: 45.5 us -> 48.7 us  [swap(): return lax.ppermute(x, axis, [(i, i ^ bits) for i in range(n)])]
    pallas_call x0 -> x1, Pallas kernels: none -> 2.54 us  [layer(): pl.pallas_call(edge_grad_kernel, out_shape=shape((share, d), F32), grid=(...]
    pallas_call x1, Pallas kernels: 7.38 us -> 6.01 us  [layer(): pl.pallas_call(functools.partial(edge_backward_kernel, n, slots), out_sha...]
    pallas_call x8 -> x10, Pallas kernels: 5.89 us -> 6.41 us  [call(): pl.pallas_call(kernel, out_shape=tuple(outs), grid=(1,), in_specs=[whole_...]
  transfers between devices with their start and end apart: 49 -> 52, of which waited for: 20 -> 20; matrix products, arithmetic and copies ran while one was open for 3% -> 1% of each run, Pallas kernels for 8% -> 11%
where the time goes in v1:
time: 137 us
  starting transfers between devices  60.7 us (44%)
  waiting for transfers between devices  48.7 us (36%)
  Pallas kernels  24.3 us (18%)
  other arithmetic  1.54 us (1%)
    ppermute x52, starting transfers between devices, swap(): return lax.ppermute(x, axis, [(i, i ^ bits) for i in range(n)])  60.7 us
    ppermute x52, waiting for transfers between devices, swap(): return lax.ppermute(x, axis, [(i, i ^ bits) for i in range(n)])  48.7 us
    pallas_call x1, Pallas kernels, layer(): pl.pallas_call(functools.partial(edge_forward_kernel, n, pairs), out_shap...  7.38 us
    pallas_call x10, Pallas kernels, call(): pl.pallas_call(kernel, out_shape=tuple(outs), grid=(1,), in_specs=[whole_...  6.41 us
    pallas_call x1, Pallas kernels, layer(): pl.pallas_call(functools.partial(edge_backward_kernel, n, slots), out_sha...  6.01 us
  transfers between devices with their start and end apart: 52, of which 20 were waited for; matrix products, arithmetic and copies ran while one was open for 1% of the time, Pallas kernels for 11%

profile of v1, /device:TPU:0, one launch (start us, length us, event | category | flops | bytes accessed | tf_op | source)
XLA Modules:
  0.0 136.6 jit_solution(5196952986919511425)
XLA Ops:
  0.7 4.0 %collective-permute-start.2 = (bf16[96,512]{1,0:T(8,128)(2,1)}, bf16[96,512]{1,0:T(8,128)(2,1)S(1)}, u32[]{:S(2)}, u32[]{:S(2)}) collective-permute-start(bf16[96,512]{1,0:T(8,128)(2,1)} %refs_0_.7), channel_id=1, source_target_pairs={{0,3},{1,2},{2,1},{3,0},{4,7},{5,6},{6,5},{7,4},{8,11},{9,10},{10,... | collective-permute-start | bytes 294920 | tf_op jit(solution)/shard_map/ppermute | solution.py:31
  4.6 1.0 shard_map.190
  5.8 2.0 %collective-permute-start.9 = (bf16[272,512]{1,0:T(8,128)(2,1)S(1)}, bf16[272,512]{1,0:T(8,128)(2,1)S(1)}, u32[]{:S(2)}, u32[]{:S(2)}) collective-permute-start(bf16[272,512]{1,0:T(8,128)(2,1)S(1)} %shard_map.190), channel_id=1, source_target_pairs={{0,2},{1,3},{2,0},{3,1},{4,6},{5,7},{6,4},{7,5},{8,10},{9,11},{10,... | collective-permute-start | bytes 835592 | tf_op jit(solution)/shard_map/ppermute | solution.py:31
  7.8 1.5 %collective-permute-start.7 = (bf16[272,512]{1,0:T(8,128)(2,1)S(1)}, bf16[272,512]{1,0:T(8,128)(2,1)S(1)}, u32[]{:S(2)}, u32[]{:S(2)}) collective-permute-start(bf16[272,512]{1,0:T(8,128)(2,1)S(1)} %shard_map.190), channel_id=1, source_target_pairs={{0,1},{1,0},{2,3},{3,2},{4,5},{5,4},{6,7},{7,6},{8,9},{9,8},{10,11... | collective-permute-start | bytes 835592 | tf_op jit(solution)/shard_map/ppermute | solution.py:31
  9.9 0.9 shard_map.191
  10.9 11.2 %collective-permute-done.1.refs_2_.refs_10_ = bf16[96,512]{1,0:T(8,128)(2,1)S(1)} collective-permute-done((bf16[96,512]{1,0:T(8,128)(2,1)}, bf16[96,512]{1,0:T(8,128)(2,1)S(1)}, u32[]{:S(2)}, u32[]{:S(2)}) %collective-permute-start.1) | collective-permute-done | bytes 98336 | tf_op jit(solution)/shard_map/ppermute | solution.py:31
  22.1 2.3 %collective-permute-start.20 = (bf16[192,512]{1,0:T(8,128)(2,1)S(1)}, bf16[192,512]{1,0:T(8,128)(2,1)S(1)}, u32[]{:S(2)}, u32[]{:S(2)}) collective-permute-start(bf16[192,512]{1,0:T(8,128)(2,1)S(1)} %shard_map.191), channel_id=1, source_target_pairs={{0,3},{1,2},{2,1},{3,0},{4,7},{5,6},{6,5},{7,4},{8,11},{9,10},{10,... | collective-permute-start | bytes 589832 | tf_op jit(solution)/shard_map/ppermute | solution.py:31
  24.9 1.2 collective-permute-done.3.other
  26.1 1.7 %collective-permute-start.4 = (bf16[32,512]{1,0:T(8,128)(2,1)S(1)}, bf16[32,512]{1,0:T(8,128)(2,1)S(1)}, u32[]{:S(2)}, u32[]{:S(2)}) collective-permute-start(bf16[32,512]{1,0:T(8,128)(2,1)S(1)} %get-tuple-element.69), channel_id=1, source_target_pairs={{0,8},{4,12},{8,0},{12,4},{16,24},{20,28},{24,16},{28,20},{1,9},{5... | collective-permute-start | bytes 98312 | tf_op jit(solution)/shard_map/ppermute | solution.py:31
  28.4 1.7 %collective-permute-done.4.refs_13_ = bf16[32,512]{1,0:T(8,128)(2,1)S(1)} collective-permute-done((bf16[32,512]{1,0:T(8,128)(2,1)S(1)}, bf16[32,512]{1,0:T(8,128)(2,1)S(1)}, u32[]{:S(2)}, u32[]{:S(2)}) %collective-permute-start.4) | collective-permute-done | bytes 32800 | tf_op jit(solution)/shard_map/ppermute | solution.py:31
  30.1 2.7 %collective-permute-start.5 = (bf16[32,512]{1,0:T(8,128)(2,1)S(1)}, bf16[32,512]{1,0:T(8,128)(2,1)S(1)}, u32[]{:S(2)}, u32[]{:S(2)}) collective-permute-start(bf16[32,512]{1,0:T(8,128)(2,1)S(1)} %get-tuple-element.70), channel_id=1, source_target_pairs={{0,16},{4,20},{8,24},{12,28},{16,0},{20,4},{24,8},{28,12},{1,17},{... | collective-permute-start | bytes 98312 | tf_op jit(solution)/shard_map/ppermute | solution.py:31
  32.8 2.1 %collective-permute-done.5.refs_14_ = bf16[32,512]{1,0:T(8,128)(2,1)S(1)} collective-permute-done((bf16[32,512]{1,0:T(8,128)(2,1)S(1)}, bf16[32,512]{1,0:T(8,128)(2,1)S(1)}, u32[]{:S(2)}, u32[]{:S(2)}) %collective-permute-start.5) | collective-permute-done | bytes 32800 | tf_op jit(solution)/shard_map/ppermute | solution.py:31
  34.9 3.9 %collective-permute-start.6 = (bf16[32,512]{1,0:T(8,128)(2,1)S(1)}, bf16[32,512]{1,0:T(8,128)(2,1)S(1)}, u32[]{:S(2)}, u32[]{:S(2)}) collective-permute-start(bf16[32,512]{1,0:T(8,128)(2,1)S(1)} %get-tuple-element.71), channel_id=1, source_target_pairs={{0,24},{4,28},{8,16},{12,20},{16,8},{20,12},{24,0},{28,4},{1,25},{... | collective-permute-start | bytes 98312 | tf_op jit(solution)/shard_map/ppermute | solution.py:31
  38.8 1.9 %collective-permute-done.6.refs_15_ = bf16[32,512]{1,0:T(8,128)(2,1)S(1)} collective-permute-done((bf16[32,512]{1,0:T(8,128)(2,1)S(1)}, bf16[32,512]{1,0:T(8,128)(2,1)S(1)}, u32[]{:S(2)}, u32[]{:S(2)}) %collective-permute-start.6) | collective-permute-done | bytes 32800 | tf_op jit(solution)/shard_map/ppermute | solution.py:31
  43.1 3.2 %collective-permute-done.18.refs_6_ = bf16[192,512]{1,0:T(8,128)(2,1)S(1)} collective-permute-done((bf16[192,512]{1,0:T(8,128)(2,1)S(1)}, bf16[192,512]{1,0:T(8,128)(2,1)S(1)}, u32[]{:S(2)}, u32[]{:S(2)}) %collective-permute-start.18) | collective-permute-done | bytes 196640 | tf_op jit(solution)/shard_map/ppermute | solution.py:31
  47.5 7.4 %edge_forward.1 = (bf16[768,512]{1,0:T(8,128)(2,1)}, bf16[768,512]{1,0:T(8,128)(2,1)S(1)}, bf16[768,512]{1,0:T(8,128)(2,1)S(1)}, bf16[768,512]{1,0:T(8,128)(2,1)...) custom-call(bf16[768,512]{1,0:T(8,128)(2,1)S(1)} %copy-done.10, ...), custom_call_target="tpu_custom_call" | custom-call | flops 2818572288 | bytes 3145728 | tf_op jit(solution)/shard_map/edge_forward/pallas_call | solution.py:585
  55.6 1.3 collective-permute-start.14
  56.9 1.4 %collective-permute-start.15 = (bf16[96,512]{1,0:T(8,128)(2,1)S(1)}, bf16[96,512]{1,0:T(8,128)(2,1)S(1)}, u32[]{:S(2)}, u32[]{:S(2)}) collective-permute-start(bf16[96,512]{1,0:T(8,128)(2,1)S(1)} %get-tuple-element.76), channel_id=1, source_target_pairs={{0,3},{1,2},{2,1},{3,0},{4,7},{5,6},{6,5},{7,4},{8,11},{9,10},{10,... | collective-permute-start | bytes 294920 | tf_op jit(solution)/shard_map/ppermute | solution.py:31
  58.4 1.6 %collective-permute-done.13.refs_1_ = bf16[96,512]{1,0:T(8,128)(2,1)S(1)} collective-permute-done((bf16[96,512]{1,0:T(8,128)(2,1)S(1)}, bf16[96,512]{1,0:T(8,128)(2,1)S(1)}, u32[]{:S(2)}, u32[]{:S(2)}) %collective-permute-start.13) | collective-permute-done | bytes 98336 | tf_op jit(solution)/shard_map/ppermute | solution.py:31
  60.0 1.2 collective-permute-done.14.refs_2_
  61.2 1.4 %collective-permute-done.15.refs_3_ = bf16[96,512]{1,0:T(8,128)(2,1)S(1)} collective-permute-done((bf16[96,512]{1,0:T(8,128)(2,1)S(1)}, bf16[96,512]{1,0:T(8,128)(2,1)S(1)}, u32[]{:S(2)}, u32[]{:S(2)}) %collective-permute-start.15) | collective-permute-done | bytes 98336 | tf_op jit(solution)/shard_map/ppermute | solution.py:31
  62.7 2.1 %shard_map.192 = (bf16[96,512]{1,0:T(8,128)(2,1)}, bf16[96,512]{1,0:T(8,128)(2,1)S(1)}, f32[96,512]{1,0:T(8,128)S(1)}, bf16[96,1280]{1,0:T(8,128)(2,1)S(1)}, bf1...) custom-call(bf16[96,512]{1,0:T(8,128)(2,1)S(1)} %copy-done.1, ...), custom_call_target="tpu_custom_call" | custom-call | flops 301989888 | bytes 3555328 | tf_op jit(solution)/shard_map/pallas_call | solution.py:91
  64.8 1.8 %collective-permute-start.24 = (bf16[96,512]{1,0:T(8,128)(2,1)S(1)}, bf16[96,512]{1,0:T(8,128)(2,1)S(1)}, u32[]{:S(2)}, u32[]{:S(2)}) collective-permute-start(bf16[96,512]{1,0:T(8,128)(2,1)S(1)} %get-tuple-element.86.refs_12_), channel_id=1, source_target_pairs={{0,3},{1,2},{2,1},{3,0},{4,7},{5,6},{6,5},{7,4},{8,11},{9,10},{10,... | collective-permute-start | bytes 294920 | tf_op jit(solution)/shard_map/ppermute | solution.py:31
  68.3 2.5 %collective-permute-done.24.refs_15_ = bf16[96,512]{1,0:T(8,128)(2,1)S(1)} collective-permute-done((bf16[96,512]{1,0:T(8,128)(2,1)S(1)}, bf16[96,512]{1,0:T(8,128)(2,1)S(1)}, u32[]{:S(2)}, u32[]{:S(2)}) %collective-permute-start.24) | collective-permute-done | bytes 98336 | tf_op jit(solution)/shard_map/ppermute | solution.py:31
  70.8 1.0 collective-permute-done.23.refs_14_
  72.1 6.0 %edge_backward.1 = (bf16[768,512]{1,0:T(8,128)(2,1)S(1)}, bf16[1088,512]{1,0:T(8,128)(2,1)S(1)}, bf16[1088,512]{1,0:T(8,128)(2,1)S(1)}, bf16[512,512]{1,0:T(8,12...) custom-call(bf16[768,512]{1,0:T(8,128)(2,1)S(1)} %copy-done.10, bf16[768,512]{1,0:T(8,128)(2,1)S(1)} %copy-done.2, ...), custom_call_target="tpu_custom_call" | custom-call | flops 4026531840 | bytes 6291456 | tf_op jit(solution)/shard_map/edge_backward/pallas_call | solution.py:616
  79.1 1.0 collective-permute-start.39
  80.1 1.7 %collective-permute-start.40 = (bf16[96,1280]{1,0:T(8,128)(2,1)S(1)}, bf16[96,1280]{1,0:T(8,128)(2,1)S(1)}, u32[]{:S(2)}, u32[]{:S(2)}) collective-permute-start(bf16[96,1280]{1,0:T(8,128)(2,1)S(1)} %get-tuple-element.113), channel_id=1, source_target_pairs={{0,3},{1,2},{2,1},{3,0},{4,7},{5,6},{6,5},{7,4},{8,11},{9,10},{10,... | collective-permute-start | bytes 737288 | tf_op jit(solution)/shard_map/ppermute | solution.py:31
  81.8 5.3 %collective-permute-done.38.refs_5_ = bf16[96,1280]{1,0:T(8,128)(2,1)S(1)} collective-permute-done((bf16[96,1280]{1,0:T(8,128)(2,1)S(1)}, bf16[96,1280]{1,0:T(8,128)(2,1)S(1)}, u32[]{:S(2)}, u32[]{:S(2)}) %collective-permute-start.38) | collective-permute-done | bytes 245792 | tf_op jit(solution)/shard_map/ppermute | solution.py:31
  87.5 4.9 %collective-permute-done.40.refs_7_ = bf16[96,1280]{1,0:T(8,128)(2,1)S(1)} collective-permute-done((bf16[96,1280]{1,0:T(8,128)(2,1)S(1)}, bf16[96,1280]{1,0:T(8,128)(2,1)S(1)}, u32[]{:S(2)}, u32[]{:S(2)}) %collective-permute-start.40) | collective-permute-done | bytes 245792 | tf_op jit(solution)/shard_map/ppermute | solution.py:31
  93.6 1.2 collective-permute-start.32
  94.9 1.1 collective-permute-start.33
  96.0 1.2 collective-permute-start.34
  97.2 4.4 %collective-permute-start.27 = (bf16[32,512]{1,0:T(8,128)(2,1)S(1)}, bf16[32,512]{1,0:T(8,128)(2,1)S(1)}, u32[]{:S(2)}, u32[]{:S(2)}) collective-permute-start(bf16[32,512]{1,0:T(8,128)(2,1)S(1)} %get-tuple-element.94), channel_id=1, source_target_pairs={{0,16},{4,20},{8,24},{12,28},{16,0},{20,4},{24,8},{28,12},{1,17},{... | collective-permute-start | bytes 98312 | tf_op jit(solution)/shard_map/ppermute | solution.py:31
  101.6 3.3 %collective-permute-start.28 = (bf16[32,512]{1,0:T(8,128)(2,1)S(1)}, bf16[32,512]{1,0:T(8,128)(2,1)S(1)}, u32[]{:S(2)}, u32[]{:S(2)}) collective-permute-start(bf16[32,512]{1,0:T(8,128)(2,1)S(1)} %get-tuple-element.95), channel_id=1, source_target_pairs={{0,24},{4,28},{8,16},{12,20},{16,8},{20,12},{24,0},{28,4},{1,25},{... | collective-permute-start | bytes 98312 | tf_op jit(solution)/shard_map/ppermute | solution.py:31
  105.1 2.5 %collective-permute-done.28.refs_3_ = bf16[32,512]{1,0:T(8,128)(2,1)S(1)} collective-permute-done((bf16[32,512]{1,0:T(8,128)(2,1)S(1)}, bf16[32,512]{1,0:T(8,128)(2,1)S(1)}, u32[]{:S(2)}, u32[]{:S(2)}) %collective-permute-start.28) | collective-permute-done | bytes 32800 | tf_op jit(solution)/shard_map/ppermute | solution.py:31
  107.8 1.0 shard_map.194
  108.8 1.2 collective-permute-start.29
  110.2 3.8 %collective-permute-start.35 = (bf16[64,512]{1,0:T(8,128)(2,1)S(1)}, bf16[64,512]{1,0:T(8,128)(2,1)S(1)}, u32[]{:S(2)}, u32[]{:S(2)}) collective-permute-start(bf16[64,512]{1,0:T(8,128)(2,1)S(1)} %get-tuple-element.107), channel_id=1, source_target_pairs={{0,8},{4,12},{8,0},{12,4},{16,24},{20,28},{24,16},{28,20},{1,9},{5... | collective-permute-start | bytes 196616 | tf_op jit(solution)/shard_map/ppermute | solution.py:31
  114.0 2.4 %collective-permute-start.37 = (bf16[64,512]{1,0:T(8,128)(2,1)S(1)}, bf16[64,512]{1,0:T(8,128)(2,1)S(1)}, u32[]{:S(2)}, u32[]{:S(2)}) collective-permute-start(bf16[64,512]{1,0:T(8,128)(2,1)S(1)} %get-tuple-element.109), channel_id=1, source_target_pairs={{0,24},{4,28},{8,16},{12,20},{16,8},{20,12},{24,0},{28,4},{1,25},{... | collective-permute-start | bytes 196616 | tf_op jit(solution)/shard_map/ppermute | solution.py:31
  116.5 1.4 %collective-permute-start.44 = (bf16[48,512]{1,0:T(8,128)(2,1)S(1)}, bf16[48,512]{1,0:T(8,128)(2,1)S(1)}, u32[]{:S(2)}, u32[]{:S(2)}) collective-permute-start(bf16[48,512]{1,0:T(8,128)(2,1)S(1)} %get-tuple-element.119), channel_id=1, source_target_pairs={{0,24},{4,28},{8,16},{12,20},{16,8},{20,12},{24,0},{28,4},{1,25},{... | collective-permute-start | bytes 147464 | tf_op jit(solution)/shard_map/ppermute | solution.py:31
  117.9 4.6 %collective-permute-done.44.refs_7_ = bf16[48,512]{1,0:T(8,128)(2,1)S(1)} collective-permute-done((bf16[48,512]{1,0:T(8,128)(2,1)S(1)}, bf16[48,512]{1,0:T(8,128)(2,1)S(1)}, u32[]{:S(2)}, u32[]{:S(2)}) %collective-permute-start.44) | collective-permute-done | bytes 49184 | tf_op jit(solution)/shard_map/ppermute | solution.py:31
  122.5 1.5 %collective-permute-start.47 = (bf16[112,512]{1,0:T(8,128)(2,1)S(1)}, bf16[112,512]{1,0:T(8,128)(2,1)S(1)}, u32[]{:S(2)}, u32[]{:S(2)}) collective-permute-start(bf16[112,512]{1,0:T(8,128)(2,1)S(1)} %shard_map.198.refs_0_), channel_id=1, source_target_pairs={{0,24},{4,28},{8,16},{12,20},{16,8},{20,12},{24,0},{28,4},{1,25},{... | collective-permute-start | bytes 344072 | tf_op jit(solution)/shard_map/ppermute | solution.py:31
  124.0 3.8 %collective-permute-start.46 = (bf16[112,512]{1,0:T(8,128)(2,1)S(1)}, bf16[112,512]{1,0:T(8,128)(2,1)S(1)}, u32[]{:S(2)}, u32[]{:S(2)}) collective-permute-start(bf16[112,512]{1,0:T(8,128)(2,1)S(1)} %shard_map.198.refs_0_), channel_id=1, source_target_pairs={{0,16},{4,20},{8,24},{12,28},{16,0},{20,4},{24,8},{28,12},{1,17},{... | collective-permute-start | bytes 344072 | tf_op jit(solution)/shard_map/ppermute | solution.py:31
  127.8 1.1 collective-permute-start.30
  128.9 1.5 %collective-permute-start.31 = (bf16[96,512]{1,0:T(8,128)(2,1)S(1)}, bf16[96,512]{1,0:T(8,128)(2,1)S(1)}, u32[]{:S(2)}, u32[]{:S(2)}) collective-permute-start(bf16[96,512]{1,0:T(8,128)(2,1)S(1)} %get-tuple-element.99), channel_id=1, source_target_pairs={{0,3},{1,2},{2,1},{3,0},{4,7},{5,6},{6,5},{7,4},{8,11},{9,10},{10,... | collective-permute-start | bytes 294920 | tf_op jit(solution)/shard_map/ppermute | solution.py:31
  130.4 2.5 %edge_grad.1 = f32[768,512]{1,0:T(8,128)} custom-call(bf16[768,512]{1,0:T(8,128)(2,1)S(1)} %copy-done.2, s32[768,1]{1,0:T(8,128)S(1)} %broadcast_in_dim.28.refs_2_.refs_6_.r_at, bf16[384,512]{1,0:T(8,128)(2,1)S(1)} %get-tuple-element.100.near, bf16[768,512]{1,0:T(8,128)(2,1)S(1)} %get-tuple-element.101.pre_grad, ...), custom_call_target="tpu_custom_call" | custom-call | flops 805306368 | bytes 3145728 | tf_op jit(solution)/shard_map/edge_grad/pallas_call | solution.py:658
  135.2 1.4 %shard_map.199 = (f32[384,512]{1,0:T(8,128)}, f32[128,512]{1,0:T(8,128)}, f32[256,512]{1,0:T(8,128)}, f32[128,512]{1,0:T(8,128)}) custom-call(bf16[112,512]{1,0:T(8,128)(2,1)S(1)} %shard_map.198.refs_0_, bf16[112,512]{1,0:T(8,128)(2,1)S(1)} %collective-permute-done.45.refs_1_, bf16[112,512]{1,0:T(8,128)(2,1)S(1)} %collective-permute-done.46.refs_2_, ...), custom_call_target="tpu_custom_call" | custom-call | bytes 2752512 | tf_op jit(solution)/shard_map/pallas_call | solution.py:91
  (99 shorter events, 13.3 us)
Async XLA Ops:
  0.7 9.2 %collective-permute-start.2 = (bf16[96,512]{1,0:T(8,128)(2,1)}, bf16[96,512]{1,0:T(8,128)(2,1)S(1)}, u32[]{:S(2)}, u32[]{:S(2)}) collective-permute-start(bf16[96,512]{1,0:T(8,128)(2,1)} %refs_0_.7), channel_id=1, source_target_pairs={{0,3},{1,2},{2,1},{3,0},{4,7},{5,6},{6,5},{7,4},{8,11},{9,10},{10,... | collective-permute-start | bytes 294920 | tf_op jit(solution)/shard_map/ppermute | solution.py:31
  5.7 22.1 %collective-permute-start.11 = (bf16[272,512]{1,0:T(8,128)(2,1)S(1)}, bf16[272,512]{1,0:T(8,128)(2,1)S(1)}, u32[]{:S(2)}, u32[]{:S(2)}) collective-permute-start(bf16[272,512]{1,0:T(8,128)(2,1)S(1)} %shard_map.190), channel_id=1, source_target_pairs={{0,3},{1,2},{2,1},{3,0},{4,7},{5,6},{6,5},{7,4},{8,11},{9,10},{10,... | collective-permute-start | bytes 835592 | tf_op jit(solution)/shard_map/ppermute | solution.py:31
  5.8 22.0 %collective-permute-start.9 = (bf16[272,512]{1,0:T(8,128)(2,1)S(1)}, bf16[272,512]{1,0:T(8,128)(2,1)S(1)}, u32[]{:S(2)}, u32[]{:S(2)}) collective-permute-start(bf16[272,512]{1,0:T(8,128)(2,1)S(1)} %shard_map.190), channel_id=1, source_target_pairs={{0,2},{1,3},{2,0},{3,1},{4,6},{5,7},{6,4},{7,5},{8,10},{9,11},{10,... | collective-permute-start | bytes 835592 | tf_op jit(solution)/shard_map/ppermute | solution.py:31
  7.8 20.5 %collective-permute-start.7 = (bf16[272,512]{1,0:T(8,128)(2,1)S(1)}, bf16[272,512]{1,0:T(8,128)(2,1)S(1)}, u32[]{:S(2)}, u32[]{:S(2)}) collective-permute-start(bf16[272,512]{1,0:T(8,128)(2,1)S(1)} %shard_map.190), channel_id=1, source_target_pairs={{0,1},{1,0},{2,3},{3,2},{4,5},{5,4},{6,7},{7,6},{8,9},{9,8},{10,11... | collective-permute-start | bytes 835592 | tf_op jit(solution)/shard_map/ppermute | solution.py:31
  9.3 12.8 %collective-permute-start.1 = (bf16[96,512]{1,0:T(8,128)(2,1)}, bf16[96,512]{1,0:T(8,128)(2,1)S(1)}, u32[]{:S(2)}, u32[]{:S(2)}) collective-permute-start(bf16[96,512]{1,0:T(8,128)(2,1)} %refs_0_.7), channel_id=1, source_target_pairs={{0,2},{1,3},{2,0},{3,1},{4,6},{5,7},{6,4},{7,5},{8,10},{9,11},{10,... | collective-permute-start | bytes 294920 | tf_op jit(solution)/shard_map/ppermute | solution.py:31
  9.8 14.5 %collective-permute-start = (bf16[96,512]{1,0:T(8,128)(2,1)}, bf16[96,512]{1,0:T(8,128)(2,1)S(1)}, u32[]{:S(2)}, u32[]{:S(2)}) collective-permute-start(bf16[96,512]{1,0:T(8,128)(2,1)} %refs_0_.7), channel_id=1, source_target_pairs={{0,1},{1,0},{2,3},{3,2},{4,5},{5,4},{6,7},{7,6},{8,9},{9,8},{10,11... | collective-permute-start | bytes 294920 | tf_op jit(solution)/shard_map/ppermute | solution.py:31
  22.1 19.1 %collective-permute-start.20 = (bf16[192,512]{1,0:T(8,128)(2,1)S(1)}, bf16[192,512]{1,0:T(8,128)(2,1)S(1)}, u32[]{:S(2)}, u32[]{:S(2)}) collective-permute-start(bf16[192,512]{1,0:T(8,128)(2,1)S(1)} %shard_map.191), channel_id=1, source_target_pairs={{0,3},{1,2},{2,1},{3,0},{4,7},{5,6},{6,5},{7,4},{8,11},{9,10},{10,... | collective-permute-start | bytes 589832 | tf_op jit(solution)/shard_map/ppermute | solution.py:31
  26.1 4.0 %collective-permute-start.4 = (bf16[32,512]{1,0:T(8,128)(2,1)S(1)}, bf16[32,512]{1,0:T(8,128)(2,1)S(1)}, u32[]{:S(2)}, u32[]{:S(2)}) collective-permute-start(bf16[32,512]{1,0:T(8,128)(2,1)S(1)} %get-tuple-element.69), channel_id=1, source_target_pairs={{0,8},{4,12},{8,0},{12,4},{16,24},{20,28},{24,16},{28,20},{1,9},{5... | collective-permute-start | bytes 98312 | tf_op jit(solution)/shard_map/ppermute | solution.py:31
  27.8 19.1 %collective-permute-start.12 = (bf16[272,512]{1,0:T(8,128)(2,1)S(1)}, bf16[272,512]{1,0:T(8,128)(2,1)}, u32[]{:S(2)}, u32[]{:S(2)}) collective-permute-start(bf16[272,512]{1,0:T(8,128)(2,1)S(1)} %collective-permute-done.11.refs_20_), channel_id=1, source_target_pairs={{0,4},{4,0},{8,12},{12,8},{16,20},{20,16},{24,28},{28,24},{1,5},{5... | collective-permute-start | bytes 835592 | tf_op jit(solution)/shard_map/ppermute | solution.py:31
  27.8 19.6 %collective-permute-start.10 = (bf16[272,512]{1,0:T(8,128)(2,1)S(1)}, bf16[272,512]{1,0:T(8,128)(2,1)}, u32[]{:S(2)}, u32[]{:S(2)}) collective-permute-start(bf16[272,512]{1,0:T(8,128)(2,1)S(1)} %collective-permute-done.9.refs_18_), channel_id=1, source_target_pairs={{0,4},{4,0},{8,12},{12,8},{16,20},{20,16},{24,28},{28,24},{1,5},{5... | collective-permute-start | bytes 835592 | tf_op jit(solution)/shard_map/ppermute | solution.py:31
  28.3 19.1 %collective-permute-start.8 = (bf16[272,512]{1,0:T(8,128)(2,1)S(1)}, bf16[272,512]{1,0:T(8,128)(2,1)}, u32[]{:S(2)}, u32[]{:S(2)}) collective-permute-start(bf16[272,512]{1,0:T(8,128)(2,1)S(1)} %collective-permute-done.7.refs_16_), channel_id=1, source_target_pairs={{0,4},{4,0},{8,12},{12,8},{16,20},{20,16},{24,28},{28,24},{1,5},{5... | collective-permute-start | bytes 835592 | tf_op jit(solution)/shard_map/ppermute | solution.py:31
  30.1 4.8 %collective-permute-start.5 = (bf16[32,512]{1,0:T(8,128)(2,1)S(1)}, bf16[32,512]{1,0:T(8,128)(2,1)S(1)}, u32[]{:S(2)}, u32[]{:S(2)}) collective-permute-start(bf16[32,512]{1,0:T(8,128)(2,1)S(1)} %get-tuple-element.70), channel_id=1, source_target_pairs={{0,16},{4,20},{8,24},{12,28},{16,0},{20,4},{24,8},{28,12},{1,17},{... | collective-permute-start | bytes 98312 | tf_op jit(solution)/shard_map/ppermute | solution.py:31
  34.9 5.8 %collective-permute-start.6 = (bf16[32,512]{1,0:T(8,128)(2,1)S(1)}, bf16[32,512]{1,0:T(8,128)(2,1)S(1)}, u32[]{:S(2)}, u32[]{:S(2)}) collective-permute-start(bf16[32,512]{1,0:T(8,128)(2,1)S(1)} %get-tuple-element.71), channel_id=1, source_target_pairs={{0,24},{4,28},{8,16},{12,20},{16,8},{20,12},{24,0},{28,4},{1,25},{... | collective-permute-start | bytes 98312 | tf_op jit(solution)/shard_map/ppermute | solution.py:31
  40.7 5.7 %collective-permute-start.18 = (bf16[192,512]{1,0:T(8,128)(2,1)S(1)}, bf16[192,512]{1,0:T(8,128)(2,1)S(1)}, u32[]{:S(2)}, u32[]{:S(2)}) collective-permute-start(bf16[192,512]{1,0:T(8,128)(2,1)S(1)} %shard_map.191), channel_id=1, source_target_pairs={{0,2},{1,3},{2,0},{3,1},{4,6},{5,7},{6,4},{7,5},{8,10},{9,11},{10,... | collective-permute-start | bytes 589832 | tf_op jit(solution)/shard_map/ppermute | solution.py:31
  41.2 5.7 %collective-permute-start.16 = (bf16[192,512]{1,0:T(8,128)(2,1)S(1)}, bf16[192,512]{1,0:T(8,128)(2,1)S(1)}, u32[]{:S(2)}, u32[]{:S(2)}) collective-permute-start(bf16[192,512]{1,0:T(8,128)(2,1)S(1)} %shard_map.191), channel_id=1, source_target_pairs={{0,1},{1,0},{2,3},{3,2},{4,5},{5,4},{6,7},{7,6},{8,9},{9,8},{10,11... | collective-permute-start | bytes 589832 | tf_op jit(solution)/shard_map/ppermute | solution.py:31
  46.4 10.6 %collective-permute-start.21 = (bf16[192,512]{1,0:T(8,128)(2,1)S(1)}, bf16[192,512]{1,0:T(8,128)(2,1)S(1)}, u32[]{:S(2)}, u32[]{:S(2)}) collective-permute-start(bf16[192,512]{1,0:T(8,128)(2,1)S(1)} %collective-permute-done.20.refs_8_), channel_id=1, source_target_pairs={{0,4},{4,0},{8,12},{12,8},{16,20},{20,16},{24,28},{28,24},{1,5},{5... | collective-permute-start | bytes 589832 | tf_op jit(solution)/shard_map/ppermute | solution.py:31
  46.9 11.5 %collective-permute-start.19 = (bf16[192,512]{1,0:T(8,128)(2,1)S(1)}, bf16[192,512]{1,0:T(8,128)(2,1)S(1)}, u32[]{:S(2)}, u32[]{:S(2)}) collective-permute-start(bf16[192,512]{1,0:T(8,128)(2,1)S(1)} %collective-permute-done.18.refs_6_), channel_id=1, source_target_pairs={{0,4},{4,0},{8,12},{12,8},{16,20},{20,16},{24,28},{28,24},{1,5},{5... | collective-permute-start | bytes 589832 | tf_op jit(solution)/shard_map/ppermute | solution.py:31
  46.9 11.5 %collective-permute-start.17 = (bf16[192,512]{1,0:T(8,128)(2,1)S(1)}, bf16[192,512]{1,0:T(8,128)(2,1)S(1)}, u32[]{:S(2)}, u32[]{:S(2)}) collective-permute-start(bf16[192,512]{1,0:T(8,128)(2,1)S(1)} %collective-permute-done.16.refs_4_), channel_id=1, source_target_pairs={{0,4},{4,0},{8,12},{12,8},{16,20},{20,16},{24,28},{28,24},{1,5},{5... | collective-permute-start | bytes 589832 | tf_op jit(solution)/shard_map/ppermute | solution.py:31
  54.9 5.1 %collective-permute-start.13 = (bf16[96,512]{1,0:T(8,128)(2,1)S(1)}, bf16[96,512]{1,0:T(8,128)(2,1)S(1)}, u32[]{:S(2)}, u32[]{:S(2)}) collective-permute-start(bf16[96,512]{1,0:T(8,128)(2,1)S(1)} %get-tuple-element.74), channel_id=1, source_target_pairs={{0,1},{1,0},{2,3},{3,2},{4,5},{5,4},{6,7},{7,6},{8,9},{9,8},{10,11... | collective-permute-start | bytes 294920 | tf_op jit(solution)/shard_map/ppermute | solution.py:31
  55.6 5.6 %collective-permute-start.14 = (bf16[96,512]{1,0:T(8,128)(2,1)S(1)}, bf16[96,512]{1,0:T(8,128)(2,1)S(1)}, u32[]{:S(2)}, u32[]{:S(2)}) collective-permute-start(bf16[96,512]{1,0:T(8,128)(2,1)S(1)} %get-tuple-element.75), channel_id=1, source_target_pairs={{0,2},{1,3},{2,0},{3,1},{4,6},{5,7},{6,4},{7,5},{8,10},{9,11},{10,... | collective-permute-start | bytes 294920 | tf_op jit(solution)/shard_map/ppermute | solution.py:31
  56.9 5.7 %collective-permute-start.15 = (bf16[96,512]{1,0:T(8,128)(2,1)S(1)}, bf16[96,512]{1,0:T(8,128)(2,1)S(1)}, u32[]{:S(2)}, u32[]{:S(2)}) collective-permute-start(bf16[96,512]{1,0:T(8,128)(2,1)S(1)} %get-tuple-element.76), channel_id=1, source_target_pairs={{0,3},{1,2},{2,1},{3,0},{4,7},{5,6},{6,5},{7,4},{8,11},{9,10},{10,... | collective-permute-start | bytes 294920 | tf_op jit(solution)/shard_map/ppermute | solution.py:31
  64.8 6.0 %collective-permute-start.24 = (bf16[96,512]{1,0:T(8,128)(2,1)S(1)}, bf16[96,512]{1,0:T(8,128)(2,1)S(1)}, u32[]{:S(2)}, u32[]{:S(2)}) collective-permute-start(bf16[96,512]{1,0:T(8,128)(2,1)S(1)} %get-tuple-element.86.refs_12_), channel_id=1, source_target_pairs={{0,3},{1,2},{2,1},{3,0},{4,7},{5,6},{6,5},{7,4},{8,11},{9,10},{10,... | collective-permute-start | bytes 294920 | tf_op jit(solution)/shard_map/ppermute | solution.py:31
  66.6 5.2 %collective-permute-start.23 = (bf16[96,512]{1,0:T(8,128)(2,1)S(1)}, bf16[96,512]{1,0:T(8,128)(2,1)S(1)}, u32[]{:S(2)}, u32[]{:S(2)}) collective-permute-start(bf16[96,512]{1,0:T(8,128)(2,1)S(1)} %get-tuple-element.86.refs_12_), channel_id=1, source_target_pairs={{0,2},{1,3},{2,0},{3,1},{4,6},{5,7},{6,4},{7,5},{8,10},{9,11},{10,... | collective-permute-start | bytes 294920 | tf_op jit(solution)/shard_map/ppermute | solution.py:31
  67.5 4.6 %collective-permute-start.22 = (bf16[96,512]{1,0:T(8,128)(2,1)S(1)}, bf16[96,512]{1,0:T(8,128)(2,1)S(1)}, u32[]{:S(2)}, u32[]{:S(2)}) collective-permute-start(bf16[96,512]{1,0:T(8,128)(2,1)S(1)} %get-tuple-element.86.refs_12_), channel_id=1, source_target_pairs={{0,1},{1,0},{2,3},{3,2},{4,5},{5,4},{6,7},{7,6},{8,9},{9,8},{10,11... | collective-permute-start | bytes 294920 | tf_op jit(solution)/shard_map/ppermute | solution.py:31
  78.2 15.2 %collective-permute-start.25 = (bf16[1088,512]{1,0:T(8,128)(2,1)S(1)}, bf16[1088,512]{1,0:T(8,128)(2,1)S(1)}, u32[]{:S(2)}, u32[]{:S(2)}) collective-permute-start(bf16[1088,512]{1,0:T(8,128)(2,1)S(1)} %get-tuple-element.91), channel_id=1, source_target_pairs={{0,4},{4,0},{8,12},{12,8},{16,20},{20,16},{24,28},{28,24},{1,5},{5... | collective-permute-start | bytes 3342344 | tf_op jit(solution)/shard_map/ppermute | solution.py:31
  78.2 8.9 %collective-permute-start.38 = (bf16[96,1280]{1,0:T(8,128)(2,1)S(1)}, bf16[96,1280]{1,0:T(8,128)(2,1)S(1)}, u32[]{:S(2)}, u32[]{:S(2)}) collective-permute-start(bf16[96,1280]{1,0:T(8,128)(2,1)S(1)} %get-tuple-element.111), channel_id=1, source_target_pairs={{0,1},{1,0},{2,3},{3,2},{4,5},{5,4},{6,7},{7,6},{8,9},{9,8},{10,11... | collective-permute-start | bytes 737288 | tf_op jit(solution)/shard_map/ppermute | solution.py:31
  79.1 8.5 %collective-permute-start.39 = (bf16[96,1280]{1,0:T(8,128)(2,1)S(1)}, bf16[96,1280]{1,0:T(8,128)(2,1)S(1)}, u32[]{:S(2)}, u32[]{:S(2)}) collective-permute-start(bf16[96,1280]{1,0:T(8,128)(2,1)S(1)} %get-tuple-element.112), channel_id=1, source_target_pairs={{0,2},{1,3},{2,0},{3,1},{4,6},{5,7},{6,4},{7,5},{8,10},{9,11},{10,... | collective-permute-start | bytes 737288 | tf_op jit(solution)/shard_map/ppermute | solution.py:31
  80.1 12.4 %collective-permute-start.40 = (bf16[96,1280]{1,0:T(8,128)(2,1)S(1)}, bf16[96,1280]{1,0:T(8,128)(2,1)S(1)}, u32[]{:S(2)}, u32[]{:S(2)}) collective-permute-start(bf16[96,1280]{1,0:T(8,128)(2,1)S(1)} %get-tuple-element.113), channel_id=1, source_target_pairs={{0,3},{1,2},{2,1},{3,0},{4,7},{5,6},{6,5},{7,4},{8,11},{9,10},{10,... | collective-permute-start | bytes 737288 | tf_op jit(solution)/shard_map/ppermute | solution.py:31
  93.3 3.9 %collective-permute-start.41 = (bf16[192,512]{1,0:T(8,128)(2,1)S(1)}, bf16[192,512]{1,0:T(8,128)(2,1)S(1)}, u32[]{:S(2)}, u32[]{:S(2)}) collective-permute-start(bf16[192,512]{1,0:T(8,128)(2,1)S(1)} %get-tuple-element.115), channel_id=1, source_target_pairs={{0,4},{4,0},{8,12},{12,8},{16,20},{20,16},{24,28},{28,24},{1,5},{5... | collective-permute-start | bytes 589832 | tf_op jit(solution)/shard_map/ppermute | solution.py:31
  93.6 15.1 %collective-permute-start.32 = (bf16[256,512]{1,0:T(8,128)(2,1)S(1)}, bf16[256,512]{1,0:T(8,128)(2,1)S(1)}, u32[]{:S(2)}, u32[]{:S(2)}) collective-permute-start(bf16[256,512]{1,0:T(8,128)(2,1)S(1)} %get-tuple-element.103), channel_id=1, source_target_pairs={{0,1},{1,0},{2,3},{3,2},{4,5},{5,4},{6,7},{7,6},{8,9},{9,8},{10,11... | collective-permute-start | bytes 786440 | tf_op jit(solution)/shard_map/ppermute | solution.py:31
  94.9 15.1 %collective-permute-start.33 = (bf16[256,512]{1,0:T(8,128)(2,1)S(1)}, bf16[256,512]{1,0:T(8,128)(2,1)S(1)}, u32[]{:S(2)}, u32[]{:S(2)}) collective-permute-start(bf16[256,512]{1,0:T(8,128)(2,1)S(1)} %get-tuple-element.104), channel_id=1, source_target_pairs={{0,2},{1,3},{2,0},{3,1},{4,6},{5,7},{6,4},{7,5},{8,10},{9,11},{10,... | collective-permute-start | bytes 786440 | tf_op jit(solution)/shard_map/ppermute | solution.py:31
  96.0 14.0 %collective-permute-start.34 = (bf16[256,512]{1,0:T(8,128)(2,1)S(1)}, bf16[256,512]{1,0:T(8,128)(2,1)S(1)}, u32[]{:S(2)}, u32[]{:S(2)}) collective-permute-start(bf16[256,512]{1,0:T(8,128)(2,1)S(1)} %get-tuple-element.105), channel_id=1, source_target_pairs={{0,3},{1,2},{2,1},{3,0},{4,7},{5,6},{6,5},{7,4},{8,11},{9,10},{10,... | collective-permute-start | bytes 786440 | tf_op jit(solution)/shard_map/ppermute | solution.py:31
  97.2 4.4 %collective-permute-start.26 = (bf16[32,512]{1,0:T(8,128)(2,1)S(1)}, bf16[32,512]{1,0:T(8,128)(2,1)S(1)}, u32[]{:S(2)}, u32[]{:S(2)}) collective-permute-start(bf16[32,512]{1,0:T(8,128)(2,1)S(1)} %get-tuple-element.93), channel_id=1, source_target_pairs={{0,8},{4,12},{8,0},{12,4},{16,24},{20,28},{24,16},{28,20},{1,9},{5... | collective-permute-start | bytes 98312 | tf_op jit(solution)/shard_map/ppermute | solution.py:31
  97.2 7.8 %collective-permute-start.27 = (bf16[32,512]{1,0:T(8,128)(2,1)S(1)}, bf16[32,512]{1,0:T(8,128)(2,1)S(1)}, u32[]{:S(2)}, u32[]{:S(2)}) collective-permute-start(bf16[32,512]{1,0:T(8,128)(2,1)S(1)} %get-tuple-element.94), channel_id=1, source_target_pairs={{0,16},{4,20},{8,24},{12,28},{16,0},{20,4},{24,8},{28,12},{1,17},{... | collective-permute-start | bytes 98312 | tf_op jit(solution)/shard_map/ppermute | solution.py:31
  101.6 6.1 %collective-permute-start.28 = (bf16[32,512]{1,0:T(8,128)(2,1)S(1)}, bf16[32,512]{1,0:T(8,128)(2,1)S(1)}, u32[]{:S(2)}, u32[]{:S(2)}) collective-permute-start(bf16[32,512]{1,0:T(8,128)(2,1)S(1)} %get-tuple-element.95), channel_id=1, source_target_pairs={{0,24},{4,28},{8,16},{12,20},{16,8},{20,12},{24,0},{28,4},{1,25},{... | collective-permute-start | bytes 98312 | tf_op jit(solution)/shard_map/ppermute | solution.py:31
  105.0 9.0 %collective-permute-start.42 = (bf16[48,512]{1,0:T(8,128)(2,1)S(1)}, bf16[48,512]{1,0:T(8,128)(2,1)S(1)}, u32[]{:S(2)}, u32[]{:S(2)}) collective-permute-start(bf16[48,512]{1,0:T(8,128)(2,1)S(1)} %get-tuple-element.117), channel_id=1, source_target_pairs={{0,8},{4,12},{8,0},{12,4},{16,24},{20,28},{24,16},{28,20},{1,9},{5... | collective-permute-start | bytes 147464 | tf_op jit(solution)/shard_map/ppermute | solution.py:31
  107.7 8.8 %collective-permute-start.43 = (bf16[48,512]{1,0:T(8,128)(2,1)S(1)}, bf16[48,512]{1,0:T(8,128)(2,1)S(1)}, u32[]{:S(2)}, u32[]{:S(2)}) collective-permute-start(bf16[48,512]{1,0:T(8,128)(2,1)S(1)} %get-tuple-element.118), channel_id=1, source_target_pairs={{0,16},{4,20},{8,24},{12,28},{16,0},{20,4},{24,8},{28,12},{1,17},{... | collective-permute-start | bytes 147464 | tf_op jit(solution)/shard_map/ppermute | solution.py:31
  108.8 20.1 %collective-permute-start.29 = (bf16[96,512]{1,0:T(8,128)(2,1)S(1)}, bf16[96,512]{1,0:T(8,128)(2,1)S(1)}, u32[]{:S(2)}, u32[]{:S(2)}) collective-permute-start(bf16[96,512]{1,0:T(8,128)(2,1)S(1)} %get-tuple-element.97), channel_id=1, source_target_pairs={{0,1},{1,0},{2,3},{3,2},{4,5},{5,4},{6,7},{7,6},{8,9},{9,8},{10,11... | collective-permute-start | bytes 294920 | tf_op jit(solution)/shard_map/ppermute | solution.py:31
  110.2 12.2 %collective-permute-start.35 = (bf16[64,512]{1,0:T(8,128)(2,1)S(1)}, bf16[64,512]{1,0:T(8,128)(2,1)S(1)}, u32[]{:S(2)}, u32[]{:S(2)}) collective-permute-start(bf16[64,512]{1,0:T(8,128)(2,1)S(1)} %get-tuple-element.107), channel_id=1, source_target_pairs={{0,8},{4,12},{8,0},{12,4},{16,24},{20,28},{24,16},{28,20},{1,9},{5... | collective-permute-start | bytes 196616 | tf_op jit(solution)/shard_map/ppermute | solution.py:31
  114.0 8.4 %collective-permute-start.36 = (bf16[64,512]{1,0:T(8,128)(2,1)S(1)}, bf16[64,512]{1,0:T(8,128)(2,1)S(1)}, u32[]{:S(2)}, u32[]{:S(2)}) collective-permute-start(bf16[64,512]{1,0:T(8,128)(2,1)S(1)} %get-tuple-element.108), channel_id=1, source_target_pairs={{0,16},{4,20},{8,24},{12,28},{16,0},{20,4},{24,8},{28,12},{1,17},{... | collective-permute-start | bytes 196616 | tf_op jit(solution)/shard_map/ppermute | solution.py:31
  114.0 8.4 %collective-permute-start.37 = (bf16[64,512]{1,0:T(8,128)(2,1)S(1)}, bf16[64,512]{1,0:T(8,128)(2,1)S(1)}, u32[]{:S(2)}, u32[]{:S(2)}) collective-permute-start(bf16[64,512]{1,0:T(8,128)(2,1)S(1)} %get-tuple-element.109), channel_id=1, source_target_pairs={{0,24},{4,28},{8,16},{12,20},{16,8},{20,12},{24,0},{28,4},{1,25},{... | collective-permute-start | bytes 196616 | tf_op jit(solution)/shard_map/ppermute | solution.py:31
  116.5 6.0 %collective-permute-start.44 = (bf16[48,512]{1,0:T(8,128)(2,1)S(1)}, bf16[48,512]{1,0:T(8,128)(2,1)S(1)}, u32[]{:S(2)}, u32[]{:S(2)}) collective-permute-start(bf16[48,512]{1,0:T(8,128)(2,1)S(1)} %get-tuple-element.119), channel_id=1, source_target_pairs={{0,24},{4,28},{8,16},{12,20},{16,8},{20,12},{24,0},{28,4},{1,25},{... | collective-permute-start | bytes 147464 | tf_op jit(solution)/shard_map/ppermute | solution.py:31
  122.5 10.4 %collective-permute-start.47 = (bf16[112,512]{1,0:T(8,128)(2,1)S(1)}, bf16[112,512]{1,0:T(8,128)(2,1)S(1)}, u32[]{:S(2)}, u32[]{:S(2)}) collective-permute-start(bf16[112,512]{1,0:T(8,128)(2,1)S(1)} %shard_map.198.refs_0_), channel_id=1, source_target_pairs={{0,24},{4,28},{8,16},{12,20},{16,8},{20,12},{24,0},{28,4},{1,25},{... | collective-permute-start | bytes 344072 | tf_op jit(solution)/shard_map/ppermute | solution.py:31
  124.0 9.4 %collective-permute-start.46 = (bf16[112,512]{1,0:T(8,128)(2,1)S(1)}, bf16[112,512]{1,0:T(8,128)(2,1)S(1)}, u32[]{:S(2)}, u32[]{:S(2)}) collective-permute-start(bf16[112,512]{1,0:T(8,128)(2,1)S(1)} %shard_map.198.refs_0_), channel_id=1, source_target_pairs={{0,16},{4,20},{8,24},{12,28},{16,0},{20,4},{24,8},{28,12},{1,17},{... | collective-permute-start | bytes 344072 | tf_op jit(solution)/shard_map/ppermute | solution.py:31
  127.8 6.0 %collective-permute-start.45 = (bf16[112,512]{1,0:T(8,128)(2,1)S(1)}, bf16[112,512]{1,0:T(8,128)(2,1)S(1)}, u32[]{:S(2)}, u32[]{:S(2)}) collective-permute-start(bf16[112,512]{1,0:T(8,128)(2,1)S(1)} %shard_map.198.refs_0_), channel_id=1, source_target_pairs={{0,8},{4,12},{8,0},{12,4},{16,24},{20,28},{24,16},{28,20},{1,9},{5... | collective-permute-start | bytes 344072 | tf_op jit(solution)/shard_map/ppermute | solution.py:31
  127.8 5.1 %collective-permute-start.30 = (bf16[96,512]{1,0:T(8,128)(2,1)S(1)}, bf16[96,512]{1,0:T(8,128)(2,1)S(1)}, u32[]{:S(2)}, u32[]{:S(2)}) collective-permute-start(bf16[96,512]{1,0:T(8,128)(2,1)S(1)} %get-tuple-element.98), channel_id=1, source_target_pairs={{0,2},{1,3},{2,0},{3,1},{4,6},{5,7},{6,4},{7,5},{8,10},{9,11},{10,... | collective-permute-start | bytes 294920 | tf_op jit(solution)/shard_map/ppermute | solution.py:31
  128.9 5.5 %collective-permute-start.31 = (bf16[96,512]{1,0:T(8,128)(2,1)S(1)}, bf16[96,512]{1,0:T(8,128)(2,1)S(1)}, u32[]{:S(2)}, u32[]{:S(2)}) collective-permute-start(bf16[96,512]{1,0:T(8,128)(2,1)S(1)} %get-tuple-element.99), channel_id=1, source_target_pairs={{0,3},{1,2},{2,1},{3,0},{4,7},{5,6},{6,5},{7,4},{8,11},{9,10},{10,... | collective-permute-start | bytes 294920 | tf_op jit(solution)/shard_map/ppermute | solution.py:31
  132.9 2.3 %collective-permute-start.48 = (bf16[112,512]{1,0:T(8,128)(2,1)S(1)}, bf16[112,512]{1,0:T(8,128)(2,1)S(1)}, u32[]{:S(2)}, u32[]{:S(2)}) collective-permute-start(bf16[112,512]{1,0:T(8,128)(2,1)S(1)} %shard_map.198.refs_0_), channel_id=1, source_target_pairs={{0,4},{4,0},{8,12},{12,8},{16,20},{20,16},{24,28},{28,24},{1,5},{5... | collective-permute-start | bytes 344072 | tf_op jit(solution)/shard_map/ppermute | solution.py:31
  (15 other events, 325.6 us)

commit v2 on v1

--- a/solution.py
+++ b/solution.py
@@ -137,47 +137,51 @@
                     out[pl.ds(start, half), :] = grads[u // 2, at : at + half, :].astype(BF16)
 
 
-def pack_kernel(inner, outer, *refs):
-    m = inner.shape[0] + 1
-    half = outer.shape[0] // 2
-    count = (len(refs) - 2) // 2
-    gains, pack, sems, held = refs[:count], refs[count], refs[count + 1], refs[count + 2 :]
+def prepare_kernel(edge_in, edge_out, node_in, node_out, edge_gain, node_gain, lat, rows, *refs):
+    edge_pack, node_pack, lat_out, rows_out, sems, edge_held, node_held = refs
+    half = edge_out.shape[0] // 2
     at = pl.multiple_of(lax.axis_index("region") % 2 * half, half)
-    copies = [pltpu.make_async_copy(gain, ref, sems.at[m + k]) for k, (gain, ref) in enumerate(zip(gains, held))]
-    for k in range(m):
-        source = inner.at[k, pl.ds(at, half)] if k < m - 1 else outer.at[pl.ds(at, half)]
-        copies.append(pltpu.make_async_copy(source, pack.at[pl.ds(k * half, half)], sems.at[k]))
+    moves = [(edge_gain, edge_held), (node_gain, node_held)]
+    for inner, outer, pack in ((edge_in, edge_out, edge_pack), (node_in, node_out, node_pack)):
+        m = inner.shape[0]
+        for k in range(m):
+            moves.append((inner.at[k, pl.ds(at, half)], pack.at[pl.ds(k * half, half)]))
+        moves.append((outer.at[pl.ds(at, half)], pack.at[pl.ds(m * half, half)]))
+    moves += [(lat, lat_out), (rows, rows_out)]
+    copies = [pltpu.make_async_copy(a, b, sems.at[k]) for k, (a, b) in enumerate(moves)]
     for copy in copies:
         copy.start()
+    below = edge_pack.shape[0] - 16
+    edge_pack[below:, :] = jnp.zeros((16, edge_pack.shape[1]), BF16)
     for copy in copies:
         copy.wait()
-    if gains:
-        parts = []
-        for ref in held:
-            left = ref[...]
-            for _ in range(3):
-                part = left.astype(BF16)
-                left = left - part.astype(F32)
-                parts.append(part.astype(F32))
-        parts.append(jnp.zeros((16 - len(parts), left.shape[1]), F32))
-        pack[m * half :, :] = jnp.zeros((16, pack.shape[1]), BF16)
-        pack[m * half :, : left.shape[1]] = jnp.concatenate(parts, axis=0).astype(BF16)
-
-
-def pack_halves(inner, outer, gains):
-    m, d = inner.shape[0] + 1, inner.shape[2]
-    rows = m * (outer.shape[0] // 2) + (16 if gains else 0)
-    ins = [pltpu.with_memory_space_constraint(x, pltpu.HBM) for x in (inner, outer, *gains)]
+    parts = []
+    for ref in (edge_held, node_held):
+        left = ref[...]
+        for _ in range(3):
+            part = left.astype(BF16)
+            left = left - part.astype(F32)
+            parts.append(part.astype(F32))
+    parts.append(jnp.zeros((16 - len(parts), left.shape[1]), F32))
+    edge_pack[below:, : left.shape[1]] = jnp.concatenate(parts, axis=0).astype(BF16)
+
+
+def prepare(*ins):
+    edge_in, edge_out, node_in, _, edge_gain, _, lat, rows = ins
+    half, d = edge_out.shape[0] // 2, edge_out.shape[1]
+    counts = [(edge_in.shape[0] + 1), (node_in.shape[0] + 1)]
+    outs = [shape((counts[0] * half + 16, d)), shape((counts[1] * half, d)), shape(lat.shape), shape(rows.shape, rows.dtype)]
     return pl.pallas_call(
-        pack_kernel,
-        out_shape=shape((rows, d)),
+        prepare_kernel,
+        out_shape=tuple(outs),
         grid=(1,),
         in_specs=[pl.BlockSpec(memory_space=pltpu.HBM)] * len(ins),
-        out_specs=whole_block((rows, d)),
-        scratch_shapes=[pltpu.SemaphoreType.DMA((m + len(gains),))] + [pltpu.VMEM(x.shape, F32) for x in gains],
+        out_specs=tuple(whole_block(x.shape) for x in outs),
+        scratch_shapes=[pltpu.SemaphoreType.DMA((sum(counts) + 4,))] + [pltpu.VMEM(edge_gain.shape, F32)] * 2,
         compiler_params=pltpu.CompilerParams(vmem_limit_bytes=VMEM_LIMIT),
-        cost_estimate=pl.CostEstimate(flops=rows * d, bytes_accessed=4 * rows * d, transcendentals=0),
-    )(*ins)
+        cost_estimate=pl.CostEstimate(flops=8 * half * d, bytes_accessed=32 * half * d, transcendentals=0),
+        name="prepare",
+    )(*(pltpu.with_memory_space_constraint(x, pltpu.HBM) for x in ins))
 
 
 def fill_gains(gain_ref, blocks, own, pieces, here):
@@ -382,23 +386,33 @@
     blocks, outs = refs[:pairs], refs[pairs:]
     nodes = received.shape[0]
     own = nodes // n
-    rows = blocks[0].shape[0]
+    rows = at_ref.shape[1] // pairs
     total = dot_t(sent[:nodes, :], w[1]) + dot_t(received[...], w[2])
     for b in range(pairs):
-        total = total + dot(hot_t(at_ref[0:1, b * rows : (b + 1) * rows], nodes), blocks[b][...])
+        total = total + dot(hot_t(at_ref[0:1, b * rows : (b + 1) * rows], nodes), blocks[b][:rows, :])
     for b in range(n):
         outs[b][...] = total[b * own : (b + 1) * own, :].astype(BF16)
 
 
-def pair_sum_kernel(n, slots, keep, got, *outs):
+def pair_sum_kernel(n, keep, got, *outs):
     block = outs[0].shape[0]
     for b in range(n):
         rows = slice(b * block, (b + 1) * block)
         outs[b][...] = (keep[rows, :].astype(F32) + got[rows, :].astype(F32)).astype(BF16)
-    for b, out in enumerate(outs[n:]):
-        rows = slice(n * block + b * slots, n * block + (b + 1) * slots)
-        out[:slots, :] = keep[rows, :]
-        out[slots:, :] = got[rows, :]
+
+
+def chip_rows_kernel(slots, mine, theirs, *refs):
+    pairs = mine.shape[0] // slots
+    node_parts, outs, total = (refs[:2], refs[2:-1], refs[-1]) if len(refs) > pairs else ((), refs, None)
+    z = lax.axis_index("region") // 2
+    if node_parts:
+        total[...] = add_all([part[...] for part in node_parts])
+    for b, out in enumerate(outs):
+        out[:slots, :] = mine[b * slots : (b + 1) * slots, :]
+        out[slots : 2 * slots, :] = theirs[b * slots : (b + 1) * slots, :]
+        if node_parts:
+            rows = out.shape[0] - 2 * slots
+            out[2 * slots :, :] = total[pl.ds(pl.multiple_of((z ^ b) * rows, 16), rows), :].astype(BF16)
 
 
 def scatter_sum_kernel(n, pairs, *refs):
@@ -413,8 +427,9 @@
 def sum_kernel(pairs, *refs):
     edge, node, out = refs[:pairs], refs[pairs : 2 * pairs], refs[2 * pairs]
     cut = edge[0].shape[0]
+    first = node[0].shape[0] - (out.shape[0] - cut)
     out[:cut, :] = add_all([part[...] for part in edge]).astype(BF16)
-    out[cut:, :] = add_all([part[...] for part in node]).astype(BF16)
+    out[cut:, :] = add_all([part[first:, :] for part in node]).astype(BF16)
 
 
 def finish_kernel(pairs, cut, edge_norm, node_norm, *refs):
@@ -457,7 +472,8 @@
     return [blocks[0]] + [swap(blocks[b], "region", 2 * b) for b in range(1, len(blocks))]
 
 
-def reduce_grads(parts, node_parts, portion, edge_norm, node_norm):
+def reduce_grads(parts, node_parts, back, slots, portion, edge_norm, node_norm):
+    n = len(parts)
     half, d = parts[0].shape
     pairs = lax.axis_size("region") // 2
     z = lax.axis_index("region") // 2
@@ -468,37 +484,45 @@
     aligned = cut % 16 == 0 and rows % 16 == 0
     outs = [shape((k * portion, d), F32) for k in (3, 1, 2, 1)]
 
-    def scattered(parts, total):
-        rows = total // pairs
-        if aligned:
-            parts = call(
-                functools.partial(scatter_sum_kernel, len(parts), pairs),
-                parts,
-                [shape((rows, d))] * pairs,
-                [pltpu.VMEM((total, d), F32)],
-            )
-        else:
-            mine = add_all(parts).astype(BF16).reshape(pairs, rows, d)
-            parts = [lax.dynamic_index_in_dim(mine, z ^ b, 0, keepdims=False) for b in range(pairs)]
-        return chip_exchange(parts)
-
-    node_parts = scattered(node_parts, node_half)
-    parts = scattered(parts, half)
+    def chunks(parts):
+        mine = add_all(parts).astype(BF16).reshape(pairs, -1, d)
+        return [lax.dynamic_index_in_dim(mine, z ^ b, 0, keepdims=False) for b in range(pairs)]
+
+    given = node_parts if aligned else []
+    returned = call(
+        functools.partial(chip_rows_kernel, slots),
+        [*back, *given],
+        [shape((2 * slots + (rows - cut if given else 0), d))] * pairs,
+        [pltpu.VMEM((node_half, d), F32)] if given else [],
+    )
+    if not aligned:
+        returned = [jnp.concatenate(pair) for pair in zip(returned, chunks(node_parts))]
+    returned = chip_exchange(returned)
     if aligned:
-        (chunk,) = call(
-            functools.partial(sum_kernel, pairs), [*parts, *node_parts], [shape((rows, d))]
+        parts = call(
+            functools.partial(scatter_sum_kernel, n, pairs),
+            parts,
+            [shape((cut, d))] * pairs,
+            [pltpu.VMEM((half, d), F32)],
         )
     else:
+        parts = chunks(parts)
+    parts = chip_exchange(parts)
+    if aligned:
+        (chunk,) = call(functools.partial(sum_kernel, pairs), [*parts, *returned], [shape((rows, d))])
+    else:
+        node_parts = [part[2 * slots :] for part in returned]
         chunk = jnp.concatenate([add_all(parts), add_all(node_parts)]).astype(BF16)
     mine = chip_exchange([chunk] * pairs)
     theirs = [swap(piece, "region", 1) for piece in mine]
     if aligned:
-        return call(
+        grads = call(
             functools.partial(finish_kernel, pairs, cut, edge_norm, node_norm),
             mine + theirs,
             outs,
             [pltpu.VMEM((2 * size, d), F32)],
         )
+        return grads, returned
     order = jnp.arange(pairs) ^ z
     sides = []
     for side in (mine, theirs):
@@ -510,7 +534,7 @@
     def from_total(*refs):
         spread(refs[0], refs[1:], edge_norm, node_norm)
 
-    return call(from_total, [total], outs)
+    return call(from_total, [total], outs), returned
 
 
 def layer(
@@ -551,19 +575,21 @@
         nodes + ((remote // slots) ^ region) * slots + remote % slots,
     )
     receiver_at = relative(local_receivers)
+    sender_column, receiver_column, receiver_line = sender_at[:, None], receiver_at[:, None], receiver_at[None]
 
     portion = d // n
     half = portion // 2
     gain_rows = [edge_gain[None], node_gain[None]]
-    near = feat_swaps([node_lat] * n)
-    edge_pack = pack_halves(w_edge_in, w_edge_out, gain_rows)
-    node_pack = pack_halves(w_node_in, w_node_out, [])
+    edge_pack, node_pack, own_lat, listed = prepare(
+        w_edge_in, w_edge_out, w_node_in, w_node_out, *gain_rows, node_lat, send_rows[0]
+    )
+    near = [own_lat] + feat_swaps([node_lat] * n)[1:]
     w_edge = gather_halves(edge_pack)
 
     square = 2 * d * d
     keep, send, send_at = call(
         functools.partial(outgoing_kernel, n),
-        [send_rows[0], *near],
+        [listed, *near],
         [shape((pairs, slots, d))] * 2 + [shape((8, regions * slots), jnp.int32)],
         flops=2 * regions * slots * nodes * d,
     )
@@ -578,7 +604,7 @@
     edge_params = pltpu.CompilerParams(
         dimension_semantics=("arbitrary",), vmem_limit_bytes=VMEM_LIMIT
     )
-    ins = [edge_lat, sender_at[:, None], receiver_at[:, None], receiver_at[None]]
+    ins = [edge_lat, sender_column, receiver_column, receiver_line]
     rest = [*gain_rows, w_edge_in, w_edge_out, *near, *remote_rows, *w_edge]
     outs = [shape((share, d))] * 4 + [shape((share, 128), F32)]
     kept = [shape((table_size, d)), shape((4, d, d)), shape((8, d), F32)] + [shape((own, d))] * n
@@ -609,7 +635,7 @@
     grad_near = feat_swaps([pooled_grad] * n)
     messages = feat_swaps(messages)
 
-    ins = [edge_lat, edge_cot, hidden, slope, normed, inverse, receiver_at[:, None], sender_at[None], receiver_at[None]]
+    ins = [edge_lat, edge_cot, hidden, slope, normed, inverse, receiver_column, sender_at[None], receiver_line]
     rest = [gains, table, w_full, *grad_near]
     kept = [shape((n * 2 * portion + pairs * slots, d))] * 2
     kept += [shape((table_size, d)), shape((nodes, d)), shape((nodes, d))]
@@ -640,20 +666,18 @@
         flops=3 * nodes * square // n,
     )
     node_got = swap(node_send, "region", 1)
-    outs = call(
-        functools.partial(pair_sum_kernel, n, slots),
-        [keep, got],
-        [shape((4 * half, d))] * n + [shape((2 * slots, d))] * pairs,
-    )
-    parts = feat_swaps(outs[:n])
-    returned = chip_exchange(outs[n:])
-    grad_edge_in, grad_edge_out, grad_node_in, grad_node_out = reduce_grads(
-        parts,
+    outs = call(functools.partial(pair_sum_kernel, n), [keep, got], [shape((4 * half, d))] * n)
+    below = n * 4 * half
+    grads, returned = reduce_grads(
+        feat_swaps(outs),
         [node_keep, node_got],
+        [keep[below:], got[below:]],
+        slots,
         portion,
         float((share * n * regions) ** -0.5),
         float((nodes * regions) ** -0.5),
     )
+    grad_edge_in, grad_edge_out, grad_node_in, grad_node_out = grads
 
     edge_grad = pl.pallas_call(
         edge_grad_kernel,
@@ -664,7 +688,7 @@
         compiler_params=edge_params,
         cost_estimate=pl.CostEstimate(flops=2 * share * square, bytes_accessed=8 * share * d, transcendentals=0),
         name="edge_grad",
-    )(edge_cot, receiver_at[:, None], near_grad, edge_pre_grad, w_full)
+    )(edge_cot, receiver_column, near_grad, edge_pre_grad, w_full)
     parts = call(
         functools.partial(return_kernel, n, pairs),
         [sent, received, w_full, send_at, *returned],

time: 137 us -> 137 us (level)
  starting transfers between devices: 60.7 us -> 58.2 us
  waiting for transfers between devices: 48.7 us -> 51.2 us
    ppermute x52 -> x49, waiting for transfers between devices: 48.7 us -> 51.2 us  [swap(): return lax.ppermute(x, axis, [(i, i ^ bits) for i in range(n)])]
    ppermute x52 -> x49, starting transfers between devices: 60.7 us -> 58.2 us  [swap(): return lax.ppermute(x, axis, [(i, i ^ bits) for i in range(n)])]
  transfers between devices with their start and end apart: 52 -> 49, of which waited for: 20 -> 23; matrix products, arithmetic and copies ran while one was open for 1% -> 1% of each run, Pallas kernels for 11% -> 11%
where the time goes in v2:
time: 137 us
  starting transfers between devices  58.2 us (42%)
  waiting for transfers between devices  51.2 us (37%)
  Pallas kernels  24.3 us (18%)
  other arithmetic  1.53 us (1%)
    ppermute x49, starting transfers between devices, swap(): return lax.ppermute(x, axis, [(i, i ^ bits) for i in range(n)])  58.2 us
    ppermute x49, waiting for transfers between devices, swap(): return lax.ppermute(x, axis, [(i, i ^ bits) for i in range(n)])  51.2 us
    pallas_call x1, Pallas kernels, layer(): pl.pallas_call(functools.partial(edge_forward_kernel, n, pairs), out_shap...  7.32 us
    pallas_call x10, Pallas kernels, call(): pl.pallas_call(kernel, out_shape=tuple(outs), grid=(1,), in_specs=[whole_...  6.42 us
    pallas_call x1, Pallas kernels, layer(): pl.pallas_call(functools.partial(edge_backward_kernel, n, slots), out_sha...  6.02 us
  transfers between devices with their start and end apart: 49, of which 23 were waited for; matrix products, arithmetic and copies ran while one was open for 1% of the time, Pallas kernels for 11%

profile of v2, /device:TPU:0, one launch (start us, length us, event | category | flops | bytes accessed | tf_op | source)
XLA Modules:
  0.0 136.6 jit_solution(7172462538462835403)
XLA Ops:
  0.6 3.1 %collective-permute-start.1 = (bf16[96,512]{1,0:T(8,128)(2,1)}, bf16[96,512]{1,0:T(8,128)(2,1)S(1)}, u32[]{:S(2)}, u32[]{:S(2)}) collective-permute-start(bf16[96,512]{1,0:T(8,128)(2,1)} %lat_ref.1), channel_id=1, source_target_pairs={{0,2},{1,3},{2,0},{3,1},{4,6},{5,7},{6,4},{7,5},{8,10},{9,11},{10,... | collective-permute-start | bytes 294920 | tf_op jit(solution)/shard_map/ppermute | solution.py:31
  3.7 2.0 %prepare.1 = (bf16[272,512]{1,0:T(8,128)(2,1)S(1)}, bf16[192,512]{1,0:T(8,128)(2,1)}, bf16[96,512]{1,0:T(8,128)(2,1)S(1)}, s32[8,16]{1,0:T(8,128)S(1)}) custom-call(bf16[3,128,512]{2,1,0:T(8,128)(2,1)} %refs_6_.1, bf16[128,512]{1,0:T(8,128)(2,1)} %refs_7_.1, bf16[2,128,512]{2,1,0:T(8,128)(2,1)} %own_in.1, bf16[128,512]{1,0:T(8,128)(2,1)} %own_out.1, ...), custom_call_target="tpu_custom_call" | custom-call | flops 262144 | bytes 1048576 | tf_op jit(solution)/shard_map/prepare/pallas_call | solution.py:174
  5.7 1.5 %collective-permute-start.11 = (bf16[272,512]{1,0:T(8,128)(2,1)S(1)}, bf16[272,512]{1,0:T(8,128)(2,1)S(1)}, u32[]{:S(2)}, u32[]{:S(2)}) collective-permute-start(bf16[272,512]{1,0:T(8,128)(2,1)S(1)} %get-tuple-element.74), channel_id=1, source_target_pairs={{0,3},{1,2},{2,1},{3,0},{4,7},{5,6},{6,5},{7,4},{8,11},{9,10},{10,... | collective-permute-start | bytes 835592 | tf_op jit(solution)/shard_map/ppermute | solution.py:31
  7.2 1.5 %collective-permute-start.9 = (bf16[272,512]{1,0:T(8,128)(2,1)S(1)}, bf16[272,512]{1,0:T(8,128)(2,1)S(1)}, u32[]{:S(2)}, u32[]{:S(2)}) collective-permute-start(bf16[272,512]{1,0:T(8,128)(2,1)S(1)} %get-tuple-element.74), channel_id=1, source_target_pairs={{0,2},{1,3},{2,0},{3,1},{4,6},{5,7},{6,4},{7,5},{8,10},{9,11},{10,... | collective-permute-start | bytes 835592 | tf_op jit(solution)/shard_map/ppermute | solution.py:31
  9.3 1.5 %collective-permute-start = (bf16[96,512]{1,0:T(8,128)(2,1)}, bf16[96,512]{1,0:T(8,128)(2,1)S(1)}, u32[]{:S(2)}, u32[]{:S(2)}) collective-permute-start(bf16[96,512]{1,0:T(8,128)(2,1)} %lat_ref.1), channel_id=1, source_target_pairs={{0,1},{1,0},{2,3},{3,2},{4,5},{5,4},{6,7},{7,6},{8,9},{9,8},{10,11... | collective-permute-start | bytes 294920 | tf_op jit(solution)/shard_map/ppermute | solution.py:31
  10.9 12.0 %collective-permute-done.refs_1_.refs_9_ = bf16[96,512]{1,0:T(8,128)(2,1)S(1)} collective-permute-done((bf16[96,512]{1,0:T(8,128)(2,1)}, bf16[96,512]{1,0:T(8,128)(2,1)S(1)}, u32[]{:S(2)}, u32[]{:S(2)}) %collective-permute-start) | collective-permute-done | bytes 98336 | tf_op jit(solution)/shard_map/ppermute | solution.py:31
  22.9 2.6 %collective-permute-start.20 = (bf16[192,512]{1,0:T(8,128)(2,1)}, bf16[192,512]{1,0:T(8,128)(2,1)S(1)}, u32[]{:S(2)}, u32[]{:S(2)}) collective-permute-start(bf16[192,512]{1,0:T(8,128)(2,1)} %get-tuple-element.80), channel_id=1, source_target_pairs={{0,3},{1,2},{2,1},{3,0},{4,7},{5,6},{6,5},{7,4},{8,11},{9,10},{10,... | collective-permute-start | bytes 589832 | tf_op jit(solution)/shard_map/ppermute | solution.py:31
  26.1 1.2 collective-permute-done.3.other
  27.4 1.7 %collective-permute-start.4 = (bf16[32,512]{1,0:T(8,128)(2,1)S(1)}, bf16[32,512]{1,0:T(8,128)(2,1)S(1)}, u32[]{:S(2)}, u32[]{:S(2)}) collective-permute-start(bf16[32,512]{1,0:T(8,128)(2,1)S(1)} %get-tuple-element.71), channel_id=1, source_target_pairs={{0,8},{4,12},{8,0},{12,4},{16,24},{20,28},{24,16},{28,20},{1,9},{5... | collective-permute-start | bytes 98312 | tf_op jit(solution)/shard_map/ppermute | solution.py:31
  29.7 1.6 %collective-permute-done.4.refs_13_ = bf16[32,512]{1,0:T(8,128)(2,1)S(1)} collective-permute-done((bf16[32,512]{1,0:T(8,128)(2,1)S(1)}, bf16[32,512]{1,0:T(8,128)(2,1)S(1)}, u32[]{:S(2)}, u32[]{:S(2)}) %collective-permute-start.4) | collective-permute-done | bytes 32800 | tf_op jit(solution)/shard_map/ppermute | solution.py:31
  31.4 2.7 %collective-permute-start.5 = (bf16[32,512]{1,0:T(8,128)(2,1)S(1)}, bf16[32,512]{1,0:T(8,128)(2,1)S(1)}, u32[]{:S(2)}, u32[]{:S(2)}) collective-permute-start(bf16[32,512]{1,0:T(8,128)(2,1)S(1)} %get-tuple-element.72), channel_id=1, source_target_pairs={{0,16},{4,20},{8,24},{12,28},{16,0},{20,4},{24,8},{28,12},{1,17},{... | collective-permute-start | bytes 98312 | tf_op jit(solution)/shard_map/ppermute | solution.py:31
  34.0 2.1 %collective-permute-done.5.refs_14_ = bf16[32,512]{1,0:T(8,128)(2,1)S(1)} collective-permute-done((bf16[32,512]{1,0:T(8,128)(2,1)S(1)}, bf16[32,512]{1,0:T(8,128)(2,1)S(1)}, u32[]{:S(2)}, u32[]{:S(2)}) %collective-permute-start.5) | collective-permute-done | bytes 32800 | tf_op jit(solution)/shard_map/ppermute | solution.py:31
  36.2 3.9 %collective-permute-start.6 = (bf16[32,512]{1,0:T(8,128)(2,1)S(1)}, bf16[32,512]{1,0:T(8,128)(2,1)S(1)}, u32[]{:S(2)}, u32[]{:S(2)}) collective-permute-start(bf16[32,512]{1,0:T(8,128)(2,1)S(1)} %get-tuple-element.73), channel_id=1, source_target_pairs={{0,24},{4,28},{8,16},{12,20},{16,8},{20,12},{24,0},{28,4},{1,25},{... | collective-permute-start | bytes 98312 | tf_op jit(solution)/shard_map/ppermute | solution.py:31
  40.1 1.9 %collective-permute-done.6.refs_15_ = bf16[32,512]{1,0:T(8,128)(2,1)S(1)} collective-permute-done((bf16[32,512]{1,0:T(8,128)(2,1)S(1)}, bf16[32,512]{1,0:T(8,128)(2,1)S(1)}, u32[]{:S(2)}, u32[]{:S(2)}) %collective-permute-start.6) | collective-permute-done | bytes 32800 | tf_op jit(solution)/shard_map/ppermute | solution.py:31
  42.3 1.2 collective-permute-start.16
  44.6 3.2 %collective-permute-done.18.refs_6_ = bf16[192,512]{1,0:T(8,128)(2,1)S(1)} collective-permute-done((bf16[192,512]{1,0:T(8,128)(2,1)}, bf16[192,512]{1,0:T(8,128)(2,1)S(1)}, u32[]{:S(2)}, u32[]{:S(2)}) %collective-permute-start.18) | collective-permute-done | bytes 196640 | tf_op jit(solution)/shard_map/ppermute | solution.py:31
  48.8 7.3 %edge_forward.1 = (bf16[768,512]{1,0:T(8,128)(2,1)}, bf16[768,512]{1,0:T(8,128)(2,1)S(1)}, bf16[768,512]{1,0:T(8,128)(2,1)S(1)}, bf16[768,512]{1,0:T(8,128)(2,1)...) custom-call(bf16[768,512]{1,0:T(8,128)(2,1)S(1)} %copy-done.9, ...), custom_call_target="tpu_custom_call" | custom-call | flops 2818572288 | bytes 3145728 | tf_op jit(solution)/shard_map/edge_forward/pallas_call | solution.py:611
  56.1 1.3 collective-permute-start.13
  57.4 2.0 %collective-permute-start.14 = (bf16[96,512]{1,0:T(8,128)(2,1)S(1)}, bf16[96,512]{1,0:T(8,128)(2,1)S(1)}, u32[]{:S(2)}, u32[]{:S(2)}) collective-permute-start(bf16[96,512]{1,0:T(8,128)(2,1)S(1)} %get-tuple-element.78), channel_id=1, source_target_pairs={{0,2},{1,3},{2,0},{3,1},{4,6},{5,7},{6,4},{7,5},{8,10},{9,11},{10,... | collective-permute-start | bytes 294920 | tf_op jit(solution)/shard_map/ppermute | solution.py:31
  59.6 1.4 %collective-permute-done.13.refs_1_ = bf16[96,512]{1,0:T(8,128)(2,1)S(1)} collective-permute-done((bf16[96,512]{1,0:T(8,128)(2,1)S(1)}, bf16[96,512]{1,0:T(8,128)(2,1)S(1)}, u32[]{:S(2)}, u32[]{:S(2)}) %collective-permute-start.13) | collective-permute-done | bytes 98336 | tf_op jit(solution)/shard_map/ppermute | solution.py:31
  61.0 2.4 %collective-permute-done.14.refs_2_ = bf16[96,512]{1,0:T(8,128)(2,1)S(1)} collective-permute-done((bf16[96,512]{1,0:T(8,128)(2,1)S(1)}, bf16[96,512]{1,0:T(8,128)(2,1)S(1)}, u32[]{:S(2)}, u32[]{:S(2)}) %collective-permute-start.14) | collective-permute-done | bytes 98336 | tf_op jit(solution)/shard_map/ppermute | solution.py:31
  63.5 1.4 %collective-permute-done.15.refs_3_ = bf16[96,512]{1,0:T(8,128)(2,1)S(1)} collective-permute-done((bf16[96,512]{1,0:T(8,128)(2,1)S(1)}, bf16[96,512]{1,0:T(8,128)(2,1)S(1)}, u32[]{:S(2)}, u32[]{:S(2)}) %collective-permute-start.15) | collective-permute-done | bytes 98336 | tf_op jit(solution)/shard_map/ppermute | solution.py:31
  64.9 2.1 %shard_map.190 = (bf16[96,512]{1,0:T(8,128)(2,1)}, bf16[96,512]{1,0:T(8,128)(2,1)S(1)}, f32[96,512]{1,0:T(8,128)S(1)}, bf16[96,1280]{1,0:T(8,128)(2,1)S(1)}, bf1...) custom-call(bf16[96,512]{1,0:T(8,128)(2,1)S(1)} %copy-done.3, ...), custom_call_target="tpu_custom_call" | custom-call | flops 301989888 | bytes 3555328 | tf_op jit(solution)/shard_map/pallas_call | solution.py:91
  67.0 1.2 collective-permute-start.24
  68.2 1.0 collective-permute-start.23
  69.2 1.3 collective-permute-start.22
  70.5 2.3 %collective-permute-done.24.refs_15_ = bf16[96,512]{1,0:T(8,128)(2,1)S(1)} collective-permute-done((bf16[96,512]{1,0:T(8,128)(2,1)S(1)}, bf16[96,512]{1,0:T(8,128)(2,1)S(1)}, u32[]{:S(2)}, u32[]{:S(2)}) %collective-permute-start.24) | collective-permute-done | bytes 98336 | tf_op jit(solution)/shard_map/ppermute | solution.py:31
  73.8 6.0 %edge_backward.1 = (bf16[768,512]{1,0:T(8,128)(2,1)S(1)}, bf16[1088,512]{1,0:T(8,128)(2,1)S(1)}, bf16[1088,512]{1,0:T(8,128)(2,1)S(1)}, bf16[512,512]{1,0:T(8,12...) custom-call(bf16[768,512]{1,0:T(8,128)(2,1)S(1)} %copy-done.9, bf16[768,512]{1,0:T(8,128)(2,1)S(1)} %copy-done.1, ...), custom_call_target="tpu_custom_call" | custom-call | flops 4026531840 | bytes 6291456 | tf_op jit(solution)/shard_map/edge_backward/pallas_call | solution.py:642
  79.9 1.4 collective-permute-start.26
  81.3 1.1 collective-permute-start.27
  82.4 1.1 collective-permute-start.28
  83.5 5.3 %collective-permute-done.26.refs_5_ = bf16[96,1280]{1,0:T(8,128)(2,1)S(1)} collective-permute-done((bf16[96,1280]{1,0:T(8,128)(2,1)S(1)}, bf16[96,1280]{1,0:T(8,128)(2,1)S(1)}, u32[]{:S(2)}, u32[]{:S(2)}) %collective-permute-start.26) | collective-permute-done | bytes 245792 | tf_op jit(solution)/shard_map/ppermute | solution.py:31
  88.8 5.7 %collective-permute-done.27.refs_6_ = bf16[96,1280]{1,0:T(8,128)(2,1)S(1)} collective-permute-done((bf16[96,1280]{1,0:T(8,128)(2,1)S(1)}, bf16[96,1280]{1,0:T(8,128)(2,1)S(1)}, u32[]{:S(2)}, u32[]{:S(2)}) %collective-permute-start.27) | collective-permute-done | bytes 245792 | tf_op jit(solution)/shard_map/ppermute | solution.py:31
  96.7 0.9 collective-permute-start.37
  97.6 1.8 %collective-permute-start.38 = (bf16[256,512]{1,0:T(8,128)(2,1)S(1)}, bf16[256,512]{1,0:T(8,128)(2,1)S(1)}, u32[]{:S(2)}, u32[]{:S(2)}) collective-permute-start(bf16[256,512]{1,0:T(8,128)(2,1)S(1)} %get-tuple-element.115), channel_id=1, source_target_pairs={{0,3},{1,2},{2,1},{3,0},{4,7},{5,6},{6,5},{7,4},{8,11},{9,10},{10,... | collective-permute-start | bytes 786440 | tf_op jit(solution)/shard_map/ppermute | solution.py:31
  99.5 4.4 %collective-permute-start.31 = (bf16[80,512]{1,0:T(8,128)(2,1)S(1)}, bf16[80,512]{1,0:T(8,128)(2,1)S(1)}, u32[]{:S(2)}, u32[]{:S(2)}) collective-permute-start(bf16[80,512]{1,0:T(8,128)(2,1)S(1)} %get-tuple-element.104), channel_id=1, source_target_pairs={{0,16},{4,20},{8,24},{12,28},{16,0},{20,4},{24,8},{28,12},{1,17},{... | collective-permute-start | bytes 245768 | tf_op jit(solution)/shard_map/ppermute | solution.py:31
  104.0 4.4 %collective-permute-start.32 = (bf16[80,512]{1,0:T(8,128)(2,1)S(1)}, bf16[80,512]{1,0:T(8,128)(2,1)S(1)}, u32[]{:S(2)}, u32[]{:S(2)}) collective-permute-start(bf16[80,512]{1,0:T(8,128)(2,1)S(1)} %get-tuple-element.105), channel_id=1, source_target_pairs={{0,24},{4,28},{8,16},{12,20},{16,8},{20,12},{24,0},{28,4},{1,25},{... | collective-permute-start | bytes 245768 | tf_op jit(solution)/shard_map/ppermute | solution.py:31
  109.0 1.9 %collective-permute-done.32.refs_3_.refs_7_ = bf16[80,512]{1,0:T(8,128)(2,1)S(1)} collective-permute-done((bf16[80,512]{1,0:T(8,128)(2,1)S(1)}, bf16[80,512]{1,0:T(8,128)(2,1)S(1)}, u32[]{:S(2)}, u32[]{:S(2)}) %collective-permute-start.32) | collective-permute-done | bytes 81952 | tf_op jit(solution)/shard_map/ppermute | solution.py:31
  110.9 1.0 shard_map.193
  113.0 0.9 collective-permute-start.39
  113.9 3.5 %collective-permute-start.40 = (bf16[64,512]{1,0:T(8,128)(2,1)S(1)}, bf16[64,512]{1,0:T(8,128)(2,1)S(1)}, u32[]{:S(2)}, u32[]{:S(2)}) collective-permute-start(bf16[64,512]{1,0:T(8,128)(2,1)S(1)} %get-tuple-element.118), channel_id=1, source_target_pairs={{0,16},{4,20},{8,24},{12,28},{16,0},{20,4},{24,8},{28,12},{1,17},{... | collective-permute-start | bytes 196616 | tf_op jit(solution)/shard_map/ppermute | solution.py:31
  117.5 3.9 %collective-permute-done.40.refs_2_ = bf16[64,512]{1,0:T(8,128)(2,1)S(1)} collective-permute-done((bf16[64,512]{1,0:T(8,128)(2,1)S(1)}, bf16[64,512]{1,0:T(8,128)(2,1)S(1)}, u32[]{:S(2)}, u32[]{:S(2)}) %collective-permute-start.40) | collective-permute-done | bytes 65568 | tf_op jit(solution)/shard_map/ppermute | solution.py:31
  121.4 2.1 %collective-permute-done.41.refs_3_ = bf16[64,512]{1,0:T(8,128)(2,1)S(1)} collective-permute-done((bf16[64,512]{1,0:T(8,128)(2,1)S(1)}, bf16[64,512]{1,0:T(8,128)(2,1)S(1)}, u32[]{:S(2)}, u32[]{:S(2)}) %collective-permute-start.41) | collective-permute-done | bytes 65568 | tf_op jit(solution)/shard_map/ppermute | solution.py:31
  124.9 3.1 %collective-permute-start.42 = (bf16[112,512]{1,0:T(8,128)(2,1)S(1)}, bf16[112,512]{1,0:T(8,128)(2,1)S(1)}, u32[]{:S(2)}, u32[]{:S(2)}) collective-permute-start(bf16[112,512]{1,0:T(8,128)(2,1)S(1)} %shard_map.196.refs_0_), channel_id=1, source_target_pairs={{0,8},{4,12},{8,0},{12,4},{16,24},{20,28},{24,16},{28,20},{1,9},{5... | collective-permute-start | bytes 344072 | tf_op jit(solution)/shard_map/ppermute | solution.py:31
  128.0 0.9 collective-permute-start.34
  129.0 1.7 %collective-permute-start.35 = (bf16[96,512]{1,0:T(8,128)(2,1)S(1)}, bf16[96,512]{1,0:T(8,128)(2,1)S(1)}, u32[]{:S(2)}, u32[]{:S(2)}) collective-permute-start(bf16[96,512]{1,0:T(8,128)(2,1)S(1)} %get-tuple-element.109), channel_id=1, source_target_pairs={{0,3},{1,2},{2,1},{3,0},{4,7},{5,6},{6,5},{7,4},{8,11},{9,10},{10,... | collective-permute-start | bytes 294920 | tf_op jit(solution)/shard_map/ppermute | solution.py:31
  130.6 2.5 %edge_grad.1 = f32[768,512]{1,0:T(8,128)} custom-call(bf16[768,512]{1,0:T(8,128)(2,1)S(1)} %copy-done.1, s32[768,1]{1,0:T(8,128)S(1)} %broadcast_in_dim.25.refs_2_.refs_6_.r_at, bf16[384,512]{1,0:T(8,128)(2,1)S(1)} %get-tuple-element.110.near, bf16[768,512]{1,0:T(8,128)(2,1)S(1)} %get-tuple-element.111.pre_grad, ...), custom_call_target="tpu_custom_call" | custom-call | flops 805306368 | bytes 3145728 | tf_op jit(solution)/shard_map/edge_grad/pallas_call | solution.py:682
  135.2 1.4 %shard_map.197 = (f32[384,512]{1,0:T(8,128)}, f32[128,512]{1,0:T(8,128)}, f32[256,512]{1,0:T(8,128)}, f32[128,512]{1,0:T(8,128)}) custom-call(bf16[112,512]{1,0:T(8,128)(2,1)S(1)} %shard_map.196.refs_0_, bf16[112,512]{1,0:T(8,128)(2,1)S(1)} %collective-permute-done.42.refs_1_, bf16[112,512]{1,0:T(8,128)(2,1)S(1)} %collective-permute-done.43.refs_2_, ...), custom_call_target="tpu_custom_call" | custom-call | bytes 2752512 | tf_op jit(solution)/shard_map/pallas_call | solution.py:91
  (92 shorter events, 13.1 us)
Async XLA Ops:
  0.6 10.2 %collective-permute-start.1 = (bf16[96,512]{1,0:T(8,128)(2,1)}, bf16[96,512]{1,0:T(8,128)(2,1)S(1)}, u32[]{:S(2)}, u32[]{:S(2)}) collective-permute-start(bf16[96,512]{1,0:T(8,128)(2,1)} %lat_ref.1), channel_id=1, source_target_pairs={{0,2},{1,3},{2,0},{3,1},{4,6},{5,7},{6,4},{7,5},{8,10},{9,11},{10,... | collective-permute-start | bytes 294920 | tf_op jit(solution)/shard_map/ppermute | solution.py:31
  5.7 23.4 %collective-permute-start.11 = (bf16[272,512]{1,0:T(8,128)(2,1)S(1)}, bf16[272,512]{1,0:T(8,128)(2,1)S(1)}, u32[]{:S(2)}, u32[]{:S(2)}) collective-permute-start(bf16[272,512]{1,0:T(8,128)(2,1)S(1)} %get-tuple-element.74), channel_id=1, source_target_pairs={{0,3},{1,2},{2,1},{3,0},{4,7},{5,6},{6,5},{7,4},{8,11},{9,10},{10,... | collective-permute-start | bytes 835592 | tf_op jit(solution)/shard_map/ppermute | solution.py:31
  7.2 21.9 %collective-permute-start.9 = (bf16[272,512]{1,0:T(8,128)(2,1)S(1)}, bf16[272,512]{1,0:T(8,128)(2,1)S(1)}, u32[]{:S(2)}, u32[]{:S(2)}) collective-permute-start(bf16[272,512]{1,0:T(8,128)(2,1)S(1)} %get-tuple-element.74), channel_id=1, source_target_pairs={{0,2},{1,3},{2,0},{3,1},{4,6},{5,7},{6,4},{7,5},{8,10},{9,11},{10,... | collective-permute-start | bytes 835592 | tf_op jit(solution)/shard_map/ppermute | solution.py:31
  8.8 20.9 %collective-permute-start.7 = (bf16[272,512]{1,0:T(8,128)(2,1)S(1)}, bf16[272,512]{1,0:T(8,128)(2,1)S(1)}, u32[]{:S(2)}, u32[]{:S(2)}) collective-permute-start(bf16[272,512]{1,0:T(8,128)(2,1)S(1)} %get-tuple-element.74), channel_id=1, source_target_pairs={{0,1},{1,0},{2,3},{3,2},{4,5},{5,4},{6,7},{7,6},{8,9},{9,8},{10,11... | collective-permute-start | bytes 835592 | tf_op jit(solution)/shard_map/ppermute | solution.py:31
  9.3 13.6 %collective-permute-start = (bf16[96,512]{1,0:T(8,128)(2,1)}, bf16[96,512]{1,0:T(8,128)(2,1)S(1)}, u32[]{:S(2)}, u32[]{:S(2)}) collective-permute-start(bf16[96,512]{1,0:T(8,128)(2,1)} %lat_ref.1), channel_id=1, source_target_pairs={{0,1},{1,0},{2,3},{3,2},{4,5},{5,4},{6,7},{7,6},{8,9},{9,8},{10,11... | collective-permute-start | bytes 294920 | tf_op jit(solution)/shard_map/ppermute | solution.py:31
  10.8 14.8 %collective-permute-start.2 = (bf16[96,512]{1,0:T(8,128)(2,1)}, bf16[96,512]{1,0:T(8,128)(2,1)S(1)}, u32[]{:S(2)}, u32[]{:S(2)}) collective-permute-start(bf16[96,512]{1,0:T(8,128)(2,1)} %lat_ref.1), channel_id=1, source_target_pairs={{0,3},{1,2},{2,1},{3,0},{4,7},{5,6},{6,5},{7,4},{8,11},{9,10},{10,... | collective-permute-start | bytes 294920 | tf_op jit(solution)/shard_map/ppermute | solution.py:31
  22.9 19.4 %collective-permute-start.20 = (bf16[192,512]{1,0:T(8,128)(2,1)}, bf16[192,512]{1,0:T(8,128)(2,1)S(1)}, u32[]{:S(2)}, u32[]{:S(2)}) collective-permute-start(bf16[192,512]{1,0:T(8,128)(2,1)} %get-tuple-element.80), channel_id=1, source_target_pairs={{0,3},{1,2},{2,1},{3,0},{4,7},{5,6},{6,5},{7,4},{8,11},{9,10},{10,... | collective-permute-start | bytes 589832 | tf_op jit(solution)/shard_map/ppermute | solution.py:31
  27.4 4.0 %collective-permute-start.4 = (bf16[32,512]{1,0:T(8,128)(2,1)S(1)}, bf16[32,512]{1,0:T(8,128)(2,1)S(1)}, u32[]{:S(2)}, u32[]{:S(2)}) collective-permute-start(bf16[32,512]{1,0:T(8,128)(2,1)S(1)} %get-tuple-element.71), channel_id=1, source_target_pairs={{0,8},{4,12},{8,0},{12,4},{16,24},{20,28},{24,16},{28,20},{1,9},{5... | collective-permute-start | bytes 98312 | tf_op jit(solution)/shard_map/ppermute | solution.py:31
  29.1 19.3 %collective-permute-start.12 = (bf16[272,512]{1,0:T(8,128)(2,1)S(1)}, bf16[272,512]{1,0:T(8,128)(2,1)S(1)}, u32[]{:S(2)}, u32[]{:S(2)}) collective-permute-start(bf16[272,512]{1,0:T(8,128)(2,1)S(1)} %collective-permute-done.11.refs_20_), channel_id=1, source_target_pairs={{0,4},{4,0},{8,12},{12,8},{16,20},{20,16},{24,28},{28,24},{1,5},{5... | collective-permute-start | bytes 835592 | tf_op jit(solution)/shard_map/ppermute | solution.py:31
  29.1 19.6 %collective-permute-start.10 = (bf16[272,512]{1,0:T(8,128)(2,1)S(1)}, bf16[272,512]{1,0:T(8,128)(2,1)}, u32[]{:S(2)}, u32[]{:S(2)}) collective-permute-start(bf16[272,512]{1,0:T(8,128)(2,1)S(1)} %collective-permute-done.9.refs_18_), channel_id=1, source_target_pairs={{0,4},{4,0},{8,12},{12,8},{16,20},{20,16},{24,28},{28,24},{1,5},{5... | collective-permute-start | bytes 835592 | tf_op jit(solution)/shard_map/ppermute | solution.py:31
  29.6 19.1 %collective-permute-start.8 = (bf16[272,512]{1,0:T(8,128)(2,1)S(1)}, bf16[272,512]{1,0:T(8,128)(2,1)}, u32[]{:S(2)}, u32[]{:S(2)}) collective-permute-start(bf16[272,512]{1,0:T(8,128)(2,1)S(1)} %collective-permute-done.7.refs_16_), channel_id=1, source_target_pairs={{0,4},{4,0},{8,12},{12,8},{16,20},{20,16},{24,28},{28,24},{1,5},{5... | collective-permute-start | bytes 835592 | tf_op jit(solution)/shard_map/ppermute | solution.py:31
  31.4 4.8 %collective-permute-start.5 = (bf16[32,512]{1,0:T(8,128)(2,1)S(1)}, bf16[32,512]{1,0:T(8,128)(2,1)S(1)}, u32[]{:S(2)}, u32[]{:S(2)}) collective-permute-start(bf16[32,512]{1,0:T(8,128)(2,1)S(1)} %get-tuple-element.72), channel_id=1, source_target_pairs={{0,16},{4,20},{8,24},{12,28},{16,0},{20,4},{24,8},{28,12},{1,17},{... | collective-permute-start | bytes 98312 | tf_op jit(solution)/shard_map/ppermute | solution.py:31
  36.2 5.8 %collective-permute-start.6 = (bf16[32,512]{1,0:T(8,128)(2,1)S(1)}, bf16[32,512]{1,0:T(8,128)(2,1)S(1)}, u32[]{:S(2)}, u32[]{:S(2)}) collective-permute-start(bf16[32,512]{1,0:T(8,128)(2,1)S(1)} %get-tuple-element.73), channel_id=1, source_target_pairs={{0,24},{4,28},{8,16},{12,20},{16,8},{20,12},{24,0},{28,4},{1,25},{... | collective-permute-start | bytes 98312 | tf_op jit(solution)/shard_map/ppermute | solution.py:31
  42.0 5.9 %collective-permute-start.18 = (bf16[192,512]{1,0:T(8,128)(2,1)}, bf16[192,512]{1,0:T(8,128)(2,1)S(1)}, u32[]{:S(2)}, u32[]{:S(2)}) collective-permute-start(bf16[192,512]{1,0:T(8,128)(2,1)} %get-tuple-element.80), channel_id=1, source_target_pairs={{0,2},{1,3},{2,0},{3,1},{4,6},{5,7},{6,4},{7,5},{8,10},{9,11},{10,... | collective-permute-start | bytes 589832 | tf_op jit(solution)/shard_map/ppermute | solution.py:31
  42.3 5.9 %collective-permute-start.16 = (bf16[192,512]{1,0:T(8,128)(2,1)}, bf16[192,512]{1,0:T(8,128)(2,1)S(1)}, u32[]{:S(2)}, u32[]{:S(2)}) collective-permute-start(bf16[192,512]{1,0:T(8,128)(2,1)} %get-tuple-element.80), channel_id=1, source_target_pairs={{0,1},{1,0},{2,3},{3,2},{4,5},{5,4},{6,7},{7,6},{8,9},{9,8},{10,11... | collective-permute-start | bytes 589832 | tf_op jit(solution)/shard_map/ppermute | solution.py:31
  47.9 11.5 %collective-permute-start.21 = (bf16[192,512]{1,0:T(8,128)(2,1)S(1)}, bf16[192,512]{1,0:T(8,128)(2,1)S(1)}, u32[]{:S(2)}, u32[]{:S(2)}) collective-permute-start(bf16[192,512]{1,0:T(8,128)(2,1)S(1)} %collective-permute-done.20.refs_8_), channel_id=1, source_target_pairs={{0,4},{4,0},{8,12},{12,8},{16,20},{20,16},{24,28},{28,24},{1,5},{5... | collective-permute-start | bytes 589832 | tf_op jit(solution)/shard_map/ppermute | solution.py:31
  48.2 11.4 %collective-permute-start.19 = (bf16[192,512]{1,0:T(8,128)(2,1)S(1)}, bf16[192,512]{1,0:T(8,128)(2,1)S(1)}, u32[]{:S(2)}, u32[]{:S(2)}) collective-permute-start(bf16[192,512]{1,0:T(8,128)(2,1)S(1)} %collective-permute-done.18.refs_6_), channel_id=1, source_target_pairs={{0,4},{4,0},{8,12},{12,8},{16,20},{20,16},{24,28},{28,24},{1,5},{5... | collective-permute-start | bytes 589832 | tf_op jit(solution)/shard_map/ppermute | solution.py:31
  48.4 11.2 %collective-permute-start.17 = (bf16[192,512]{1,0:T(8,128)(2,1)S(1)}, bf16[192,512]{1,0:T(8,128)(2,1)S(1)}, u32[]{:S(2)}, u32[]{:S(2)}) collective-permute-start(bf16[192,512]{1,0:T(8,128)(2,1)S(1)} %collective-permute-done.16.refs_4_), channel_id=1, source_target_pairs={{0,4},{4,0},{8,12},{12,8},{16,20},{20,16},{24,28},{28,24},{1,5},{5... | collective-permute-start | bytes 589832 | tf_op jit(solution)/shard_map/ppermute | solution.py:31
  56.1 4.9 %collective-permute-start.13 = (bf16[96,512]{1,0:T(8,128)(2,1)S(1)}, bf16[96,512]{1,0:T(8,128)(2,1)S(1)}, u32[]{:S(2)}, u32[]{:S(2)}) collective-permute-start(bf16[96,512]{1,0:T(8,128)(2,1)S(1)} %get-tuple-element.77), channel_id=1, source_target_pairs={{0,1},{1,0},{2,3},{3,2},{4,5},{5,4},{6,7},{7,6},{8,9},{9,8},{10,11... | collective-permute-start | bytes 294920 | tf_op jit(solution)/shard_map/ppermute | solution.py:31
  57.4 6.1 %collective-permute-start.14 = (bf16[96,512]{1,0:T(8,128)(2,1)S(1)}, bf16[96,512]{1,0:T(8,128)(2,1)S(1)}, u32[]{:S(2)}, u32[]{:S(2)}) collective-permute-start(bf16[96,512]{1,0:T(8,128)(2,1)S(1)} %get-tuple-element.78), channel_id=1, source_target_pairs={{0,2},{1,3},{2,0},{3,1},{4,6},{5,7},{6,4},{7,5},{8,10},{9,11},{10,... | collective-permute-start | bytes 294920 | tf_op jit(solution)/shard_map/ppermute | solution.py:31
  59.3 5.5 %collective-permute-start.15 = (bf16[96,512]{1,0:T(8,128)(2,1)S(1)}, bf16[96,512]{1,0:T(8,128)(2,1)S(1)}, u32[]{:S(2)}, u32[]{:S(2)}) collective-permute-start(bf16[96,512]{1,0:T(8,128)(2,1)S(1)} %get-tuple-element.79), channel_id=1, source_target_pairs={{0,3},{1,2},{2,1},{3,0},{4,7},{5,6},{6,5},{7,4},{8,11},{9,10},{10,... | collective-permute-start | bytes 294920 | tf_op jit(solution)/shard_map/ppermute | solution.py:31
  67.0 5.8 %collective-permute-start.24 = (bf16[96,512]{1,0:T(8,128)(2,1)S(1)}, bf16[96,512]{1,0:T(8,128)(2,1)S(1)}, u32[]{:S(2)}, u32[]{:S(2)}) collective-permute-start(bf16[96,512]{1,0:T(8,128)(2,1)S(1)} %get-tuple-element.90.refs_12_), channel_id=1, source_target_pairs={{0,3},{1,2},{2,1},{3,0},{4,7},{5,6},{6,5},{7,4},{8,11},{9,10},{10,... | collective-permute-start | bytes 294920 | tf_op jit(solution)/shard_map/ppermute | solution.py:31
  68.2 5.5 %collective-permute-start.23 = (bf16[96,512]{1,0:T(8,128)(2,1)S(1)}, bf16[96,512]{1,0:T(8,128)(2,1)S(1)}, u32[]{:S(2)}, u32[]{:S(2)}) collective-permute-start(bf16[96,512]{1,0:T(8,128)(2,1)S(1)} %get-tuple-element.90.refs_12_), channel_id=1, source_target_pairs={{0,2},{1,3},{2,0},{3,1},{4,6},{5,7},{6,4},{7,5},{8,10},{9,11},{10,... | collective-permute-start | bytes 294920 | tf_op jit(solution)/shard_map/ppermute | solution.py:31
  69.2 4.6 %collective-permute-start.22 = (bf16[96,512]{1,0:T(8,128)(2,1)S(1)}, bf16[96,512]{1,0:T(8,128)(2,1)S(1)}, u32[]{:S(2)}, u32[]{:S(2)}) collective-permute-start(bf16[96,512]{1,0:T(8,128)(2,1)S(1)} %get-tuple-element.90.refs_12_), channel_id=1, source_target_pairs={{0,1},{1,0},{2,3},{3,2},{4,5},{5,4},{6,7},{7,6},{8,9},{9,8},{10,11... | collective-permute-start | bytes 294920 | tf_op jit(solution)/shard_map/ppermute | solution.py:31
  79.8 15.7 %collective-permute-start.25 = (bf16[1088,512]{1,0:T(8,128)(2,1)S(1)}, bf16[1088,512]{1,0:T(8,128)(2,1)S(1)}, u32[]{:S(2)}, u32[]{:S(2)}) collective-permute-start(bf16[1088,512]{1,0:T(8,128)(2,1)S(1)} %get-tuple-element.95), channel_id=1, source_target_pairs={{0,4},{4,0},{8,12},{12,8},{16,20},{20,16},{24,28},{28,24},{1,5},{5... | collective-permute-start | bytes 3342344 | tf_op jit(solution)/shard_map/ppermute | solution.py:31
  79.9 8.9 %collective-permute-start.26 = (bf16[96,1280]{1,0:T(8,128)(2,1)S(1)}, bf16[96,1280]{1,0:T(8,128)(2,1)S(1)}, u32[]{:S(2)}, u32[]{:S(2)}) collective-permute-start(bf16[96,1280]{1,0:T(8,128)(2,1)S(1)} %get-tuple-element.97), channel_id=1, source_target_pairs={{0,1},{1,0},{2,3},{3,2},{4,5},{5,4},{6,7},{7,6},{8,9},{9,8},{10,11... | collective-permute-start | bytes 737288 | tf_op jit(solution)/shard_map/ppermute | solution.py:31
  81.3 13.3 %collective-permute-start.27 = (bf16[96,1280]{1,0:T(8,128)(2,1)S(1)}, bf16[96,1280]{1,0:T(8,128)(2,1)S(1)}, u32[]{:S(2)}, u32[]{:S(2)}) collective-permute-start(bf16[96,1280]{1,0:T(8,128)(2,1)S(1)} %get-tuple-element.98), channel_id=1, source_target_pairs={{0,2},{1,3},{2,0},{3,1},{4,6},{5,7},{6,4},{7,5},{8,10},{9,11},{10,... | collective-permute-start | bytes 737288 | tf_op jit(solution)/shard_map/ppermute | solution.py:31
  82.4 12.2 %collective-permute-start.28 = (bf16[96,1280]{1,0:T(8,128)(2,1)S(1)}, bf16[96,1280]{1,0:T(8,128)(2,1)S(1)}, u32[]{:S(2)}, u32[]{:S(2)}) collective-permute-start(bf16[96,1280]{1,0:T(8,128)(2,1)S(1)} %get-tuple-element.99), channel_id=1, source_target_pairs={{0,3},{1,2},{2,1},{3,0},{4,7},{5,6},{6,5},{7,4},{8,11},{9,10},{10,... | collective-permute-start | bytes 737288 | tf_op jit(solution)/shard_map/ppermute | solution.py:31
  95.5 3.9 %collective-permute-start.29 = (bf16[192,512]{1,0:T(8,128)(2,1)S(1)}, bf16[192,512]{1,0:T(8,128)(2,1)S(1)}, u32[]{:S(2)}, u32[]{:S(2)}) collective-permute-start(bf16[192,512]{1,0:T(8,128)(2,1)S(1)} %get-tuple-element.101), channel_id=1, source_target_pairs={{0,4},{4,0},{8,12},{12,8},{16,20},{20,16},{24,28},{28,24},{1,5},{5... | collective-permute-start | bytes 589832 | tf_op jit(solution)/shard_map/ppermute | solution.py:31
  95.8 17.0 %collective-permute-start.36 = (bf16[256,512]{1,0:T(8,128)(2,1)S(1)}, bf16[256,512]{1,0:T(8,128)(2,1)S(1)}, u32[]{:S(2)}, u32[]{:S(2)}) collective-permute-start(bf16[256,512]{1,0:T(8,128)(2,1)S(1)} %get-tuple-element.113), channel_id=1, source_target_pairs={{0,1},{1,0},{2,3},{3,2},{4,5},{5,4},{6,7},{7,6},{8,9},{9,8},{10,11... | collective-permute-start | bytes 786440 | tf_op jit(solution)/shard_map/ppermute | solution.py:31
  96.7 16.1 %collective-permute-start.37 = (bf16[256,512]{1,0:T(8,128)(2,1)S(1)}, bf16[256,512]{1,0:T(8,128)(2,1)S(1)}, u32[]{:S(2)}, u32[]{:S(2)}) collective-permute-start(bf16[256,512]{1,0:T(8,128)(2,1)S(1)} %get-tuple-element.114), channel_id=1, source_target_pairs={{0,2},{1,3},{2,0},{3,1},{4,6},{5,7},{6,4},{7,5},{8,10},{9,11},{10,... | collective-permute-start | bytes 786440 | tf_op jit(solution)/shard_map/ppermute | solution.py:31
  97.6 15.2 %collective-permute-start.38 = (bf16[256,512]{1,0:T(8,128)(2,1)S(1)}, bf16[256,512]{1,0:T(8,128)(2,1)S(1)}, u32[]{:S(2)}, u32[]{:S(2)}) collective-permute-start(bf16[256,512]{1,0:T(8,128)(2,1)S(1)} %get-tuple-element.115), channel_id=1, source_target_pairs={{0,3},{1,2},{2,1},{3,0},{4,7},{5,6},{6,5},{7,4},{8,11},{9,10},{10,... | collective-permute-start | bytes 786440 | tf_op jit(solution)/shard_map/ppermute | solution.py:31
  99.5 4.5 %collective-permute-start.30 = (bf16[80,512]{1,0:T(8,128)(2,1)S(1)}, bf16[80,512]{1,0:T(8,128)(2,1)S(1)}, u32[]{:S(2)}, u32[]{:S(2)}) collective-permute-start(bf16[80,512]{1,0:T(8,128)(2,1)S(1)} %get-tuple-element.103), channel_id=1, source_target_pairs={{0,8},{4,12},{8,0},{12,4},{16,24},{20,28},{24,16},{28,20},{1,9},{5... | collective-permute-start | bytes 245768 | tf_op jit(solution)/shard_map/ppermute | solution.py:31
  99.5 9.4 %collective-permute-start.31 = (bf16[80,512]{1,0:T(8,128)(2,1)S(1)}, bf16[80,512]{1,0:T(8,128)(2,1)S(1)}, u32[]{:S(2)}, u32[]{:S(2)}) collective-permute-start(bf16[80,512]{1,0:T(8,128)(2,1)S(1)} %get-tuple-element.104), channel_id=1, source_target_pairs={{0,16},{4,20},{8,24},{12,28},{16,0},{20,4},{24,8},{28,12},{1,17},{... | collective-permute-start | bytes 245768 | tf_op jit(solution)/shard_map/ppermute | solution.py:31
  104.0 6.9 %collective-permute-start.32 = (bf16[80,512]{1,0:T(8,128)(2,1)S(1)}, bf16[80,512]{1,0:T(8,128)(2,1)S(1)}, u32[]{:S(2)}, u32[]{:S(2)}) collective-permute-start(bf16[80,512]{1,0:T(8,128)(2,1)S(1)} %get-tuple-element.105), channel_id=1, source_target_pairs={{0,24},{4,28},{8,16},{12,20},{16,8},{20,12},{24,0},{28,4},{1,25},{... | collective-permute-start | bytes 245768 | tf_op jit(solution)/shard_map/ppermute | solution.py:31
  111.9 17.1 %collective-permute-start.33 = (bf16[96,512]{1,0:T(8,128)(2,1)S(1)}, bf16[96,512]{1,0:T(8,128)(2,1)S(1)}, u32[]{:S(2)}, u32[]{:S(2)}) collective-permute-start(bf16[96,512]{1,0:T(8,128)(2,1)S(1)} %get-tuple-element.107), channel_id=1, source_target_pairs={{0,1},{1,0},{2,3},{3,2},{4,5},{5,4},{6,7},{7,6},{8,9},{9,8},{10,11... | collective-permute-start | bytes 294920 | tf_op jit(solution)/shard_map/ppermute | solution.py:31
  113.0 4.5 %collective-permute-start.39 = (bf16[64,512]{1,0:T(8,128)(2,1)S(1)}, bf16[64,512]{1,0:T(8,128)(2,1)S(1)}, u32[]{:S(2)}, u32[]{:S(2)}) collective-permute-start(bf16[64,512]{1,0:T(8,128)(2,1)S(1)} %get-tuple-element.117), channel_id=1, source_target_pairs={{0,8},{4,12},{8,0},{12,4},{16,24},{20,28},{24,16},{28,20},{1,9},{5... | collective-permute-start | bytes 196616 | tf_op jit(solution)/shard_map/ppermute | solution.py:31
  113.9 7.5 %collective-permute-start.40 = (bf16[64,512]{1,0:T(8,128)(2,1)S(1)}, bf16[64,512]{1,0:T(8,128)(2,1)S(1)}, u32[]{:S(2)}, u32[]{:S(2)}) collective-permute-start(bf16[64,512]{1,0:T(8,128)(2,1)S(1)} %get-tuple-element.118), channel_id=1, source_target_pairs={{0,16},{4,20},{8,24},{12,28},{16,0},{20,4},{24,8},{28,12},{1,17},{... | collective-permute-start | bytes 196616 | tf_op jit(solution)/shard_map/ppermute | solution.py:31
  117.4 6.2 %collective-permute-start.41 = (bf16[64,512]{1,0:T(8,128)(2,1)S(1)}, bf16[64,512]{1,0:T(8,128)(2,1)S(1)}, u32[]{:S(2)}, u32[]{:S(2)}) collective-permute-start(bf16[64,512]{1,0:T(8,128)(2,1)S(1)} %get-tuple-element.119), channel_id=1, source_target_pairs={{0,24},{4,28},{8,16},{12,20},{16,8},{20,12},{24,0},{28,4},{1,25},{... | collective-permute-start | bytes 196616 | tf_op jit(solution)/shard_map/ppermute | solution.py:31
  123.6 9.6 %collective-permute-start.44 = (bf16[112,512]{1,0:T(8,128)(2,1)S(1)}, bf16[112,512]{1,0:T(8,128)(2,1)S(1)}, u32[]{:S(2)}, u32[]{:S(2)}) collective-permute-start(bf16[112,512]{1,0:T(8,128)(2,1)S(1)} %shard_map.196.refs_0_), channel_id=1, source_target_pairs={{0,24},{4,28},{8,16},{12,20},{16,8},{20,12},{24,0},{28,4},{1,25},{... | collective-permute-start | bytes 344072 | tf_op jit(solution)/shard_map/ppermute | solution.py:31
  124.4 9.3 %collective-permute-start.43 = (bf16[112,512]{1,0:T(8,128)(2,1)S(1)}, bf16[112,512]{1,0:T(8,128)(2,1)S(1)}, u32[]{:S(2)}, u32[]{:S(2)}) collective-permute-start(bf16[112,512]{1,0:T(8,128)(2,1)S(1)} %shard_map.196.refs_0_), channel_id=1, source_target_pairs={{0,16},{4,20},{8,24},{12,28},{16,0},{20,4},{24,8},{28,12},{1,17},{... | collective-permute-start | bytes 344072 | tf_op jit(solution)/shard_map/ppermute | solution.py:31
  124.9 8.8 %collective-permute-start.42 = (bf16[112,512]{1,0:T(8,128)(2,1)S(1)}, bf16[112,512]{1,0:T(8,128)(2,1)S(1)}, u32[]{:S(2)}, u32[]{:S(2)}) collective-permute-start(bf16[112,512]{1,0:T(8,128)(2,1)S(1)} %shard_map.196.refs_0_), channel_id=1, source_target_pairs={{0,8},{4,12},{8,0},{12,4},{16,24},{20,28},{24,16},{28,20},{1,9},{5... | collective-permute-start | bytes 344072 | tf_op jit(solution)/shard_map/ppermute | solution.py:31
  128.0 5.1 %collective-permute-start.34 = (bf16[96,512]{1,0:T(8,128)(2,1)S(1)}, bf16[96,512]{1,0:T(8,128)(2,1)S(1)}, u32[]{:S(2)}, u32[]{:S(2)}) collective-permute-start(bf16[96,512]{1,0:T(8,128)(2,1)S(1)} %get-tuple-element.108), channel_id=1, source_target_pairs={{0,2},{1,3},{2,0},{3,1},{4,6},{5,7},{6,4},{7,5},{8,10},{9,11},{10,... | collective-permute-start | bytes 294920 | tf_op jit(solution)/shard_map/ppermute | solution.py:31
  129.0 5.5 %collective-permute-start.35 = (bf16[96,512]{1,0:T(8,128)(2,1)S(1)}, bf16[96,512]{1,0:T(8,128)(2,1)S(1)}, u32[]{:S(2)}, u32[]{:S(2)}) collective-permute-start(bf16[96,512]{1,0:T(8,128)(2,1)S(1)} %get-tuple-element.109), channel_id=1, source_target_pairs={{0,3},{1,2},{2,1},{3,0},{4,7},{5,6},{6,5},{7,4},{8,11},{9,10},{10,... | collective-permute-start | bytes 294920 | tf_op jit(solution)/shard_map/ppermute | solution.py:31
  133.2 2.0 %collective-permute-start.45 = (bf16[112,512]{1,0:T(8,128)(2,1)S(1)}, bf16[112,512]{1,0:T(8,128)(2,1)S(1)}, u32[]{:S(2)}, u32[]{:S(2)}) collective-permute-start(bf16[112,512]{1,0:T(8,128)(2,1)S(1)} %shard_map.196.refs_0_), channel_id=1, source_target_pairs={{0,4},{4,0},{8,12},{12,8},{16,20},{20,16},{24,28},{28,24},{1,5},{5... | collective-permute-start | bytes 344072 | tf_op jit(solution)/shard_map/ppermute | solution.py:31
  133.2 2.0 %collective-permute-start.48 = (bf16[112,512]{1,0:T(8,128)(2,1)S(1)}, bf16[112,512]{1,0:T(8,128)(2,1)S(1)}, u32[]{:S(2)}, u32[]{:S(2)}) collective-permute-start(bf16[112,512]{1,0:T(8,128)(2,1)S(1)} %collective-permute-done.44.refs_3_), channel_id=1, source_target_pairs={{0,4},{4,0},{8,12},{12,8},{16,20},{20,16},{24,28},{28,24},{1,5},{5... | collective-permute-start | bytes 344072 | tf_op jit(solution)/shard_map/ppermute | solution.py:31
  133.7 1.5 %collective-permute-start.47 = (bf16[112,512]{1,0:T(8,128)(2,1)S(1)}, bf16[112,512]{1,0:T(8,128)(2,1)S(1)}, u32[]{:S(2)}, u32[]{:S(2)}) collective-permute-start(bf16[112,512]{1,0:T(8,128)(2,1)S(1)} %collective-permute-done.43.refs_2_), channel_id=1, source_target_pairs={{0,4},{4,0},{8,12},{12,8},{16,20},{20,16},{24,28},{28,24},{1,5},{5... | collective-permute-start | bytes 344072 | tf_op jit(solution)/shard_map/ppermute | solution.py:31
  133.8 1.5 %collective-permute-start.46 = (bf16[112,512]{1,0:T(8,128)(2,1)S(1)}, bf16[112,512]{1,0:T(8,128)(2,1)S(1)}, u32[]{:S(2)}, u32[]{:S(2)}) collective-permute-start(bf16[112,512]{1,0:T(8,128)(2,1)S(1)} %collective-permute-done.42.refs_1_), channel_id=1, source_target_pairs={{0,4},{4,0},{8,12},{12,8},{16,20},{20,16},{24,28},{28,24},{1,5},{5... | collective-permute-start | bytes 344072 | tf_op jit(solution)/shard_map/ppermute | solution.py:31
  (11 other events, 308.5 us)

commit v3 on v2

--- a/solution.py
+++ b/solution.py
@@ -73,10 +73,26 @@
 
 
 def tile_of(rows):
-    for size in (256, 192, 128, 96, 64, 48, 32, 16):
+    if rows <= 1024:
+        return rows
+    for size in (768, 512, 384, 256, 192, 128, 96, 64, 48, 32, 16):
         if rows % size == 0:
             return size
     return rows
+
+
+def accumulate(ref, value):
+    if pl.num_programs(0) == 1:
+        ref[...] = value.astype(ref.dtype)
+    else:
+
+        @pl.when(pl.program_id(0) == 0)
+        def _():
+            ref[...] = value.astype(ref.dtype)
+
+        @pl.when(pl.program_id(0) > 0)
+        def _():
+            ref[...] += value.astype(ref.dtype)
 
 
 def shape(dims, dtype=BF16):
@@ -247,7 +263,6 @@
             at += piece.shape[0]
         fill_weights(w, own_in, own_out, pieces, parity, here)
         fill_gains(gains, blocks, (edge_gain, node_gain), pieces, here)
-        total[...] = jnp.zeros_like(total)
 
     lat = edge[...]
     senders = dot(hot(s_at[...], table.shape[0]), table[...]).astype(BF16)
@@ -261,7 +276,7 @@
     inverse_ref[...] = jnp.broadcast_to(inverse, inverse_ref.shape)
     updated = (lat.astype(F32) + normed * gains[0:1, :]).astype(BF16)
     new[...] = updated
-    total[...] += dot(hot_t(r_row[...], nodes), updated)
+    accumulate(total, dot(hot_t(r_row[...], nodes), updated))
 
     @pl.when(pl.program_id(0) == pl.num_programs(0) - 1)
     def _():
@@ -346,25 +361,22 @@
     def _():
         for b in range(n):
             near_all[b * own : (b + 1) * own, :] = near[b][...]
-        grads[...] = jnp.zeros_like(grads)
-        sent[...] = jnp.zeros_like(sent)
-        received[...] = jnp.zeros_like(received)
 
     total = cot[...].astype(F32) + dot(hot(r_at[...], nodes), near_all[...])
     mix_grad = layer_norm_back(total * gains[0:1, :], normed[...].astype(F32), inverse[:, :1])
     pre_grad = (dot_t(mix_grad, w[3]) * slope[...].astype(F32)).astype(BF16)
     pre_grad_ref[...] = pre_grad
-    grads[0] += t_dot(edge[...], pre_grad)
-    grads[3] += t_dot(hidden[...], mix_grad)
-    sent[...] += dot(hot_t(s_row[...], table.shape[0]), pre_grad)
-    received[...] += dot(hot_t(r_row[...], nodes), pre_grad)
+    accumulate(grads.at[0], t_dot(edge[...], pre_grad))
+    accumulate(grads.at[3], t_dot(hidden[...], mix_grad))
+    accumulate(sent, dot(hot_t(s_row[...], table.shape[0]), pre_grad))
+    accumulate(received, dot(hot_t(r_row[...], nodes), pre_grad))
 
     @pl.when(pl.program_id(0) == pl.num_programs(0) - 1)
     def _():
         from_senders = sent[...].astype(BF16)
         from_receivers = received[...].astype(BF16)
-        grads[1] = t_dot(table[...], from_senders)
-        grads[2] = t_dot(table[:nodes, :], from_receivers)
+        grads[1] = t_dot(table[...], from_senders).astype(grads.dtype)
+        grads[2] = t_dot(table[:nodes, :], from_receivers).astype(grads.dtype)
         split_grads(grads, n, keep, send, parity, here)
         sent_ref[...] = from_senders
         received_ref[...] = from_receivers
@@ -392,6 +404,10 @@
         total = total + dot(hot_t(at_ref[0:1, b * rows : (b + 1) * rows], nodes), blocks[b][:rows, :])
     for b in range(n):
         outs[b][...] = total[b * own : (b + 1) * own, :].astype(BF16)
+
+
+def total_kernel(*refs):
+    refs[-1][...] = add_all([part[...] for part in refs[:-1]])
 
 
 def pair_sum_kernel(n, keep, got, *outs):
@@ -599,6 +615,7 @@
 
     tile = tile_of(share)
     steps = share // tile
+    sum_type = BF16 if steps == 1 else F32
     by_rows = lambda width: pl.BlockSpec((tile, width), lambda i: (i, 0))
     by_columns = pl.BlockSpec((1, tile), lambda i: (0, i))
     edge_params = pltpu.CompilerParams(
@@ -647,9 +664,9 @@
         + [whole_block(x.shape) for x in rest],
         out_specs=tuple([by_rows(d)] + [whole_block(x.shape) for x in kept]),
         scratch_shapes=[
-            pltpu.VMEM((4, d, d), F32),
-            pltpu.VMEM((table_size, d), F32),
-            pltpu.VMEM((nodes, d), F32),
+            pltpu.VMEM((4, d, d), sum_type),
+            pltpu.VMEM((table_size, d), sum_type),
+            pltpu.VMEM((nodes, d), sum_type),
         ],
         compiler_params=edge_params,
         cost_estimate=pl.CostEstimate(
@@ -695,7 +712,7 @@
         [shape((own, d))] * n,
         flops=4 * nodes * square,
     )
-    node_grad = node_base + add_all(feat_swaps(parts))
+    (node_grad,) = call(total_kernel, [node_base, *feat_swaps(parts)], [shape((own, d), F32)])
 
     return (
         node_new,

time: 137 us -> 137 us (level)
  waiting for transfers between devices: 51.2 us -> 55.6 us
  Pallas kernels: 24.3 us -> 21.2 us
    ppermute x49, waiting for transfers between devices: 51.2 us -> 55.6 us  [swap(): return lax.ppermute(x, axis, [(i, i ^ bits) for i in range(n)])]
    pallas_call x1, Pallas kernels: 6.02 us -> 4.25 us  [layer(): pl.pallas_call(functools.partial(edge_backward_kernel, n, slots), out_sha...]
    pallas_call x1, Pallas kernels: 7.32 us -> 5.57 us  [layer(): pl.pallas_call(functools.partial(edge_forward_kernel, n, pairs), out_shap...]
    pallas_call x10 -> x11, Pallas kernels: 6.42 us -> 7.14 us  [call(): pl.pallas_call(kernel, out_shape=tuple(outs), grid=(1,), in_specs=[whole_...]
  transfers between devices with their start and end apart: 49 -> 49, of which waited for: 23 -> 24; matrix products, arithmetic and copies ran while one was open for 1% -> 1% of each run, Pallas kernels for 11% -> 10%
where the time goes in v3:
time: 137 us
  starting transfers between devices  58.3 us (43%)
  waiting for transfers between devices  55.6 us (41%)
  Pallas kernels  21.2 us (15%)
    ppermute x49, starting transfers between devices, swap(): return lax.ppermute(x, axis, [(i, i ^ bits) for i in range(n)])  58.3 us
    ppermute x49, waiting for transfers between devices, swap(): return lax.ppermute(x, axis, [(i, i ^ bits) for i in range(n)])  55.6 us
    pallas_call x11, Pallas kernels, call(): pl.pallas_call(kernel, out_shape=tuple(outs), grid=(1,), in_specs=[whole_...  7.14 us
    pallas_call x1, Pallas kernels, layer(): pl.pallas_call(functools.partial(edge_forward_kernel, n, pairs), out_shap...  5.57 us
    pallas_call x1, Pallas kernels, layer(): pl.pallas_call(functools.partial(edge_backward_kernel, n, slots), out_sha...  4.25 us
  transfers between devices with their start and end apart: 49, of which 24 were waited for; matrix products, arithmetic and copies ran while one was open for 1% of the time, Pallas kernels for 10%

profile of v3, /device:TPU:0, one launch (start us, length us, event | category | flops | bytes accessed | tf_op | source)
XLA Modules:
  0.0 137.2 jit_solution(315841878532500680)
XLA Ops:
  0.6 3.1 %collective-permute-start.1 = (bf16[96,512]{1,0:T(8,128)(2,1)}, bf16[96,512]{1,0:T(8,128)(2,1)S(1)}, u32[]{:S(2)}, u32[]{:S(2)}) collective-permute-start(bf16[96,512]{1,0:T(8,128)(2,1)} %lat_ref.1), channel_id=1, source_target_pairs={{0,2},{1,3},{2,0},{3,1},{4,6},{5,7},{6,4},{7,5},{8,10},{9,11},{10,... | collective-permute-start | bytes 294920 | tf_op jit(solution)/shard_map/ppermute | solution.py:31
  3.7 2.0 %prepare.1 = (bf16[272,512]{1,0:T(8,128)(2,1)S(1)}, bf16[192,512]{1,0:T(8,128)(2,1)}, bf16[96,512]{1,0:T(8,128)(2,1)S(1)}, s32[8,16]{1,0:T(8,128)S(1)}) custom-call(bf16[3,128,512]{2,1,0:T(8,128)(2,1)} %refs_6_.1, bf16[128,512]{1,0:T(8,128)(2,1)} %refs_7_.1, bf16[2,128,512]{2,1,0:T(8,128)(2,1)} %own_in.1, bf16[128,512]{1,0:T(8,128)(2,1)} %own_out.1, ...), custom_call_target="tpu_custom_call" | custom-call | flops 262144 | bytes 1048576 | tf_op jit(solution)/shard_map/prepare/pallas_call | solution.py:190
  5.7 1.5 %collective-permute-start.11 = (bf16[272,512]{1,0:T(8,128)(2,1)S(1)}, bf16[272,512]{1,0:T(8,128)(2,1)S(1)}, u32[]{:S(2)}, u32[]{:S(2)}) collective-permute-start(bf16[272,512]{1,0:T(8,128)(2,1)S(1)} %get-tuple-element.74), channel_id=1, source_target_pairs={{0,3},{1,2},{2,1},{3,0},{4,7},{5,6},{6,5},{7,4},{8,11},{9,10},{10,... | collective-permute-start | bytes 835592 | tf_op jit(solution)/shard_map/ppermute | solution.py:31
  7.2 1.5 %collective-permute-start.9 = (bf16[272,512]{1,0:T(8,128)(2,1)S(1)}, bf16[272,512]{1,0:T(8,128)(2,1)S(1)}, u32[]{:S(2)}, u32[]{:S(2)}) collective-permute-start(bf16[272,512]{1,0:T(8,128)(2,1)S(1)} %get-tuple-element.74), channel_id=1, source_target_pairs={{0,2},{1,3},{2,0},{3,1},{4,6},{5,7},{6,4},{7,5},{8,10},{9,11},{10,... | collective-permute-start | bytes 835592 | tf_op jit(solution)/shard_map/ppermute | solution.py:31
  9.3 1.5 %collective-permute-start = (bf16[96,512]{1,0:T(8,128)(2,1)}, bf16[96,512]{1,0:T(8,128)(2,1)S(1)}, u32[]{:S(2)}, u32[]{:S(2)}) collective-permute-start(bf16[96,512]{1,0:T(8,128)(2,1)} %lat_ref.1), channel_id=1, source_target_pairs={{0,1},{1,0},{2,3},{3,2},{4,5},{5,4},{6,7},{7,6},{8,9},{9,8},{10,11... | collective-permute-start | bytes 294920 | tf_op jit(solution)/shard_map/ppermute | solution.py:31
  10.9 12.0 %collective-permute-done.refs_1_.refs_9_ = bf16[96,512]{1,0:T(8,128)(2,1)S(1)} collective-permute-done((bf16[96,512]{1,0:T(8,128)(2,1)}, bf16[96,512]{1,0:T(8,128)(2,1)S(1)}, u32[]{:S(2)}, u32[]{:S(2)}) %collective-permute-start) | collective-permute-done | bytes 98336 | tf_op jit(solution)/shard_map/ppermute | solution.py:31
  22.9 2.6 %collective-permute-start.20 = (bf16[192,512]{1,0:T(8,128)(2,1)}, bf16[192,512]{1,0:T(8,128)(2,1)S(1)}, u32[]{:S(2)}, u32[]{:S(2)}) collective-permute-start(bf16[192,512]{1,0:T(8,128)(2,1)} %get-tuple-element.80), channel_id=1, source_target_pairs={{0,3},{1,2},{2,1},{3,0},{4,7},{5,6},{6,5},{7,4},{8,11},{9,10},{10,... | collective-permute-start | bytes 589832 | tf_op jit(solution)/shard_map/ppermute | solution.py:31
  26.1 1.2 collective-permute-done.3.other
  27.4 1.7 %collective-permute-start.4 = (bf16[32,512]{1,0:T(8,128)(2,1)S(1)}, bf16[32,512]{1,0:T(8,128)(2,1)S(1)}, u32[]{:S(2)}, u32[]{:S(2)}) collective-permute-start(bf16[32,512]{1,0:T(8,128)(2,1)S(1)} %get-tuple-element.71), channel_id=1, source_target_pairs={{0,8},{4,12},{8,0},{12,4},{16,24},{20,28},{24,16},{28,20},{1,9},{5... | collective-permute-start | bytes 98312 | tf_op jit(solution)/shard_map/ppermute | solution.py:31
  29.7 1.6 %collective-permute-done.4.refs_13_ = bf16[32,512]{1,0:T(8,128)(2,1)S(1)} collective-permute-done((bf16[32,512]{1,0:T(8,128)(2,1)S(1)}, bf16[32,512]{1,0:T(8,128)(2,1)S(1)}, u32[]{:S(2)}, u32[]{:S(2)}) %collective-permute-start.4) | collective-permute-done | bytes 32800 | tf_op jit(solution)/shard_map/ppermute | solution.py:31
  31.4 2.7 %collective-permute-start.5 = (bf16[32,512]{1,0:T(8,128)(2,1)S(1)}, bf16[32,512]{1,0:T(8,128)(2,1)S(1)}, u32[]{:S(2)}, u32[]{:S(2)}) collective-permute-start(bf16[32,512]{1,0:T(8,128)(2,1)S(1)} %get-tuple-element.72), channel_id=1, source_target_pairs={{0,16},{4,20},{8,24},{12,28},{16,0},{20,4},{24,8},{28,12},{1,17},{... | collective-permute-start | bytes 98312 | tf_op jit(solution)/shard_map/ppermute | solution.py:31
  34.0 2.1 %collective-permute-done.5.refs_14_ = bf16[32,512]{1,0:T(8,128)(2,1)S(1)} collective-permute-done((bf16[32,512]{1,0:T(8,128)(2,1)S(1)}, bf16[32,512]{1,0:T(8,128)(2,1)S(1)}, u32[]{:S(2)}, u32[]{:S(2)}) %collective-permute-start.5) | collective-permute-done | bytes 32800 | tf_op jit(solution)/shard_map/ppermute | solution.py:31
  36.2 3.9 %collective-permute-start.6 = (bf16[32,512]{1,0:T(8,128)(2,1)S(1)}, bf16[32,512]{1,0:T(8,128)(2,1)S(1)}, u32[]{:S(2)}, u32[]{:S(2)}) collective-permute-start(bf16[32,512]{1,0:T(8,128)(2,1)S(1)} %get-tuple-element.73), channel_id=1, source_target_pairs={{0,24},{4,28},{8,16},{12,20},{16,8},{20,12},{24,0},{28,4},{1,25},{... | collective-permute-start | bytes 98312 | tf_op jit(solution)/shard_map/ppermute | solution.py:31
  40.1 1.9 %collective-permute-done.6.refs_15_ = bf16[32,512]{1,0:T(8,128)(2,1)S(1)} collective-permute-done((bf16[32,512]{1,0:T(8,128)(2,1)S(1)}, bf16[32,512]{1,0:T(8,128)(2,1)S(1)}, u32[]{:S(2)}, u32[]{:S(2)}) %collective-permute-start.6) | collective-permute-done | bytes 32800 | tf_op jit(solution)/shard_map/ppermute | solution.py:31
  42.3 1.2 collective-permute-start.16
  44.6 3.2 %collective-permute-done.18.refs_6_ = bf16[192,512]{1,0:T(8,128)(2,1)S(1)} collective-permute-done((bf16[192,512]{1,0:T(8,128)(2,1)}, bf16[192,512]{1,0:T(8,128)(2,1)S(1)}, u32[]{:S(2)}, u32[]{:S(2)}) %collective-permute-start.18) | collective-permute-done | bytes 196640 | tf_op jit(solution)/shard_map/ppermute | solution.py:31
  48.8 5.6 %edge_forward.1 = (bf16[768,512]{1,0:T(8,128)(2,1)}, bf16[768,512]{1,0:T(8,128)(2,1)S(1)}, bf16[768,512]{1,0:T(8,128)(2,1)S(1)}, bf16[768,512]{1,0:T(8,128)(2,1)...) custom-call(bf16[768,512]{1,0:T(8,128)(2,1)S(1)} %copy-done.9, ...), custom_call_target="tpu_custom_call" | custom-call | flops 2818572288 | bytes 3145728 | tf_op jit(solution)/shard_map/edge_forward/pallas_call | solution.py:628
  54.4 1.3 collective-permute-start.13
  55.6 2.0 %collective-permute-start.14 = (bf16[96,512]{1,0:T(8,128)(2,1)S(1)}, bf16[96,512]{1,0:T(8,128)(2,1)S(1)}, u32[]{:S(2)}, u32[]{:S(2)}) collective-permute-start(bf16[96,512]{1,0:T(8,128)(2,1)S(1)} %get-tuple-element.78), channel_id=1, source_target_pairs={{0,2},{1,3},{2,0},{3,1},{4,6},{5,7},{6,4},{7,5},{8,10},{9,11},{10,... | collective-permute-start | bytes 294920 | tf_op jit(solution)/shard_map/ppermute | solution.py:31
  57.9 1.4 %collective-permute-done.13.refs_1_ = bf16[96,512]{1,0:T(8,128)(2,1)S(1)} collective-permute-done((bf16[96,512]{1,0:T(8,128)(2,1)S(1)}, bf16[96,512]{1,0:T(8,128)(2,1)S(1)}, u32[]{:S(2)}, u32[]{:S(2)}) %collective-permute-start.13) | collective-permute-done | bytes 98336 | tf_op jit(solution)/shard_map/ppermute | solution.py:31
  59.3 2.4 %collective-permute-done.14.refs_2_ = bf16[96,512]{1,0:T(8,128)(2,1)S(1)} collective-permute-done((bf16[96,512]{1,0:T(8,128)(2,1)S(1)}, bf16[96,512]{1,0:T(8,128)(2,1)S(1)}, u32[]{:S(2)}, u32[]{:S(2)}) %collective-permute-start.14) | collective-permute-done | bytes 98336 | tf_op jit(solution)/shard_map/ppermute | solution.py:31
  61.7 1.4 %collective-permute-done.15.refs_3_ = bf16[96,512]{1,0:T(8,128)(2,1)S(1)} collective-permute-done((bf16[96,512]{1,0:T(8,128)(2,1)S(1)}, bf16[96,512]{1,0:T(8,128)(2,1)S(1)}, u32[]{:S(2)}, u32[]{:S(2)}) %collective-permute-start.15) | collective-permute-done | bytes 98336 | tf_op jit(solution)/shard_map/ppermute | solution.py:31
  63.1 2.1 %shard_map.190 = (bf16[96,512]{1,0:T(8,128)(2,1)}, bf16[96,512]{1,0:T(8,128)(2,1)S(1)}, f32[96,512]{1,0:T(8,128)S(1)}, bf16[96,1280]{1,0:T(8,128)(2,1)S(1)}, bf1...) custom-call(bf16[96,512]{1,0:T(8,128)(2,1)S(1)} %copy-done.3, ...), custom_call_target="tpu_custom_call" | custom-call | flops 301989888 | bytes 3555328 | tf_op jit(solution)/shard_map/pallas_call | solution.py:107
  65.2 1.2 collective-permute-start.24
  67.4 1.3 collective-permute-start.22
  68.7 2.4 %collective-permute-done.24.refs_15_ = bf16[96,512]{1,0:T(8,128)(2,1)S(1)} collective-permute-done((bf16[96,512]{1,0:T(8,128)(2,1)S(1)}, bf16[96,512]{1,0:T(8,128)(2,1)S(1)}, u32[]{:S(2)}, u32[]{:S(2)}) %collective-permute-start.24) | collective-permute-done | bytes 98336 | tf_op jit(solution)/shard_map/ppermute | solution.py:31
  72.1 4.3 %edge_backward.1 = (bf16[768,512]{1,0:T(8,128)(2,1)S(1)}, bf16[1088,512]{1,0:T(8,128)(2,1)S(1)}, bf16[1088,512]{1,0:T(8,128)(2,1)S(1)}, bf16[512,512]{1,0:T(8,12...) custom-call(bf16[768,512]{1,0:T(8,128)(2,1)S(1)} %copy-done.9, bf16[768,512]{1,0:T(8,128)(2,1)S(1)} %copy-done.1, ...), custom_call_target="tpu_custom_call" | custom-call | flops 4026531840 | bytes 6291456 | tf_op jit(solution)/shard_map/edge_backward/pallas_call | solution.py:659
  76.4 1.4 collective-permute-start.26
  77.7 1.1 collective-permute-start.27
  80.0 5.3 %collective-permute-done.26.refs_5_ = bf16[96,1280]{1,0:T(8,128)(2,1)S(1)} collective-permute-done((bf16[96,1280]{1,0:T(8,128)(2,1)S(1)}, bf16[96,1280]{1,0:T(8,128)(2,1)S(1)}, u32[]{:S(2)}, u32[]{:S(2)}) %collective-permute-start.26) | collective-permute-done | bytes 245792 | tf_op jit(solution)/shard_map/ppermute | solution.py:31
  85.3 5.7 %collective-permute-done.27.refs_6_ = bf16[96,1280]{1,0:T(8,128)(2,1)S(1)} collective-permute-done((bf16[96,1280]{1,0:T(8,128)(2,1)S(1)}, bf16[96,1280]{1,0:T(8,128)(2,1)S(1)}, u32[]{:S(2)}, u32[]{:S(2)}) %collective-permute-start.27) | collective-permute-done | bytes 245792 | tf_op jit(solution)/shard_map/ppermute | solution.py:31
  94.0 1.8 %collective-permute-start.38 = (bf16[256,512]{1,0:T(8,128)(2,1)S(1)}, bf16[256,512]{1,0:T(8,128)(2,1)S(1)}, u32[]{:S(2)}, u32[]{:S(2)}) collective-permute-start(bf16[256,512]{1,0:T(8,128)(2,1)S(1)} %get-tuple-element.115), channel_id=1, source_target_pairs={{0,3},{1,2},{2,1},{3,0},{4,7},{5,6},{6,5},{7,4},{8,11},{9,10},{10,... | collective-permute-start | bytes 786440 | tf_op jit(solution)/shard_map/ppermute | solution.py:31
  96.0 4.4 %collective-permute-start.31 = (bf16[80,512]{1,0:T(8,128)(2,1)S(1)}, bf16[80,512]{1,0:T(8,128)(2,1)S(1)}, u32[]{:S(2)}, u32[]{:S(2)}) collective-permute-start(bf16[80,512]{1,0:T(8,128)(2,1)S(1)} %get-tuple-element.104), channel_id=1, source_target_pairs={{0,16},{4,20},{8,24},{12,28},{16,0},{20,4},{24,8},{28,12},{1,17},{... | collective-permute-start | bytes 245768 | tf_op jit(solution)/shard_map/ppermute | solution.py:31
  100.4 1.1 collective-permute-done.36.refs_1_
  101.5 3.8 %collective-permute-start.32 = (bf16[80,512]{1,0:T(8,128)(2,1)S(1)}, bf16[80,512]{1,0:T(8,128)(2,1)S(1)}, u32[]{:S(2)}, u32[]{:S(2)}) collective-permute-start(bf16[80,512]{1,0:T(8,128)(2,1)S(1)} %get-tuple-element.105), channel_id=1, source_target_pairs={{0,24},{4,28},{8,16},{12,20},{16,8},{20,12},{24,0},{28,4},{1,25},{... | collective-permute-start | bytes 245768 | tf_op jit(solution)/shard_map/ppermute | solution.py:31
  105.3 1.9 %collective-permute-done.38.refs_3_ = bf16[256,512]{1,0:T(8,128)(2,1)S(1)} collective-permute-done((bf16[256,512]{1,0:T(8,128)(2,1)S(1)}, bf16[256,512]{1,0:T(8,128)(2,1)S(1)}, u32[]{:S(2)}, u32[]{:S(2)}) %collective-permute-start.38) | collective-permute-done | bytes 262176 | tf_op jit(solution)/shard_map/ppermute | solution.py:31
  107.5 4.4 %collective-permute-start.40 = (bf16[64,512]{1,0:T(8,128)(2,1)S(1)}, bf16[64,512]{1,0:T(8,128)(2,1)S(1)}, u32[]{:S(2)}, u32[]{:S(2)}) collective-permute-start(bf16[64,512]{1,0:T(8,128)(2,1)S(1)} %get-tuple-element.118), channel_id=1, source_target_pairs={{0,16},{4,20},{8,24},{12,28},{16,0},{20,4},{24,8},{28,12},{1,17},{... | collective-permute-start | bytes 196616 | tf_op jit(solution)/shard_map/ppermute | solution.py:31
  111.9 4.4 %collective-permute-done.40.refs_2_ = bf16[64,512]{1,0:T(8,128)(2,1)S(1)} collective-permute-done((bf16[64,512]{1,0:T(8,128)(2,1)S(1)}, bf16[64,512]{1,0:T(8,128)(2,1)S(1)}, u32[]{:S(2)}, u32[]{:S(2)}) %collective-permute-start.40) | collective-permute-done | bytes 65568 | tf_op jit(solution)/shard_map/ppermute | solution.py:31
  116.2 1.7 %collective-permute-done.41.refs_3_ = bf16[64,512]{1,0:T(8,128)(2,1)S(1)} collective-permute-done((bf16[64,512]{1,0:T(8,128)(2,1)S(1)}, bf16[64,512]{1,0:T(8,128)(2,1)S(1)}, u32[]{:S(2)}, u32[]{:S(2)}) %collective-permute-start.41) | collective-permute-done | bytes 65568 | tf_op jit(solution)/shard_map/ppermute | solution.py:31
  118.0 1.6 %collective-permute-start.44 = (bf16[112,512]{1,0:T(8,128)(2,1)S(1)}, bf16[112,512]{1,0:T(8,128)(2,1)S(1)}, u32[]{:S(2)}, u32[]{:S(2)}) collective-permute-start(bf16[112,512]{1,0:T(8,128)(2,1)S(1)} %shard_map.197.refs_0_), channel_id=1, source_target_pairs={{0,24},{4,28},{8,16},{12,20},{16,8},{20,12},{24,0},{28,4},{1,25},{... | collective-permute-start | bytes 344072 | tf_op jit(solution)/shard_map/ppermute | solution.py:31
  119.5 2.9 %collective-permute-start.42 = (bf16[112,512]{1,0:T(8,128)(2,1)S(1)}, bf16[112,512]{1,0:T(8,128)(2,1)S(1)}, u32[]{:S(2)}, u32[]{:S(2)}) collective-permute-start(bf16[112,512]{1,0:T(8,128)(2,1)S(1)} %shard_map.197.refs_0_), channel_id=1, source_target_pairs={{0,8},{4,12},{8,0},{12,4},{16,24},{20,28},{24,16},{28,20},{1,9},{5... | collective-permute-start | bytes 344072 | tf_op jit(solution)/shard_map/ppermute | solution.py:31
  123.4 1.4 collective-permute-start.33
  124.8 1.1 collective-permute-start.34
  125.9 2.2 %collective-permute-done.33.refs_2_ = bf16[96,512]{1,0:T(8,128)(2,1)S(1)} collective-permute-done((bf16[96,512]{1,0:T(8,128)(2,1)S(1)}, bf16[96,512]{1,0:T(8,128)(2,1)S(1)}, u32[]{:S(2)}, u32[]{:S(2)}) %collective-permute-start.33) | collective-permute-done | bytes 98336 | tf_op jit(solution)/shard_map/ppermute | solution.py:31
  129.4 1.6 %collective-permute-start.35 = (bf16[96,512]{1,0:T(8,128)(2,1)S(1)}, bf16[96,512]{1,0:T(8,128)(2,1)S(1)}, u32[]{:S(2)}, u32[]{:S(2)}) collective-permute-start(bf16[96,512]{1,0:T(8,128)(2,1)S(1)} %get-tuple-element.109), channel_id=1, source_target_pairs={{0,3},{1,2},{2,1},{3,0},{4,7},{5,6},{6,5},{7,4},{8,11},{9,10},{10,... | collective-permute-start | bytes 294920 | tf_op jit(solution)/shard_map/ppermute | solution.py:31
  131.0 2.2 %edge_grad.1 = f32[768,512]{1,0:T(8,128)} custom-call(bf16[768,512]{1,0:T(8,128)(2,1)S(1)} %copy-done.1, s32[768,1]{1,0:T(8,128)S(1)} %broadcast_in_dim.25.refs_2_.refs_6_.r_at, bf16[384,512]{1,0:T(8,128)(2,1)S(1)} %get-tuple-element.110.near, bf16[768,512]{1,0:T(8,128)(2,1)S(1)} %get-tuple-element.111.pre_grad, ...), custom_call_target="tpu_custom_call" | custom-call | flops 805306368 | bytes 3145728 | tf_op jit(solution)/shard_map/edge_grad/pallas_call | solution.py:699
  133.2 1.8 %collective-permute-done.35.refs_4_ = bf16[96,512]{1,0:T(8,128)(2,1)S(1)} collective-permute-done((bf16[96,512]{1,0:T(8,128)(2,1)S(1)}, bf16[96,512]{1,0:T(8,128)(2,1)S(1)}, u32[]{:S(2)}, u32[]{:S(2)}) %collective-permute-start.35) | collective-permute-done | bytes 98336 | tf_op jit(solution)/shard_map/ppermute | solution.py:31
  135.8 1.4 %shard_map.198 = (f32[384,512]{1,0:T(8,128)}, f32[128,512]{1,0:T(8,128)}, f32[256,512]{1,0:T(8,128)}, f32[128,512]{1,0:T(8,128)}) custom-call(bf16[112,512]{1,0:T(8,128)(2,1)S(1)} %shard_map.197.refs_0_, bf16[112,512]{1,0:T(8,128)(2,1)S(1)} %collective-permute-done.42.refs_1_, bf16[112,512]{1,0:T(8,128)(2,1)S(1)} %collective-permute-done.43.refs_2_, ...), custom_call_target="tpu_custom_call" | custom-call | bytes 2752512 | tf_op jit(solution)/shard_map/pallas_call | solution.py:107
  (92 shorter events, 14.1 us)
Async XLA Ops:
  0.6 10.2 %collective-permute-start.1 = (bf16[96,512]{1,0:T(8,128)(2,1)}, bf16[96,512]{1,0:T(8,128)(2,1)S(1)}, u32[]{:S(2)}, u32[]{:S(2)}) collective-permute-start(bf16[96,512]{1,0:T(8,128)(2,1)} %lat_ref.1), channel_id=1, source_target_pairs={{0,2},{1,3},{2,0},{3,1},{4,6},{5,7},{6,4},{7,5},{8,10},{9,11},{10,... | collective-permute-start | bytes 294920 | tf_op jit(solution)/shard_map/ppermute | solution.py:31
  5.7 23.4 %collective-permute-start.11 = (bf16[272,512]{1,0:T(8,128)(2,1)S(1)}, bf16[272,512]{1,0:T(8,128)(2,1)S(1)}, u32[]{:S(2)}, u32[]{:S(2)}) collective-permute-start(bf16[272,512]{1,0:T(8,128)(2,1)S(1)} %get-tuple-element.74), channel_id=1, source_target_pairs={{0,3},{1,2},{2,1},{3,0},{4,7},{5,6},{6,5},{7,4},{8,11},{9,10},{10,... | collective-permute-start | bytes 835592 | tf_op jit(solution)/shard_map/ppermute | solution.py:31
  7.2 21.9 %collective-permute-start.9 = (bf16[272,512]{1,0:T(8,128)(2,1)S(1)}, bf16[272,512]{1,0:T(8,128)(2,1)S(1)}, u32[]{:S(2)}, u32[]{:S(2)}) collective-permute-start(bf16[272,512]{1,0:T(8,128)(2,1)S(1)} %get-tuple-element.74), channel_id=1, source_target_pairs={{0,2},{1,3},{2,0},{3,1},{4,6},{5,7},{6,4},{7,5},{8,10},{9,11},{10,... | collective-permute-start | bytes 835592 | tf_op jit(solution)/shard_map/ppermute | solution.py:31
  8.8 20.9 %collective-permute-start.7 = (bf16[272,512]{1,0:T(8,128)(2,1)S(1)}, bf16[272,512]{1,0:T(8,128)(2,1)S(1)}, u32[]{:S(2)}, u32[]{:S(2)}) collective-permute-start(bf16[272,512]{1,0:T(8,128)(2,1)S(1)} %get-tuple-element.74), channel_id=1, source_target_pairs={{0,1},{1,0},{2,3},{3,2},{4,5},{5,4},{6,7},{7,6},{8,9},{9,8},{10,11... | collective-permute-start | bytes 835592 | tf_op jit(solution)/shard_map/ppermute | solution.py:31
  9.3 13.6 %collective-permute-start = (bf16[96,512]{1,0:T(8,128)(2,1)}, bf16[96,512]{1,0:T(8,128)(2,1)S(1)}, u32[]{:S(2)}, u32[]{:S(2)}) collective-permute-start(bf16[96,512]{1,0:T(8,128)(2,1)} %lat_ref.1), channel_id=1, source_target_pairs={{0,1},{1,0},{2,3},{3,2},{4,5},{5,4},{6,7},{7,6},{8,9},{9,8},{10,11... | collective-permute-start | bytes 294920 | tf_op jit(solution)/shard_map/ppermute | solution.py:31
  10.8 14.8 %collective-permute-start.2 = (bf16[96,512]{1,0:T(8,128)(2,1)}, bf16[96,512]{1,0:T(8,128)(2,1)S(1)}, u32[]{:S(2)}, u32[]{:S(2)}) collective-permute-start(bf16[96,512]{1,0:T(8,128)(2,1)} %lat_ref.1), channel_id=1, source_target_pairs={{0,3},{1,2},{2,1},{3,0},{4,7},{5,6},{6,5},{7,4},{8,11},{9,10},{10,... | collective-permute-start | bytes 294920 | tf_op jit(solution)/shard_map/ppermute | solution.py:31
  22.9 19.4 %collective-permute-start.20 = (bf16[192,512]{1,0:T(8,128)(2,1)}, bf16[192,512]{1,0:T(8,128)(2,1)S(1)}, u32[]{:S(2)}, u32[]{:S(2)}) collective-permute-start(bf16[192,512]{1,0:T(8,128)(2,1)} %get-tuple-element.80), channel_id=1, source_target_pairs={{0,3},{1,2},{2,1},{3,0},{4,7},{5,6},{6,5},{7,4},{8,11},{9,10},{10,... | collective-permute-start | bytes 589832 | tf_op jit(solution)/shard_map/ppermute | solution.py:31
  27.4 4.0 %collective-permute-start.4 = (bf16[32,512]{1,0:T(8,128)(2,1)S(1)}, bf16[32,512]{1,0:T(8,128)(2,1)S(1)}, u32[]{:S(2)}, u32[]{:S(2)}) collective-permute-start(bf16[32,512]{1,0:T(8,128)(2,1)S(1)} %get-tuple-element.71), channel_id=1, source_target_pairs={{0,8},{4,12},{8,0},{12,4},{16,24},{20,28},{24,16},{28,20},{1,9},{5... | collective-permute-start | bytes 98312 | tf_op jit(solution)/shard_map/ppermute | solution.py:31
  29.1 19.3 %collective-permute-start.12 = (bf16[272,512]{1,0:T(8,128)(2,1)S(1)}, bf16[272,512]{1,0:T(8,128)(2,1)S(1)}, u32[]{:S(2)}, u32[]{:S(2)}) collective-permute-start(bf16[272,512]{1,0:T(8,128)(2,1)S(1)} %collective-permute-done.11.refs_20_), channel_id=1, source_target_pairs={{0,4},{4,0},{8,12},{12,8},{16,20},{20,16},{24,28},{28,24},{1,5},{5... | collective-permute-start | bytes 835592 | tf_op jit(solution)/shard_map/ppermute | solution.py:31
  29.1 19.6 %collective-permute-start.10 = (bf16[272,512]{1,0:T(8,128)(2,1)S(1)}, bf16[272,512]{1,0:T(8,128)(2,1)}, u32[]{:S(2)}, u32[]{:S(2)}) collective-permute-start(bf16[272,512]{1,0:T(8,128)(2,1)S(1)} %collective-permute-done.9.refs_18_), channel_id=1, source_target_pairs={{0,4},{4,0},{8,12},{12,8},{16,20},{20,16},{24,28},{28,24},{1,5},{5... | collective-permute-start | bytes 835592 | tf_op jit(solution)/shard_map/ppermute | solution.py:31
  29.6 19.1 %collective-permute-start.8 = (bf16[272,512]{1,0:T(8,128)(2,1)S(1)}, bf16[272,512]{1,0:T(8,128)(2,1)}, u32[]{:S(2)}, u32[]{:S(2)}) collective-permute-start(bf16[272,512]{1,0:T(8,128)(2,1)S(1)} %collective-permute-done.7.refs_16_), channel_id=1, source_target_pairs={{0,4},{4,0},{8,12},{12,8},{16,20},{20,16},{24,28},{28,24},{1,5},{5... | collective-permute-start | bytes 835592 | tf_op jit(solution)/shard_map/ppermute | solution.py:31
  31.4 4.8 %collective-permute-start.5 = (bf16[32,512]{1,0:T(8,128)(2,1)S(1)}, bf16[32,512]{1,0:T(8,128)(2,1)S(1)}, u32[]{:S(2)}, u32[]{:S(2)}) collective-permute-start(bf16[32,512]{1,0:T(8,128)(2,1)S(1)} %get-tuple-element.72), channel_id=1, source_target_pairs={{0,16},{4,20},{8,24},{12,28},{16,0},{20,4},{24,8},{28,12},{1,17},{... | collective-permute-start | bytes 98312 | tf_op jit(solution)/shard_map/ppermute | solution.py:31
  36.2 5.8 %collective-permute-start.6 = (bf16[32,512]{1,0:T(8,128)(2,1)S(1)}, bf16[32,512]{1,0:T(8,128)(2,1)S(1)}, u32[]{:S(2)}, u32[]{:S(2)}) collective-permute-start(bf16[32,512]{1,0:T(8,128)(2,1)S(1)} %get-tuple-element.73), channel_id=1, source_target_pairs={{0,24},{4,28},{8,16},{12,20},{16,8},{20,12},{24,0},{28,4},{1,25},{... | collective-permute-start | bytes 98312 | tf_op jit(solution)/shard_map/ppermute | solution.py:31
  42.0 5.9 %collective-permute-start.18 = (bf16[192,512]{1,0:T(8,128)(2,1)}, bf16[192,512]{1,0:T(8,128)(2,1)S(1)}, u32[]{:S(2)}, u32[]{:S(2)}) collective-permute-start(bf16[192,512]{1,0:T(8,128)(2,1)} %get-tuple-element.80), channel_id=1, source_target_pairs={{0,2},{1,3},{2,0},{3,1},{4,6},{5,7},{6,4},{7,5},{8,10},{9,11},{10,... | collective-permute-start | bytes 589832 | tf_op jit(solution)/shard_map/ppermute | solution.py:31
  42.3 5.9 %collective-permute-start.16 = (bf16[192,512]{1,0:T(8,128)(2,1)}, bf16[192,512]{1,0:T(8,128)(2,1)S(1)}, u32[]{:S(2)}, u32[]{:S(2)}) collective-permute-start(bf16[192,512]{1,0:T(8,128)(2,1)} %get-tuple-element.80), channel_id=1, source_target_pairs={{0,1},{1,0},{2,3},{3,2},{4,5},{5,4},{6,7},{7,6},{8,9},{9,8},{10,11... | collective-permute-start | bytes 589832 | tf_op jit(solution)/shard_map/ppermute | solution.py:31
  47.9 9.7 %collective-permute-start.21 = (bf16[192,512]{1,0:T(8,128)(2,1)S(1)}, bf16[192,512]{1,0:T(8,128)(2,1)S(1)}, u32[]{:S(2)}, u32[]{:S(2)}) collective-permute-start(bf16[192,512]{1,0:T(8,128)(2,1)S(1)} %collective-permute-done.20.refs_8_), channel_id=1, source_target_pairs={{0,4},{4,0},{8,12},{12,8},{16,20},{20,16},{24,28},{28,24},{1,5},{5... | collective-permute-start | bytes 589832 | tf_op jit(solution)/shard_map/ppermute | solution.py:31
  48.2 9.7 %collective-permute-start.19 = (bf16[192,512]{1,0:T(8,128)(2,1)S(1)}, bf16[192,512]{1,0:T(8,128)(2,1)S(1)}, u32[]{:S(2)}, u32[]{:S(2)}) collective-permute-start(bf16[192,512]{1,0:T(8,128)(2,1)S(1)} %collective-permute-done.18.refs_6_), channel_id=1, source_target_pairs={{0,4},{4,0},{8,12},{12,8},{16,20},{20,16},{24,28},{28,24},{1,5},{5... | collective-permute-start | bytes 589832 | tf_op jit(solution)/shard_map/ppermute | solution.py:31
  48.4 9.5 %collective-permute-start.17 = (bf16[192,512]{1,0:T(8,128)(2,1)S(1)}, bf16[192,512]{1,0:T(8,128)(2,1)S(1)}, u32[]{:S(2)}, u32[]{:S(2)}) collective-permute-start(bf16[192,512]{1,0:T(8,128)(2,1)S(1)} %collective-permute-done.16.refs_4_), channel_id=1, source_target_pairs={{0,4},{4,0},{8,12},{12,8},{16,20},{20,16},{24,28},{28,24},{1,5},{5... | collective-permute-start | bytes 589832 | tf_op jit(solution)/shard_map/ppermute | solution.py:31
  54.4 4.9 %collective-permute-start.13 = (bf16[96,512]{1,0:T(8,128)(2,1)S(1)}, bf16[96,512]{1,0:T(8,128)(2,1)S(1)}, u32[]{:S(2)}, u32[]{:S(2)}) collective-permute-start(bf16[96,512]{1,0:T(8,128)(2,1)S(1)} %get-tuple-element.77), channel_id=1, source_target_pairs={{0,1},{1,0},{2,3},{3,2},{4,5},{5,4},{6,7},{7,6},{8,9},{9,8},{10,11... | collective-permute-start | bytes 294920 | tf_op jit(solution)/shard_map/ppermute | solution.py:31
  55.6 6.1 %collective-permute-start.14 = (bf16[96,512]{1,0:T(8,128)(2,1)S(1)}, bf16[96,512]{1,0:T(8,128)(2,1)S(1)}, u32[]{:S(2)}, u32[]{:S(2)}) collective-permute-start(bf16[96,512]{1,0:T(8,128)(2,1)S(1)} %get-tuple-element.78), channel_id=1, source_target_pairs={{0,2},{1,3},{2,0},{3,1},{4,6},{5,7},{6,4},{7,5},{8,10},{9,11},{10,... | collective-permute-start | bytes 294920 | tf_op jit(solution)/shard_map/ppermute | solution.py:31
  57.6 5.5 %collective-permute-start.15 = (bf16[96,512]{1,0:T(8,128)(2,1)S(1)}, bf16[96,512]{1,0:T(8,128)(2,1)S(1)}, u32[]{:S(2)}, u32[]{:S(2)}) collective-permute-start(bf16[96,512]{1,0:T(8,128)(2,1)S(1)} %get-tuple-element.79), channel_id=1, source_target_pairs={{0,3},{1,2},{2,1},{3,0},{4,7},{5,6},{6,5},{7,4},{8,11},{9,10},{10,... | collective-permute-start | bytes 294920 | tf_op jit(solution)/shard_map/ppermute | solution.py:31
  65.2 5.8 %collective-permute-start.24 = (bf16[96,512]{1,0:T(8,128)(2,1)S(1)}, bf16[96,512]{1,0:T(8,128)(2,1)S(1)}, u32[]{:S(2)}, u32[]{:S(2)}) collective-permute-start(bf16[96,512]{1,0:T(8,128)(2,1)S(1)} %get-tuple-element.90.refs_12_), channel_id=1, source_target_pairs={{0,3},{1,2},{2,1},{3,0},{4,7},{5,6},{6,5},{7,4},{8,11},{9,10},{10,... | collective-permute-start | bytes 294920 | tf_op jit(solution)/shard_map/ppermute | solution.py:31
  66.4 5.5 %collective-permute-start.23 = (bf16[96,512]{1,0:T(8,128)(2,1)S(1)}, bf16[96,512]{1,0:T(8,128)(2,1)S(1)}, u32[]{:S(2)}, u32[]{:S(2)}) collective-permute-start(bf16[96,512]{1,0:T(8,128)(2,1)S(1)} %get-tuple-element.90.refs_12_), channel_id=1, source_target_pairs={{0,2},{1,3},{2,0},{3,1},{4,6},{5,7},{6,4},{7,5},{8,10},{9,11},{10,... | collective-permute-start | bytes 294920 | tf_op jit(solution)/shard_map/ppermute | solution.py:31
  67.4 4.6 %collective-permute-start.22 = (bf16[96,512]{1,0:T(8,128)(2,1)S(1)}, bf16[96,512]{1,0:T(8,128)(2,1)S(1)}, u32[]{:S(2)}, u32[]{:S(2)}) collective-permute-start(bf16[96,512]{1,0:T(8,128)(2,1)S(1)} %get-tuple-element.90.refs_12_), channel_id=1, source_target_pairs={{0,1},{1,0},{2,3},{3,2},{4,5},{5,4},{6,7},{7,6},{8,9},{9,8},{10,11... | collective-permute-start | bytes 294920 | tf_op jit(solution)/shard_map/ppermute | solution.py:31
  76.3 15.7 %collective-permute-start.25 = (bf16[1088,512]{1,0:T(8,128)(2,1)S(1)}, bf16[1088,512]{1,0:T(8,128)(2,1)S(1)}, u32[]{:S(2)}, u32[]{:S(2)}) collective-permute-start(bf16[1088,512]{1,0:T(8,128)(2,1)S(1)} %get-tuple-element.95), channel_id=1, source_target_pairs={{0,4},{4,0},{8,12},{12,8},{16,20},{20,16},{24,28},{28,24},{1,5},{5... | collective-permute-start | bytes 3342344 | tf_op jit(solution)/shard_map/ppermute | solution.py:31
  76.4 8.9 %collective-permute-start.26 = (bf16[96,1280]{1,0:T(8,128)(2,1)S(1)}, bf16[96,1280]{1,0:T(8,128)(2,1)S(1)}, u32[]{:S(2)}, u32[]{:S(2)}) collective-permute-start(bf16[96,1280]{1,0:T(8,128)(2,1)S(1)} %get-tuple-element.97), channel_id=1, source_target_pairs={{0,1},{1,0},{2,3},{3,2},{4,5},{5,4},{6,7},{7,6},{8,9},{9,8},{10,11... | collective-permute-start | bytes 737288 | tf_op jit(solution)/shard_map/ppermute | solution.py:31
  77.7 13.3 %collective-permute-start.27 = (bf16[96,1280]{1,0:T(8,128)(2,1)S(1)}, bf16[96,1280]{1,0:T(8,128)(2,1)S(1)}, u32[]{:S(2)}, u32[]{:S(2)}) collective-permute-start(bf16[96,1280]{1,0:T(8,128)(2,1)S(1)} %get-tuple-element.98), channel_id=1, source_target_pairs={{0,2},{1,3},{2,0},{3,1},{4,6},{5,7},{6,4},{7,5},{8,10},{9,11},{10,... | collective-permute-start | bytes 737288 | tf_op jit(solution)/shard_map/ppermute | solution.py:31
  78.9 12.2 %collective-permute-start.28 = (bf16[96,1280]{1,0:T(8,128)(2,1)S(1)}, bf16[96,1280]{1,0:T(8,128)(2,1)S(1)}, u32[]{:S(2)}, u32[]{:S(2)}) collective-permute-start(bf16[96,1280]{1,0:T(8,128)(2,1)S(1)} %get-tuple-element.99), channel_id=1, source_target_pairs={{0,3},{1,2},{2,1},{3,0},{4,7},{5,6},{6,5},{7,4},{8,11},{9,10},{10,... | collective-permute-start | bytes 737288 | tf_op jit(solution)/shard_map/ppermute | solution.py:31
  91.9 3.9 %collective-permute-start.29 = (bf16[192,512]{1,0:T(8,128)(2,1)S(1)}, bf16[192,512]{1,0:T(8,128)(2,1)S(1)}, u32[]{:S(2)}, u32[]{:S(2)}) collective-permute-start(bf16[192,512]{1,0:T(8,128)(2,1)S(1)} %get-tuple-element.101), channel_id=1, source_target_pairs={{0,4},{4,0},{8,12},{12,8},{16,20},{20,16},{24,28},{28,24},{1,5},{5... | collective-permute-start | bytes 589832 | tf_op jit(solution)/shard_map/ppermute | solution.py:31
  92.2 9.2 %collective-permute-start.36 = (bf16[256,512]{1,0:T(8,128)(2,1)S(1)}, bf16[256,512]{1,0:T(8,128)(2,1)S(1)}, u32[]{:S(2)}, u32[]{:S(2)}) collective-permute-start(bf16[256,512]{1,0:T(8,128)(2,1)S(1)} %get-tuple-element.113), channel_id=1, source_target_pairs={{0,1},{1,0},{2,3},{3,2},{4,5},{5,4},{6,7},{7,6},{8,9},{9,8},{10,11... | collective-permute-start | bytes 786440 | tf_op jit(solution)/shard_map/ppermute | solution.py:31
  93.1 12.2 %collective-permute-start.37 = (bf16[256,512]{1,0:T(8,128)(2,1)S(1)}, bf16[256,512]{1,0:T(8,128)(2,1)S(1)}, u32[]{:S(2)}, u32[]{:S(2)}) collective-permute-start(bf16[256,512]{1,0:T(8,128)(2,1)S(1)} %get-tuple-element.114), channel_id=1, source_target_pairs={{0,2},{1,3},{2,0},{3,1},{4,6},{5,7},{6,4},{7,5},{8,10},{9,11},{10,... | collective-permute-start | bytes 786440 | tf_op jit(solution)/shard_map/ppermute | solution.py:31
  94.0 13.1 %collective-permute-start.38 = (bf16[256,512]{1,0:T(8,128)(2,1)S(1)}, bf16[256,512]{1,0:T(8,128)(2,1)S(1)}, u32[]{:S(2)}, u32[]{:S(2)}) collective-permute-start(bf16[256,512]{1,0:T(8,128)(2,1)S(1)} %get-tuple-element.115), channel_id=1, source_target_pairs={{0,3},{1,2},{2,1},{3,0},{4,7},{5,6},{6,5},{7,4},{8,11},{9,10},{10,... | collective-permute-start | bytes 786440 | tf_op jit(solution)/shard_map/ppermute | solution.py:31
  95.9 15.9 %collective-permute-start.30 = (bf16[80,512]{1,0:T(8,128)(2,1)S(1)}, bf16[80,512]{1,0:T(8,128)(2,1)S(1)}, u32[]{:S(2)}, u32[]{:S(2)}) collective-permute-start(bf16[80,512]{1,0:T(8,128)(2,1)S(1)} %get-tuple-element.103), channel_id=1, source_target_pairs={{0,8},{4,12},{8,0},{12,4},{16,24},{20,28},{24,16},{28,20},{1,9},{5... | collective-permute-start | bytes 245768 | tf_op jit(solution)/shard_map/ppermute | solution.py:31
  96.0 15.9 %collective-permute-start.31 = (bf16[80,512]{1,0:T(8,128)(2,1)S(1)}, bf16[80,512]{1,0:T(8,128)(2,1)S(1)}, u32[]{:S(2)}, u32[]{:S(2)}) collective-permute-start(bf16[80,512]{1,0:T(8,128)(2,1)S(1)} %get-tuple-element.104), channel_id=1, source_target_pairs={{0,16},{4,20},{8,24},{12,28},{16,0},{20,4},{24,8},{28,12},{1,17},{... | collective-permute-start | bytes 245768 | tf_op jit(solution)/shard_map/ppermute | solution.py:31
  101.5 10.4 %collective-permute-start.32 = (bf16[80,512]{1,0:T(8,128)(2,1)S(1)}, bf16[80,512]{1,0:T(8,128)(2,1)S(1)}, u32[]{:S(2)}, u32[]{:S(2)}) collective-permute-start(bf16[80,512]{1,0:T(8,128)(2,1)S(1)} %get-tuple-element.105), channel_id=1, source_target_pairs={{0,24},{4,28},{8,16},{12,20},{16,8},{20,12},{24,0},{28,4},{1,25},{... | collective-permute-start | bytes 245768 | tf_op jit(solution)/shard_map/ppermute | solution.py:31
  107.4 4.5 %collective-permute-start.39 = (bf16[64,512]{1,0:T(8,128)(2,1)S(1)}, bf16[64,512]{1,0:T(8,128)(2,1)S(1)}, u32[]{:S(2)}, u32[]{:S(2)}) collective-permute-start(bf16[64,512]{1,0:T(8,128)(2,1)S(1)} %get-tuple-element.117), channel_id=1, source_target_pairs={{0,8},{4,12},{8,0},{12,4},{16,24},{20,28},{24,16},{28,20},{1,9},{5... | collective-permute-start | bytes 196616 | tf_op jit(solution)/shard_map/ppermute | solution.py:31
  107.5 8.8 %collective-permute-start.40 = (bf16[64,512]{1,0:T(8,128)(2,1)S(1)}, bf16[64,512]{1,0:T(8,128)(2,1)S(1)}, u32[]{:S(2)}, u32[]{:S(2)}) collective-permute-start(bf16[64,512]{1,0:T(8,128)(2,1)S(1)} %get-tuple-element.118), channel_id=1, source_target_pairs={{0,16},{4,20},{8,24},{12,28},{16,0},{20,4},{24,8},{28,12},{1,17},{... | collective-permute-start | bytes 196616 | tf_op jit(solution)/shard_map/ppermute | solution.py:31
  111.8 6.1 %collective-permute-start.41 = (bf16[64,512]{1,0:T(8,128)(2,1)S(1)}, bf16[64,512]{1,0:T(8,128)(2,1)S(1)}, u32[]{:S(2)}, u32[]{:S(2)}) collective-permute-start(bf16[64,512]{1,0:T(8,128)(2,1)S(1)} %get-tuple-element.119), channel_id=1, source_target_pairs={{0,24},{4,28},{8,16},{12,20},{16,8},{20,12},{24,0},{28,4},{1,25},{... | collective-permute-start | bytes 196616 | tf_op jit(solution)/shard_map/ppermute | solution.py:31
  118.0 10.2 %collective-permute-start.44 = (bf16[112,512]{1,0:T(8,128)(2,1)S(1)}, bf16[112,512]{1,0:T(8,128)(2,1)S(1)}, u32[]{:S(2)}, u32[]{:S(2)}) collective-permute-start(bf16[112,512]{1,0:T(8,128)(2,1)S(1)} %shard_map.197.refs_0_), channel_id=1, source_target_pairs={{0,24},{4,28},{8,16},{12,20},{16,8},{20,12},{24,0},{28,4},{1,25},{... | collective-permute-start | bytes 344072 | tf_op jit(solution)/shard_map/ppermute | solution.py:31
  119.5 9.3 %collective-permute-start.43 = (bf16[112,512]{1,0:T(8,128)(2,1)S(1)}, bf16[112,512]{1,0:T(8,128)(2,1)S(1)}, u32[]{:S(2)}, u32[]{:S(2)}) collective-permute-start(bf16[112,512]{1,0:T(8,128)(2,1)S(1)} %shard_map.197.refs_0_), channel_id=1, source_target_pairs={{0,16},{4,20},{8,24},{12,28},{16,0},{20,4},{24,8},{28,12},{1,17},{... | collective-permute-start | bytes 344072 | tf_op jit(solution)/shard_map/ppermute | solution.py:31
  119.5 9.3 %collective-permute-start.42 = (bf16[112,512]{1,0:T(8,128)(2,1)S(1)}, bf16[112,512]{1,0:T(8,128)(2,1)S(1)}, u32[]{:S(2)}, u32[]{:S(2)}) collective-permute-start(bf16[112,512]{1,0:T(8,128)(2,1)S(1)} %shard_map.197.refs_0_), channel_id=1, source_target_pairs={{0,8},{4,12},{8,0},{12,4},{16,24},{20,28},{24,16},{28,20},{1,9},{5... | collective-permute-start | bytes 344072 | tf_op jit(solution)/shard_map/ppermute | solution.py:31
  123.4 4.7 %collective-permute-start.33 = (bf16[96,512]{1,0:T(8,128)(2,1)S(1)}, bf16[96,512]{1,0:T(8,128)(2,1)S(1)}, u32[]{:S(2)}, u32[]{:S(2)}) collective-permute-start(bf16[96,512]{1,0:T(8,128)(2,1)S(1)} %get-tuple-element.107), channel_id=1, source_target_pairs={{0,1},{1,0},{2,3},{3,2},{4,5},{5,4},{6,7},{7,6},{8,9},{9,8},{10,11... | collective-permute-start | bytes 294920 | tf_op jit(solution)/shard_map/ppermute | solution.py:31
  124.8 4.6 %collective-permute-start.34 = (bf16[96,512]{1,0:T(8,128)(2,1)S(1)}, bf16[96,512]{1,0:T(8,128)(2,1)S(1)}, u32[]{:S(2)}, u32[]{:S(2)}) collective-permute-start(bf16[96,512]{1,0:T(8,128)(2,1)S(1)} %get-tuple-element.108), channel_id=1, source_target_pairs={{0,2},{1,3},{2,0},{3,1},{4,6},{5,7},{6,4},{7,5},{8,10},{9,11},{10,... | collective-permute-start | bytes 294920 | tf_op jit(solution)/shard_map/ppermute | solution.py:31
  128.1 7.7 %collective-permute-start.45 = (bf16[112,512]{1,0:T(8,128)(2,1)S(1)}, bf16[112,512]{1,0:T(8,128)(2,1)S(1)}, u32[]{:S(2)}, u32[]{:S(2)}) collective-permute-start(bf16[112,512]{1,0:T(8,128)(2,1)S(1)} %shard_map.197.refs_0_), channel_id=1, source_target_pairs={{0,4},{4,0},{8,12},{12,8},{16,20},{20,16},{24,28},{28,24},{1,5},{5... | collective-permute-start | bytes 344072 | tf_op jit(solution)/shard_map/ppermute | solution.py:31
  128.1 7.7 %collective-permute-start.48 = (bf16[112,512]{1,0:T(8,128)(2,1)S(1)}, bf16[112,512]{1,0:T(8,128)(2,1)S(1)}, u32[]{:S(2)}, u32[]{:S(2)}) collective-permute-start(bf16[112,512]{1,0:T(8,128)(2,1)S(1)} %collective-permute-done.44.refs_3_), channel_id=1, source_target_pairs={{0,4},{4,0},{8,12},{12,8},{16,20},{20,16},{24,28},{28,24},{1,5},{5... | collective-permute-start | bytes 344072 | tf_op jit(solution)/shard_map/ppermute | solution.py:31
  128.8 6.9 %collective-permute-start.47 = (bf16[112,512]{1,0:T(8,128)(2,1)S(1)}, bf16[112,512]{1,0:T(8,128)(2,1)S(1)}, u32[]{:S(2)}, u32[]{:S(2)}) collective-permute-start(bf16[112,512]{1,0:T(8,128)(2,1)S(1)} %collective-permute-done.43.refs_2_), channel_id=1, source_target_pairs={{0,4},{4,0},{8,12},{12,8},{16,20},{20,16},{24,28},{28,24},{1,5},{5... | collective-permute-start | bytes 344072 | tf_op jit(solution)/shard_map/ppermute | solution.py:31
  128.9 6.9 %collective-permute-start.46 = (bf16[112,512]{1,0:T(8,128)(2,1)S(1)}, bf16[112,512]{1,0:T(8,128)(2,1)S(1)}, u32[]{:S(2)}, u32[]{:S(2)}) collective-permute-start(bf16[112,512]{1,0:T(8,128)(2,1)S(1)} %collective-permute-done.42.refs_1_), channel_id=1, source_target_pairs={{0,4},{4,0},{8,12},{12,8},{16,20},{20,16},{24,28},{28,24},{1,5},{5... | collective-permute-start | bytes 344072 | tf_op jit(solution)/shard_map/ppermute | solution.py:31
  129.4 5.6 %collective-permute-start.35 = (bf16[96,512]{1,0:T(8,128)(2,1)S(1)}, bf16[96,512]{1,0:T(8,128)(2,1)S(1)}, u32[]{:S(2)}, u32[]{:S(2)}) collective-permute-start(bf16[96,512]{1,0:T(8,128)(2,1)S(1)} %get-tuple-element.109), channel_id=1, source_target_pairs={{0,3},{1,2},{2,1},{3,0},{4,7},{5,6},{6,5},{7,4},{8,11},{9,10},{10,... | collective-permute-start | bytes 294920 | tf_op jit(solution)/shard_map/ppermute | solution.py:31
  (11 other events, 301.5 us)

commit v4 on v3

--- a/solution.py
+++ b/solution.py
@@ -288,8 +288,8 @@
     parts, refs = refs[:n], refs[n:]
     pieces = [(refs[2 * b], refs[2 * b + 1]) for b in range(n - 1)]
     refs = refs[2 * (n - 1) :]
-    new, pooled_grad, base = refs[:3]
-    messages, w = refs[3 : 3 + n], refs[3 + n]
+    new, pre_grad_ref, base, w_pooled = refs[:4]
+    messages, w = refs[4 : 4 + n], refs[4 + n]
     here = lax.axis_index("feat")
     parity = lax.axis_index("region") % 2
     gain = gains[1:2, :]
@@ -303,25 +303,26 @@
     cot = cot_ref[...].astype(F32)
     mix_grad = layer_norm_back(cot * gain, normed, inverse)
     pre_grad = (dot_t(mix_grad, w[2]) * slope).astype(BF16)
-    pooled_grad[...] = dot_t(pre_grad, w[1]).astype(BF16)
+    pre_grad_ref[...] = pre_grad
+    w_pooled[...] = w[1]
     base[...] = cot + dot_t(pre_grad, w[0])
     d = lat.shape[1]
     portion = d // n
     for b in range(n):
-        messages[b][:, :d] = pre_grad
-        messages[b][:, d : 2 * d] = mix_grad
+        messages[b][:, :d] = mix_grad
     for f in range(n):
 
         @pl.when(here == f)
         def _():
             for b in range(n):
                 block = slice((f ^ b) * portion, ((f ^ b) + 1) * portion)
-                messages[b][:, 2 * d : 2 * d + portion] = pooled[:, block]
-                messages[b][:, 2 * d + portion :] = hidden[:, block]
+                messages[b][:, d : d + portion] = pooled[:, block]
+                messages[b][:, d + portion :] = hidden[:, block]
 
 
 def node_weight_kernel(n, *refs):
-    near, messages, (keep, send, lat, grads) = refs[:n], refs[n : 2 * n], refs[2 * n :]
+    near, pre_grads, messages = refs[:n], refs[n : 2 * n], refs[2 * n : 3 * n]
+    keep, send, lat, grads = refs[3 * n :]
     here = lax.axis_index("feat")
     parity = lax.axis_index("region") % 2
     _, d = near[0].shape
@@ -335,11 +336,11 @@
 
     totals = [jnp.zeros((portion, d), F32)] * 3
     for b in range(n):
-        pre_grad = messages[b][:, :d]
-        mix_grad = messages[b][:, d : 2 * d]
+        pre_grad = pre_grads[b][...]
+        mix_grad = messages[b][:, :d]
         totals[0] = totals[0] + t_dot(lat[b], pre_grad)
-        totals[1] = totals[1] + t_dot(messages[b][:, 2 * d : 2 * d + portion], pre_grad)
-        totals[2] = totals[2] + t_dot(messages[b][:, 2 * d + portion :], mix_grad)
+        totals[1] = totals[1] + t_dot(messages[b][:, d : d + portion], pre_grad)
+        totals[2] = totals[2] + t_dot(messages[b][:, d + portion :], mix_grad)
     for k in range(3):
         grads[k * portion : (k + 1) * portion, :] = totals[k]
     half = keep.shape[0]
@@ -349,7 +350,7 @@
 
 def edge_backward_kernel(n, slots, *refs):
     edge, cot, hidden, slope, normed, inverse, r_at, s_row, r_row, gains, table, w = refs[:12]
-    near, refs = refs[12 : 12 + n], refs[12 + n :]
+    w_pooled, near, refs = refs[12], refs[13 : 13 + n], refs[13 + n :]
     pre_grad_ref, keep, send, sent_ref, received_ref, near_all = refs[:6]
     grads, sent, received = refs[6:]
     here = lax.axis_index("feat")
@@ -361,6 +362,7 @@
     def _():
         for b in range(n):
             near_all[b * own : (b + 1) * own, :] = near[b][...]
+        near_all[...] = dot_t(near_all[...], w_pooled[...]).astype(BF16)
 
     total = cot[...].astype(F32) + dot(hot(r_at[...], nodes), near_all[...])
     mix_grad = layer_norm_back(total * gains[0:1, :], normed[...].astype(F32), inverse[:, :1])
@@ -458,9 +460,9 @@
         for side, ref in ((parity, mine[b]), (1 - parity, theirs[b])):
             base = side * pairs * rows
             start = pl.multiple_of(base + (z ^ b) * cut, 16)
-            total[pl.ds(start, cut), :] = ref[:cut, :].astype(F32)
+            total[pl.ds(start, cut), :] = ref[:cut, :]
             start = pl.multiple_of(base + pairs * cut + (z ^ b) * (rows - cut), 16)
-            total[pl.ds(start, rows - cut), :] = ref[cut:, :].astype(F32)
+            total[pl.ds(start, rows - cut), :] = ref[cut:, :]
     spread(total, outs, edge_norm, node_norm)
 
 
@@ -473,7 +475,7 @@
             row = u * (portion // 2)
             source = (row // half) * size + at + row % half
             out, start = (pair[0], row) if u < 2 * m - 2 else (pair[1], row - (m - 1) * portion)
-            out[start : start + portion // 2, :] = total[source : source + portion // 2, :] * norm
+            out[start : start + portion // 2, :] = total[source : source + portion // 2, :].astype(F32) * norm
 
 
 def gather_halves(mine):
@@ -536,7 +538,7 @@
             functools.partial(finish_kernel, pairs, cut, edge_norm, node_norm),
             mine + theirs,
             outs,
-            [pltpu.VMEM((2 * size, d), F32)],
+            [pltpu.VMEM((2 * size, d), BF16)],
         )
         return grads, returned
     order = jnp.arange(pairs) ^ z
@@ -641,19 +643,19 @@
     )(*ins, *rest)
 
     parts = feat_swaps(pooled_parts)
-    node_new, pooled_grad, node_base, *messages = call(
+    node_new, node_pre_grad, node_base, w_pooled, *messages = call(
         functools.partial(node_kernel, n),
         [node_lat, node_cot, gains, w_node_in, w_node_out, *parts, *w_node],
-        [shape((own, d)), shape((own, d)), shape((own, d), F32)]
-        + [shape((own, 2 * d + 2 * portion))] * n,
+        [shape((own, d)), shape((own, d)), shape((own, d), F32), shape((d, d))]
+        + [shape((own, d + 2 * portion))] * n,
         [pltpu.VMEM((3, d, d), BF16)],
         flops=6 * own * square,
     )
-    grad_near = feat_swaps([pooled_grad] * n)
+    grad_near = feat_swaps([node_pre_grad] * n)
     messages = feat_swaps(messages)
 
     ins = [edge_lat, edge_cot, hidden, slope, normed, inverse, receiver_column, sender_at[None], receiver_line]
-    rest = [gains, table, w_full, *grad_near]
+    rest = [gains, table, w_full, w_pooled, *grad_near]
     kept = [shape((n * 2 * portion + pairs * slots, d))] * 2
     kept += [shape((table_size, d)), shape((nodes, d)), shape((nodes, d))]
     edge_pre_grad, keep, send, sent, received, near_grad = pl.pallas_call(
@@ -677,7 +679,7 @@
     got = swap(send, "region", 1)
     node_keep, node_send = call(
         functools.partial(node_weight_kernel, n),
-        [*near, *messages],
+        [*near, *grad_near, *messages],
         [shape((3 * half, d))] * 2,
         [pltpu.VMEM((n, own, portion), BF16), pltpu.VMEM((3 * portion, d), F32)],
         flops=3 * nodes * square // n,

time: 137 us -> 133 us (0.971)
  waiting for transfers between devices: 55.6 us -> 51.4 us
    ppermute x49, waiting for transfers between devices: 55.6 us -> 51.4 us  [swap(): return lax.ppermute(x, axis, [(i, i ^ bits) for i in range(n)])]
where the time goes in v4:
time: 133 us
  starting transfers between devices  58.2 us (44%)
  waiting for transfers between devices  51.4 us (39%)
  Pallas kernels  21.3 us (16%)
    ppermute x49, starting transfers between devices, swap(): return lax.ppermute(x, axis, [(i, i ^ bits) for i in range(n)])  58.2 us
    ppermute x49, waiting for transfers between devices, swap(): return lax.ppermute(x, axis, [(i, i ^ bits) for i in range(n)])  51.4 us
    pallas_call x11, Pallas kernels, call(): pl.pallas_call(kernel, out_shape=tuple(outs), grid=(1,), in_specs=[whole_...  6.95 us
    pallas_call x1, Pallas kernels, layer(): pl.pallas_call(functools.partial(edge_forward_kernel, n, pairs), out_shap...  5.57 us
    pallas_call x1, Pallas kernels, layer(): pl.pallas_call(functools.partial(edge_backward_kernel, n, slots), out_sha...  4.56 us
  transfers between devices with their start and end apart: 49, of which 24 were waited for; matrix products, arithmetic and copies ran while one was open for 1% of the time, Pallas kernels for 10%

profile of v4, /device:TPU:0, one launch (start us, length us, event | category | flops | bytes accessed | tf_op | source)
XLA Modules:
  0.0 133.0 jit_solution(14119517203486279156)
XLA Ops:
  0.6 3.1 %collective-permute-start.1 = (bf16[96,512]{1,0:T(8,128)(2,1)}, bf16[96,512]{1,0:T(8,128)(2,1)S(1)}, u32[]{:S(2)}, u32[]{:S(2)}) collective-permute-start(bf16[96,512]{1,0:T(8,128)(2,1)} %lat_ref.1), channel_id=1, source_target_pairs={{0,2},{1,3},{2,0},{3,1},{4,6},{5,7},{6,4},{7,5},{8,10},{9,11},{10,... | collective-permute-start | bytes 294920 | tf_op jit(solution)/shard_map/ppermute | solution.py:31
  3.7 2.0 %prepare.1 = (bf16[272,512]{1,0:T(8,128)(2,1)S(1)}, bf16[192,512]{1,0:T(8,128)(2,1)}, bf16[96,512]{1,0:T(8,128)(2,1)S(1)}, s32[8,16]{1,0:T(8,128)S(1)}) custom-call(bf16[3,128,512]{2,1,0:T(8,128)(2,1)} %refs_6_.1, bf16[128,512]{1,0:T(8,128)(2,1)} %refs_7_.1, bf16[2,128,512]{2,1,0:T(8,128)(2,1)} %own_in.1, bf16[128,512]{1,0:T(8,128)(2,1)} %own_out.1, ...), custom_call_target="tpu_custom_call" | custom-call | flops 262144 | bytes 1048576 | tf_op jit(solution)/shard_map/prepare/pallas_call | solution.py:190
  5.7 1.5 %collective-permute-start.11 = (bf16[272,512]{1,0:T(8,128)(2,1)S(1)}, bf16[272,512]{1,0:T(8,128)(2,1)S(1)}, u32[]{:S(2)}, u32[]{:S(2)}) collective-permute-start(bf16[272,512]{1,0:T(8,128)(2,1)S(1)} %get-tuple-element.75), channel_id=1, source_target_pairs={{0,3},{1,2},{2,1},{3,0},{4,7},{5,6},{6,5},{7,4},{8,11},{9,10},{10,... | collective-permute-start | bytes 835592 | tf_op jit(solution)/shard_map/ppermute | solution.py:31
  7.2 1.5 %collective-permute-start.9 = (bf16[272,512]{1,0:T(8,128)(2,1)S(1)}, bf16[272,512]{1,0:T(8,128)(2,1)S(1)}, u32[]{:S(2)}, u32[]{:S(2)}) collective-permute-start(bf16[272,512]{1,0:T(8,128)(2,1)S(1)} %get-tuple-element.75), channel_id=1, source_target_pairs={{0,2},{1,3},{2,0},{3,1},{4,6},{5,7},{6,4},{7,5},{8,10},{9,11},{10,... | collective-permute-start | bytes 835592 | tf_op jit(solution)/shard_map/ppermute | solution.py:31
  9.3 1.5 %collective-permute-start = (bf16[96,512]{1,0:T(8,128)(2,1)}, bf16[96,512]{1,0:T(8,128)(2,1)S(1)}, u32[]{:S(2)}, u32[]{:S(2)}) collective-permute-start(bf16[96,512]{1,0:T(8,128)(2,1)} %lat_ref.1), channel_id=1, source_target_pairs={{0,1},{1,0},{2,3},{3,2},{4,5},{5,4},{6,7},{7,6},{8,9},{9,8},{10,11... | collective-permute-start | bytes 294920 | tf_op jit(solution)/shard_map/ppermute | solution.py:31
  10.9 12.0 %collective-permute-done.refs_1_.refs_9_ = bf16[96,512]{1,0:T(8,128)(2,1)S(1)} collective-permute-done((bf16[96,512]{1,0:T(8,128)(2,1)}, bf16[96,512]{1,0:T(8,128)(2,1)S(1)}, u32[]{:S(2)}, u32[]{:S(2)}) %collective-permute-start) | collective-permute-done | bytes 98336 | tf_op jit(solution)/shard_map/ppermute | solution.py:31
  22.9 2.6 %collective-permute-start.20 = (bf16[192,512]{1,0:T(8,128)(2,1)}, bf16[192,512]{1,0:T(8,128)(2,1)S(1)}, u32[]{:S(2)}, u32[]{:S(2)}) collective-permute-start(bf16[192,512]{1,0:T(8,128)(2,1)} %get-tuple-element.81), channel_id=1, source_target_pairs={{0,3},{1,2},{2,1},{3,0},{4,7},{5,6},{6,5},{7,4},{8,11},{9,10},{10,... | collective-permute-start | bytes 589832 | tf_op jit(solution)/shard_map/ppermute | solution.py:31
  26.1 1.2 collective-permute-done.3.other
  27.4 1.7 %collective-permute-start.4 = (bf16[32,512]{1,0:T(8,128)(2,1)S(1)}, bf16[32,512]{1,0:T(8,128)(2,1)S(1)}, u32[]{:S(2)}, u32[]{:S(2)}) collective-permute-start(bf16[32,512]{1,0:T(8,128)(2,1)S(1)} %get-tuple-element.72), channel_id=1, source_target_pairs={{0,8},{4,12},{8,0},{12,4},{16,24},{20,28},{24,16},{28,20},{1,9},{5... | collective-permute-start | bytes 98312 | tf_op jit(solution)/shard_map/ppermute | solution.py:31
  29.7 1.6 %collective-permute-done.4.refs_13_ = bf16[32,512]{1,0:T(8,128)(2,1)S(1)} collective-permute-done((bf16[32,512]{1,0:T(8,128)(2,1)S(1)}, bf16[32,512]{1,0:T(8,128)(2,1)S(1)}, u32[]{:S(2)}, u32[]{:S(2)}) %collective-permute-start.4) | collective-permute-done | bytes 32800 | tf_op jit(solution)/shard_map/ppermute | solution.py:31
  31.4 2.7 %collective-permute-start.5 = (bf16[32,512]{1,0:T(8,128)(2,1)S(1)}, bf16[32,512]{1,0:T(8,128)(2,1)S(1)}, u32[]{:S(2)}, u32[]{:S(2)}) collective-permute-start(bf16[32,512]{1,0:T(8,128)(2,1)S(1)} %get-tuple-element.73), channel_id=1, source_target_pairs={{0,16},{4,20},{8,24},{12,28},{16,0},{20,4},{24,8},{28,12},{1,17},{... | collective-permute-start | bytes 98312 | tf_op jit(solution)/shard_map/ppermute | solution.py:31
  34.0 2.1 %collective-permute-done.5.refs_14_ = bf16[32,512]{1,0:T(8,128)(2,1)S(1)} collective-permute-done((bf16[32,512]{1,0:T(8,128)(2,1)S(1)}, bf16[32,512]{1,0:T(8,128)(2,1)S(1)}, u32[]{:S(2)}, u32[]{:S(2)}) %collective-permute-start.5) | collective-permute-done | bytes 32800 | tf_op jit(solution)/shard_map/ppermute | solution.py:31
  36.2 3.9 %collective-permute-start.6 = (bf16[32,512]{1,0:T(8,128)(2,1)S(1)}, bf16[32,512]{1,0:T(8,128)(2,1)S(1)}, u32[]{:S(2)}, u32[]{:S(2)}) collective-permute-start(bf16[32,512]{1,0:T(8,128)(2,1)S(1)} %get-tuple-element.74), channel_id=1, source_target_pairs={{0,24},{4,28},{8,16},{12,20},{16,8},{20,12},{24,0},{28,4},{1,25},{... | collective-permute-start | bytes 98312 | tf_op jit(solution)/shard_map/ppermute | solution.py:31
  40.1 1.9 %collective-permute-done.6.refs_15_ = bf16[32,512]{1,0:T(8,128)(2,1)S(1)} collective-permute-done((bf16[32,512]{1,0:T(8,128)(2,1)S(1)}, bf16[32,512]{1,0:T(8,128)(2,1)S(1)}, u32[]{:S(2)}, u32[]{:S(2)}) %collective-permute-start.6) | collective-permute-done | bytes 32800 | tf_op jit(solution)/shard_map/ppermute | solution.py:31
  42.3 1.2 collective-permute-start.16
  44.6 3.2 %collective-permute-done.18.refs_6_ = bf16[192,512]{1,0:T(8,128)(2,1)S(1)} collective-permute-done((bf16[192,512]{1,0:T(8,128)(2,1)}, bf16[192,512]{1,0:T(8,128)(2,1)S(1)}, u32[]{:S(2)}, u32[]{:S(2)}) %collective-permute-start.18) | collective-permute-done | bytes 196640 | tf_op jit(solution)/shard_map/ppermute | solution.py:31
  48.8 5.6 %edge_forward.1 = (bf16[768,512]{1,0:T(8,128)(2,1)}, bf16[768,512]{1,0:T(8,128)(2,1)S(1)}, bf16[768,512]{1,0:T(8,128)(2,1)S(1)}, bf16[768,512]{1,0:T(8,128)(2,1)...) custom-call(bf16[768,512]{1,0:T(8,128)(2,1)S(1)} %copy-done.9, ...), custom_call_target="tpu_custom_call" | custom-call | flops 2818572288 | bytes 3145728 | tf_op jit(solution)/shard_map/edge_forward/pallas_call | solution.py:630
  54.4 1.3 collective-permute-start.13
  55.6 2.0 %collective-permute-start.14 = (bf16[96,512]{1,0:T(8,128)(2,1)S(1)}, bf16[96,512]{1,0:T(8,128)(2,1)S(1)}, u32[]{:S(2)}, u32[]{:S(2)}) collective-permute-start(bf16[96,512]{1,0:T(8,128)(2,1)S(1)} %get-tuple-element.79), channel_id=1, source_target_pairs={{0,2},{1,3},{2,0},{3,1},{4,6},{5,7},{6,4},{7,5},{8,10},{9,11},{10,... | collective-permute-start | bytes 294920 | tf_op jit(solution)/shard_map/ppermute | solution.py:31
  57.9 1.4 %collective-permute-done.13.refs_1_ = bf16[96,512]{1,0:T(8,128)(2,1)S(1)} collective-permute-done((bf16[96,512]{1,0:T(8,128)(2,1)S(1)}, bf16[96,512]{1,0:T(8,128)(2,1)S(1)}, u32[]{:S(2)}, u32[]{:S(2)}) %collective-permute-start.13) | collective-permute-done | bytes 98336 | tf_op jit(solution)/shard_map/ppermute | solution.py:31
  59.3 2.4 %collective-permute-done.14.refs_2_ = bf16[96,512]{1,0:T(8,128)(2,1)S(1)} collective-permute-done((bf16[96,512]{1,0:T(8,128)(2,1)S(1)}, bf16[96,512]{1,0:T(8,128)(2,1)S(1)}, u32[]{:S(2)}, u32[]{:S(2)}) %collective-permute-start.14) | collective-permute-done | bytes 98336 | tf_op jit(solution)/shard_map/ppermute | solution.py:31
  61.7 1.4 %collective-permute-done.15.refs_3_ = bf16[96,512]{1,0:T(8,128)(2,1)S(1)} collective-permute-done((bf16[96,512]{1,0:T(8,128)(2,1)S(1)}, bf16[96,512]{1,0:T(8,128)(2,1)S(1)}, u32[]{:S(2)}, u32[]{:S(2)}) %collective-permute-start.15) | collective-permute-done | bytes 98336 | tf_op jit(solution)/shard_map/ppermute | solution.py:31
  63.1 1.9 %shard_map.190 = (bf16[96,512]{1,0:T(8,128)(2,1)}, bf16[96,512]{1,0:T(8,128)(2,1)S(1)}, f32[96,512]{1,0:T(8,128)S(1)}, bf16[512,512]{1,0:T(8,128)(2,1)S(1)}, bf1...) custom-call(bf16[96,512]{1,0:T(8,128)(2,1)S(1)} %copy-done.3, ...), custom_call_target="tpu_custom_call" | custom-call | flops 301989888 | bytes 3686400 | tf_op jit(solution)/shard_map/pallas_call | solution.py:107
  65.1 1.2 collective-permute-start.24
  67.3 1.3 collective-permute-start.22
  68.6 2.3 %collective-permute-done.24.refs_16_.refs_7_ = bf16[96,512]{1,0:T(8,128)(2,1)S(1)} collective-permute-done((bf16[96,512]{1,0:T(8,128)(2,1)S(1)}, bf16[96,512]{1,0:T(8,128)(2,1)S(1)}, u32[]{:S(2)}, u32[]{:S(2)}) %collective-permute-start.24) | collective-permute-done | bytes 98336 | tf_op jit(solution)/shard_map/ppermute | solution.py:31
  71.9 4.6 %edge_backward.1 = (bf16[768,512]{1,0:T(8,128)(2,1)S(1)}, bf16[1088,512]{1,0:T(8,128)(2,1)S(1)}, bf16[1088,512]{1,0:T(8,128)(2,1)S(1)}, bf16[512,512]{1,0:T(8,12...) custom-call(bf16[768,512]{1,0:T(8,128)(2,1)S(1)} %copy-done.9, bf16[768,512]{1,0:T(8,128)(2,1)S(1)} %copy-done.1, ...), custom_call_target="tpu_custom_call" | custom-call | flops 4026531840 | bytes 6291456 | tf_op jit(solution)/shard_map/edge_backward/pallas_call | solution.py:661
  76.5 1.4 %collective-permute-start.26 = (bf16[96,768]{1,0:T(8,128)(2,1)S(1)}, bf16[96,768]{1,0:T(8,128)(2,1)S(1)}, u32[]{:S(2)}, u32[]{:S(2)}) collective-permute-start(bf16[96,768]{1,0:T(8,128)(2,1)S(1)} %get-tuple-element.99), channel_id=1, source_target_pairs={{0,1},{1,0},{2,3},{3,2},{4,5},{5,4},{6,7},{7,6},{8,9},{9,8},{10,11... | collective-permute-start | bytes 442376 | tf_op jit(solution)/shard_map/ppermute | solution.py:31
  77.9 1.1 collective-permute-start.27
  79.0 1.1 collective-permute-start.28
  80.1 3.2 %collective-permute-done.26.refs_9_ = bf16[96,768]{1,0:T(8,128)(2,1)S(1)} collective-permute-done((bf16[96,768]{1,0:T(8,128)(2,1)S(1)}, bf16[96,768]{1,0:T(8,128)(2,1)S(1)}, u32[]{:S(2)}, u32[]{:S(2)}) %collective-permute-start.26) | collective-permute-done | bytes 147488 | tf_op jit(solution)/shard_map/ppermute | solution.py:31
  83.3 3.6 %collective-permute-done.27.refs_10_ = bf16[96,768]{1,0:T(8,128)(2,1)S(1)} collective-permute-done((bf16[96,768]{1,0:T(8,128)(2,1)S(1)}, bf16[96,768]{1,0:T(8,128)(2,1)S(1)}, u32[]{:S(2)}, u32[]{:S(2)}) %collective-permute-start.27) | collective-permute-done | bytes 147488 | tf_op jit(solution)/shard_map/ppermute | solution.py:31
  90.0 1.8 %collective-permute-start.38 = (bf16[256,512]{1,0:T(8,128)(2,1)S(1)}, bf16[256,512]{1,0:T(8,128)(2,1)S(1)}, u32[]{:S(2)}, u32[]{:S(2)}) collective-permute-start(bf16[256,512]{1,0:T(8,128)(2,1)S(1)} %get-tuple-element.117), channel_id=1, source_target_pairs={{0,3},{1,2},{2,1},{3,0},{4,7},{5,6},{6,5},{7,4},{8,11},{9,10},{10,... | collective-permute-start | bytes 786440 | tf_op jit(solution)/shard_map/ppermute | solution.py:31
  92.0 4.4 %collective-permute-start.31 = (bf16[80,512]{1,0:T(8,128)(2,1)S(1)}, bf16[80,512]{1,0:T(8,128)(2,1)S(1)}, u32[]{:S(2)}, u32[]{:S(2)}) collective-permute-start(bf16[80,512]{1,0:T(8,128)(2,1)S(1)} %get-tuple-element.106), channel_id=1, source_target_pairs={{0,16},{4,20},{8,24},{12,28},{16,0},{20,4},{24,8},{28,12},{1,17},{... | collective-permute-start | bytes 245768 | tf_op jit(solution)/shard_map/ppermute | solution.py:31
  96.3 1.1 collective-permute-done.36.refs_1_
  97.4 3.8 %collective-permute-start.32 = (bf16[80,512]{1,0:T(8,128)(2,1)S(1)}, bf16[80,512]{1,0:T(8,128)(2,1)S(1)}, u32[]{:S(2)}, u32[]{:S(2)}) collective-permute-start(bf16[80,512]{1,0:T(8,128)(2,1)S(1)} %get-tuple-element.107), channel_id=1, source_target_pairs={{0,24},{4,28},{8,16},{12,20},{16,8},{20,12},{24,0},{28,4},{1,25},{... | collective-permute-start | bytes 245768 | tf_op jit(solution)/shard_map/ppermute | solution.py:31
  101.3 1.9 %collective-permute-done.38.refs_3_ = bf16[256,512]{1,0:T(8,128)(2,1)S(1)} collective-permute-done((bf16[256,512]{1,0:T(8,128)(2,1)S(1)}, bf16[256,512]{1,0:T(8,128)(2,1)S(1)}, u32[]{:S(2)}, u32[]{:S(2)}) %collective-permute-start.38) | collective-permute-done | bytes 262176 | tf_op jit(solution)/shard_map/ppermute | solution.py:31
  103.4 4.3 %collective-permute-start.40 = (bf16[64,512]{1,0:T(8,128)(2,1)S(1)}, bf16[64,512]{1,0:T(8,128)(2,1)S(1)}, u32[]{:S(2)}, u32[]{:S(2)}) collective-permute-start(bf16[64,512]{1,0:T(8,128)(2,1)S(1)} %get-tuple-element.120), channel_id=1, source_target_pairs={{0,16},{4,20},{8,24},{12,28},{16,0},{20,4},{24,8},{28,12},{1,17},{... | collective-permute-start | bytes 196616 | tf_op jit(solution)/shard_map/ppermute | solution.py:31
  107.8 4.4 %collective-permute-done.40.refs_2_ = bf16[64,512]{1,0:T(8,128)(2,1)S(1)} collective-permute-done((bf16[64,512]{1,0:T(8,128)(2,1)S(1)}, bf16[64,512]{1,0:T(8,128)(2,1)S(1)}, u32[]{:S(2)}, u32[]{:S(2)}) %collective-permute-start.40) | collective-permute-done | bytes 65568 | tf_op jit(solution)/shard_map/ppermute | solution.py:31
  112.2 1.7 %collective-permute-done.41.refs_3_ = bf16[64,512]{1,0:T(8,128)(2,1)S(1)} collective-permute-done((bf16[64,512]{1,0:T(8,128)(2,1)S(1)}, bf16[64,512]{1,0:T(8,128)(2,1)S(1)}, u32[]{:S(2)}, u32[]{:S(2)}) %collective-permute-start.41) | collective-permute-done | bytes 65568 | tf_op jit(solution)/shard_map/ppermute | solution.py:31
  113.9 1.6 %collective-permute-start.44 = (bf16[112,512]{1,0:T(8,128)(2,1)S(1)}, bf16[112,512]{1,0:T(8,128)(2,1)S(1)}, u32[]{:S(2)}, u32[]{:S(2)}) collective-permute-start(bf16[112,512]{1,0:T(8,128)(2,1)S(1)} %shard_map.197.refs_0_), channel_id=1, source_target_pairs={{0,24},{4,28},{8,16},{12,20},{16,8},{20,12},{24,0},{28,4},{1,25},{... | collective-permute-start | bytes 344072 | tf_op jit(solution)/shard_map/ppermute | solution.py:31
  115.4 2.9 %collective-permute-start.42 = (bf16[112,512]{1,0:T(8,128)(2,1)S(1)}, bf16[112,512]{1,0:T(8,128)(2,1)S(1)}, u32[]{:S(2)}, u32[]{:S(2)}) collective-permute-start(bf16[112,512]{1,0:T(8,128)(2,1)S(1)} %shard_map.197.refs_0_), channel_id=1, source_target_pairs={{0,8},{4,12},{8,0},{12,4},{16,24},{20,28},{24,16},{28,20},{1,9},{5... | collective-permute-start | bytes 344072 | tf_op jit(solution)/shard_map/ppermute | solution.py:31
  119.4 1.4 %collective-permute-start.33 = (bf16[96,512]{1,0:T(8,128)(2,1)S(1)}, bf16[96,512]{1,0:T(8,128)(2,1)S(1)}, u32[]{:S(2)}, u32[]{:S(2)}) collective-permute-start(bf16[96,512]{1,0:T(8,128)(2,1)S(1)} %get-tuple-element.109), channel_id=1, source_target_pairs={{0,1},{1,0},{2,3},{3,2},{4,5},{5,4},{6,7},{7,6},{8,9},{9,8},{10,11... | collective-permute-start | bytes 294920 | tf_op jit(solution)/shard_map/ppermute | solution.py:31
  121.8 2.2 %collective-permute-done.33.refs_2_ = bf16[96,512]{1,0:T(8,128)(2,1)S(1)} collective-permute-done((bf16[96,512]{1,0:T(8,128)(2,1)S(1)}, bf16[96,512]{1,0:T(8,128)(2,1)S(1)}, u32[]{:S(2)}, u32[]{:S(2)}) %collective-permute-start.33) | collective-permute-done | bytes 98336 | tf_op jit(solution)/shard_map/ppermute | solution.py:31
  125.4 1.5 %collective-permute-start.35 = (bf16[96,512]{1,0:T(8,128)(2,1)S(1)}, bf16[96,512]{1,0:T(8,128)(2,1)S(1)}, u32[]{:S(2)}, u32[]{:S(2)}) collective-permute-start(bf16[96,512]{1,0:T(8,128)(2,1)S(1)} %get-tuple-element.111), channel_id=1, source_target_pairs={{0,3},{1,2},{2,1},{3,0},{4,7},{5,6},{6,5},{7,4},{8,11},{9,10},{10,... | collective-permute-start | bytes 294920 | tf_op jit(solution)/shard_map/ppermute | solution.py:31
  126.9 2.2 %edge_grad.1 = f32[768,512]{1,0:T(8,128)} custom-call(bf16[768,512]{1,0:T(8,128)(2,1)S(1)} %copy-done.1, s32[768,1]{1,0:T(8,128)S(1)} %broadcast_in_dim.25.refs_2_.refs_6_.r_at, bf16[384,512]{1,0:T(8,128)(2,1)S(1)} %get-tuple-element.112.near, bf16[768,512]{1,0:T(8,128)(2,1)S(1)} %get-tuple-element.113.pre_grad, ...), custom_call_target="tpu_custom_call" | custom-call | flops 805306368 | bytes 3145728 | tf_op jit(solution)/shard_map/edge_grad/pallas_call | solution.py:701
  129.1 1.9 %collective-permute-done.35.refs_4_ = bf16[96,512]{1,0:T(8,128)(2,1)S(1)} collective-permute-done((bf16[96,512]{1,0:T(8,128)(2,1)S(1)}, bf16[96,512]{1,0:T(8,128)(2,1)S(1)}, u32[]{:S(2)}, u32[]{:S(2)}) %collective-permute-start.35) | collective-permute-done | bytes 98336 | tf_op jit(solution)/shard_map/ppermute | solution.py:31
  131.7 1.3 shard_map.198
  (92 shorter events, 14.2 us)
Async XLA Ops:
  0.6 10.2 %collective-permute-start.1 = (bf16[96,512]{1,0:T(8,128)(2,1)}, bf16[96,512]{1,0:T(8,128)(2,1)S(1)}, u32[]{:S(2)}, u32[]{:S(2)}) collective-permute-start(bf16[96,512]{1,0:T(8,128)(2,1)} %lat_ref.1), channel_id=1, source_target_pairs={{0,2},{1,3},{2,0},{3,1},{4,6},{5,7},{6,4},{7,5},{8,10},{9,11},{10,... | collective-permute-start | bytes 294920 | tf_op jit(solution)/shard_map/ppermute | solution.py:31
  5.7 23.4 %collective-permute-start.11 = (bf16[272,512]{1,0:T(8,128)(2,1)S(1)}, bf16[272,512]{1,0:T(8,128)(2,1)S(1)}, u32[]{:S(2)}, u32[]{:S(2)}) collective-permute-start(bf16[272,512]{1,0:T(8,128)(2,1)S(1)} %get-tuple-element.75), channel_id=1, source_target_pairs={{0,3},{1,2},{2,1},{3,0},{4,7},{5,6},{6,5},{7,4},{8,11},{9,10},{10,... | collective-permute-start | bytes 835592 | tf_op jit(solution)/shard_map/ppermute | solution.py:31
  7.2 21.9 %collective-permute-start.9 = (bf16[272,512]{1,0:T(8,128)(2,1)S(1)}, bf16[272,512]{1,0:T(8,128)(2,1)S(1)}, u32[]{:S(2)}, u32[]{:S(2)}) collective-permute-start(bf16[272,512]{1,0:T(8,128)(2,1)S(1)} %get-tuple-element.75), channel_id=1, source_target_pairs={{0,2},{1,3},{2,0},{3,1},{4,6},{5,7},{6,4},{7,5},{8,10},{9,11},{10,... | collective-permute-start | bytes 835592 | tf_op jit(solution)/shard_map/ppermute | solution.py:31
  8.8 20.9 %collective-permute-start.7 = (bf16[272,512]{1,0:T(8,128)(2,1)S(1)}, bf16[272,512]{1,0:T(8,128)(2,1)S(1)}, u32[]{:S(2)}, u32[]{:S(2)}) collective-permute-start(bf16[272,512]{1,0:T(8,128)(2,1)S(1)} %get-tuple-element.75), channel_id=1, source_target_pairs={{0,1},{1,0},{2,3},{3,2},{4,5},{5,4},{6,7},{7,6},{8,9},{9,8},{10,11... | collective-permute-start | bytes 835592 | tf_op jit(solution)/shard_map/ppermute | solution.py:31
  9.3 13.6 %collective-permute-start = (bf16[96,512]{1,0:T(8,128)(2,1)}, bf16[96,512]{1,0:T(8,128)(2,1)S(1)}, u32[]{:S(2)}, u32[]{:S(2)}) collective-permute-start(bf16[96,512]{1,0:T(8,128)(2,1)} %lat_ref.1), channel_id=1, source_target_pairs={{0,1},{1,0},{2,3},{3,2},{4,5},{5,4},{6,7},{7,6},{8,9},{9,8},{10,11... | collective-permute-start | bytes 294920 | tf_op jit(solution)/shard_map/ppermute | solution.py:31
  10.8 14.8 %collective-permute-start.2 = (bf16[96,512]{1,0:T(8,128)(2,1)}, bf16[96,512]{1,0:T(8,128)(2,1)S(1)}, u32[]{:S(2)}, u32[]{:S(2)}) collective-permute-start(bf16[96,512]{1,0:T(8,128)(2,1)} %lat_ref.1), channel_id=1, source_target_pairs={{0,3},{1,2},{2,1},{3,0},{4,7},{5,6},{6,5},{7,4},{8,11},{9,10},{10,... | collective-permute-start | bytes 294920 | tf_op jit(solution)/shard_map/ppermute | solution.py:31
  22.9 19.4 %collective-permute-start.20 = (bf16[192,512]{1,0:T(8,128)(2,1)}, bf16[192,512]{1,0:T(8,128)(2,1)S(1)}, u32[]{:S(2)}, u32[]{:S(2)}) collective-permute-start(bf16[192,512]{1,0:T(8,128)(2,1)} %get-tuple-element.81), channel_id=1, source_target_pairs={{0,3},{1,2},{2,1},{3,0},{4,7},{5,6},{6,5},{7,4},{8,11},{9,10},{10,... | collective-permute-start | bytes 589832 | tf_op jit(solution)/shard_map/ppermute | solution.py:31
  27.4 4.0 %collective-permute-start.4 = (bf16[32,512]{1,0:T(8,128)(2,1)S(1)}, bf16[32,512]{1,0:T(8,128)(2,1)S(1)}, u32[]{:S(2)}, u32[]{:S(2)}) collective-permute-start(bf16[32,512]{1,0:T(8,128)(2,1)S(1)} %get-tuple-element.72), channel_id=1, source_target_pairs={{0,8},{4,12},{8,0},{12,4},{16,24},{20,28},{24,16},{28,20},{1,9},{5... | collective-permute-start | bytes 98312 | tf_op jit(solution)/shard_map/ppermute | solution.py:31
  29.1 19.3 %collective-permute-start.12 = (bf16[272,512]{1,0:T(8,128)(2,1)S(1)}, bf16[272,512]{1,0:T(8,128)(2,1)S(1)}, u32[]{:S(2)}, u32[]{:S(2)}) collective-permute-start(bf16[272,512]{1,0:T(8,128)(2,1)S(1)} %collective-permute-done.11.refs_20_), channel_id=1, source_target_pairs={{0,4},{4,0},{8,12},{12,8},{16,20},{20,16},{24,28},{28,24},{1,5},{5... | collective-permute-start | bytes 835592 | tf_op jit(solution)/shard_map/ppermute | solution.py:31
  29.1 19.6 %collective-permute-start.10 = (bf16[272,512]{1,0:T(8,128)(2,1)S(1)}, bf16[272,512]{1,0:T(8,128)(2,1)}, u32[]{:S(2)}, u32[]{:S(2)}) collective-permute-start(bf16[272,512]{1,0:T(8,128)(2,1)S(1)} %collective-permute-done.9.refs_18_), channel_id=1, source_target_pairs={{0,4},{4,0},{8,12},{12,8},{16,20},{20,16},{24,28},{28,24},{1,5},{5... | collective-permute-start | bytes 835592 | tf_op jit(solution)/shard_map/ppermute | solution.py:31
  29.6 19.1 %collective-permute-start.8 = (bf16[272,512]{1,0:T(8,128)(2,1)S(1)}, bf16[272,512]{1,0:T(8,128)(2,1)}, u32[]{:S(2)}, u32[]{:S(2)}) collective-permute-start(bf16[272,512]{1,0:T(8,128)(2,1)S(1)} %collective-permute-done.7.refs_16_), channel_id=1, source_target_pairs={{0,4},{4,0},{8,12},{12,8},{16,20},{20,16},{24,28},{28,24},{1,5},{5... | collective-permute-start | bytes 835592 | tf_op jit(solution)/shard_map/ppermute | solution.py:31
  31.4 4.8 %collective-permute-start.5 = (bf16[32,512]{1,0:T(8,128)(2,1)S(1)}, bf16[32,512]{1,0:T(8,128)(2,1)S(1)}, u32[]{:S(2)}, u32[]{:S(2)}) collective-permute-start(bf16[32,512]{1,0:T(8,128)(2,1)S(1)} %get-tuple-element.73), channel_id=1, source_target_pairs={{0,16},{4,20},{8,24},{12,28},{16,0},{20,4},{24,8},{28,12},{1,17},{... | collective-permute-start | bytes 98312 | tf_op jit(solution)/shard_map/ppermute | solution.py:31
  36.2 5.8 %collective-permute-start.6 = (bf16[32,512]{1,0:T(8,128)(2,1)S(1)}, bf16[32,512]{1,0:T(8,128)(2,1)S(1)}, u32[]{:S(2)}, u32[]{:S(2)}) collective-permute-start(bf16[32,512]{1,0:T(8,128)(2,1)S(1)} %get-tuple-element.74), channel_id=1, source_target_pairs={{0,24},{4,28},{8,16},{12,20},{16,8},{20,12},{24,0},{28,4},{1,25},{... | collective-permute-start | bytes 98312 | tf_op jit(solution)/shard_map/ppermute | solution.py:31
  42.0 5.9 %collective-permute-start.18 = (bf16[192,512]{1,0:T(8,128)(2,1)}, bf16[192,512]{1,0:T(8,128)(2,1)S(1)}, u32[]{:S(2)}, u32[]{:S(2)}) collective-permute-start(bf16[192,512]{1,0:T(8,128)(2,1)} %get-tuple-element.81), channel_id=1, source_target_pairs={{0,2},{1,3},{2,0},{3,1},{4,6},{5,7},{6,4},{7,5},{8,10},{9,11},{10,... | collective-permute-start | bytes 589832 | tf_op jit(solution)/shard_map/ppermute | solution.py:31
  42.3 5.9 %collective-permute-start.16 = (bf16[192,512]{1,0:T(8,128)(2,1)}, bf16[192,512]{1,0:T(8,128)(2,1)S(1)}, u32[]{:S(2)}, u32[]{:S(2)}) collective-permute-start(bf16[192,512]{1,0:T(8,128)(2,1)} %get-tuple-element.81), channel_id=1, source_target_pairs={{0,1},{1,0},{2,3},{3,2},{4,5},{5,4},{6,7},{7,6},{8,9},{9,8},{10,11... | collective-permute-start | bytes 589832 | tf_op jit(solution)/shard_map/ppermute | solution.py:31
  47.9 9.7 %collective-permute-start.21 = (bf16[192,512]{1,0:T(8,128)(2,1)S(1)}, bf16[192,512]{1,0:T(8,128)(2,1)S(1)}, u32[]{:S(2)}, u32[]{:S(2)}) collective-permute-start(bf16[192,512]{1,0:T(8,128)(2,1)S(1)} %collective-permute-done.20.refs_8_), channel_id=1, source_target_pairs={{0,4},{4,0},{8,12},{12,8},{16,20},{20,16},{24,28},{28,24},{1,5},{5... | collective-permute-start | bytes 589832 | tf_op jit(solution)/shard_map/ppermute | solution.py:31
  48.2 9.7 %collective-permute-start.19 = (bf16[192,512]{1,0:T(8,128)(2,1)S(1)}, bf16[192,512]{1,0:T(8,128)(2,1)S(1)}, u32[]{:S(2)}, u32[]{:S(2)}) collective-permute-start(bf16[192,512]{1,0:T(8,128)(2,1)S(1)} %collective-permute-done.18.refs_6_), channel_id=1, source_target_pairs={{0,4},{4,0},{8,12},{12,8},{16,20},{20,16},{24,28},{28,24},{1,5},{5... | collective-permute-start | bytes 589832 | tf_op jit(solution)/shard_map/ppermute | solution.py:31
  48.4 9.5 %collective-permute-start.17 = (bf16[192,512]{1,0:T(8,128)(2,1)S(1)}, bf16[192,512]{1,0:T(8,128)(2,1)S(1)}, u32[]{:S(2)}, u32[]{:S(2)}) collective-permute-start(bf16[192,512]{1,0:T(8,128)(2,1)S(1)} %collective-permute-done.16.refs_4_), channel_id=1, source_target_pairs={{0,4},{4,0},{8,12},{12,8},{16,20},{20,16},{24,28},{28,24},{1,5},{5... | collective-permute-start | bytes 589832 | tf_op jit(solution)/shard_map/ppermute | solution.py:31
  54.4 4.9 %collective-permute-start.13 = (bf16[96,512]{1,0:T(8,128)(2,1)S(1)}, bf16[96,512]{1,0:T(8,128)(2,1)S(1)}, u32[]{:S(2)}, u32[]{:S(2)}) collective-permute-start(bf16[96,512]{1,0:T(8,128)(2,1)S(1)} %get-tuple-element.78), channel_id=1, source_target_pairs={{0,1},{1,0},{2,3},{3,2},{4,5},{5,4},{6,7},{7,6},{8,9},{9,8},{10,11... | collective-permute-start | bytes 294920 | tf_op jit(solution)/shard_map/ppermute | solution.py:31
  55.6 6.1 %collective-permute-start.14 = (bf16[96,512]{1,0:T(8,128)(2,1)S(1)}, bf16[96,512]{1,0:T(8,128)(2,1)S(1)}, u32[]{:S(2)}, u32[]{:S(2)}) collective-permute-start(bf16[96,512]{1,0:T(8,128)(2,1)S(1)} %get-tuple-element.79), channel_id=1, source_target_pairs={{0,2},{1,3},{2,0},{3,1},{4,6},{5,7},{6,4},{7,5},{8,10},{9,11},{10,... | collective-permute-start | bytes 294920 | tf_op jit(solution)/shard_map/ppermute | solution.py:31
  57.6 5.5 %collective-permute-start.15 = (bf16[96,512]{1,0:T(8,128)(2,1)S(1)}, bf16[96,512]{1,0:T(8,128)(2,1)S(1)}, u32[]{:S(2)}, u32[]{:S(2)}) collective-permute-start(bf16[96,512]{1,0:T(8,128)(2,1)S(1)} %get-tuple-element.80), channel_id=1, source_target_pairs={{0,3},{1,2},{2,1},{3,0},{4,7},{5,6},{6,5},{7,4},{8,11},{9,10},{10,... | collective-permute-start | bytes 294920 | tf_op jit(solution)/shard_map/ppermute | solution.py:31
  65.1 5.8 %collective-permute-start.24 = (bf16[96,512]{1,0:T(8,128)(2,1)S(1)}, bf16[96,512]{1,0:T(8,128)(2,1)S(1)}, u32[]{:S(2)}, u32[]{:S(2)}) collective-permute-start(bf16[96,512]{1,0:T(8,128)(2,1)S(1)} %get-tuple-element.92.refs_13_.refs_4_), channel_id=1, source_target_pairs={{0,3},{1,2},{2,1},{3,0},{4,7},{5,6},{6,5},{7,4},{8,11},{9,10},{10,... | collective-permute-start | bytes 294920 | tf_op jit(solution)/shard_map/ppermute | solution.py:31
  66.2 5.5 %collective-permute-start.23 = (bf16[96,512]{1,0:T(8,128)(2,1)S(1)}, bf16[96,512]{1,0:T(8,128)(2,1)S(1)}, u32[]{:S(2)}, u32[]{:S(2)}) collective-permute-start(bf16[96,512]{1,0:T(8,128)(2,1)S(1)} %get-tuple-element.92.refs_13_.refs_4_), channel_id=1, source_target_pairs={{0,2},{1,3},{2,0},{3,1},{4,6},{5,7},{6,4},{7,5},{8,10},{9,11},{10,... | collective-permute-start | bytes 294920 | tf_op jit(solution)/shard_map/ppermute | solution.py:31
  67.3 4.6 %collective-permute-start.22 = (bf16[96,512]{1,0:T(8,128)(2,1)S(1)}, bf16[96,512]{1,0:T(8,128)(2,1)S(1)}, u32[]{:S(2)}, u32[]{:S(2)}) collective-permute-start(bf16[96,512]{1,0:T(8,128)(2,1)S(1)} %get-tuple-element.92.refs_13_.refs_4_), channel_id=1, source_target_pairs={{0,1},{1,0},{2,3},{3,2},{4,5},{5,4},{6,7},{7,6},{8,9},{9,8},{10,11... | collective-permute-start | bytes 294920 | tf_op jit(solution)/shard_map/ppermute | solution.py:31
  76.5 11.5 %collective-permute-start.25 = (bf16[1088,512]{1,0:T(8,128)(2,1)S(1)}, bf16[1088,512]{1,0:T(8,128)(2,1)S(1)}, u32[]{:S(2)}, u32[]{:S(2)}) collective-permute-start(bf16[1088,512]{1,0:T(8,128)(2,1)S(1)} %get-tuple-element.97), channel_id=1, source_target_pairs={{0,4},{4,0},{8,12},{12,8},{16,20},{20,16},{24,28},{28,24},{1,5},{5... | collective-permute-start | bytes 3342344 | tf_op jit(solution)/shard_map/ppermute | solution.py:31
  76.5 6.8 %collective-permute-start.26 = (bf16[96,768]{1,0:T(8,128)(2,1)S(1)}, bf16[96,768]{1,0:T(8,128)(2,1)S(1)}, u32[]{:S(2)}, u32[]{:S(2)}) collective-permute-start(bf16[96,768]{1,0:T(8,128)(2,1)S(1)} %get-tuple-element.99), channel_id=1, source_target_pairs={{0,1},{1,0},{2,3},{3,2},{4,5},{5,4},{6,7},{7,6},{8,9},{9,8},{10,11... | collective-permute-start | bytes 442376 | tf_op jit(solution)/shard_map/ppermute | solution.py:31
  77.9 9.1 %collective-permute-start.27 = (bf16[96,768]{1,0:T(8,128)(2,1)S(1)}, bf16[96,768]{1,0:T(8,128)(2,1)S(1)}, u32[]{:S(2)}, u32[]{:S(2)}) collective-permute-start(bf16[96,768]{1,0:T(8,128)(2,1)S(1)} %get-tuple-element.100), channel_id=1, source_target_pairs={{0,2},{1,3},{2,0},{3,1},{4,6},{5,7},{6,4},{7,5},{8,10},{9,11},{10,... | collective-permute-start | bytes 442376 | tf_op jit(solution)/shard_map/ppermute | solution.py:31
  79.0 8.0 %collective-permute-start.28 = (bf16[96,768]{1,0:T(8,128)(2,1)S(1)}, bf16[96,768]{1,0:T(8,128)(2,1)S(1)}, u32[]{:S(2)}, u32[]{:S(2)}) collective-permute-start(bf16[96,768]{1,0:T(8,128)(2,1)S(1)} %get-tuple-element.101), channel_id=1, source_target_pairs={{0,3},{1,2},{2,1},{3,0},{4,7},{5,6},{6,5},{7,4},{8,11},{9,10},{10,... | collective-permute-start | bytes 442376 | tf_op jit(solution)/shard_map/ppermute | solution.py:31
  87.9 3.9 %collective-permute-start.29 = (bf16[192,512]{1,0:T(8,128)(2,1)S(1)}, bf16[192,512]{1,0:T(8,128)(2,1)S(1)}, u32[]{:S(2)}, u32[]{:S(2)}) collective-permute-start(bf16[192,512]{1,0:T(8,128)(2,1)S(1)} %get-tuple-element.103), channel_id=1, source_target_pairs={{0,4},{4,0},{8,12},{12,8},{16,20},{20,16},{24,28},{28,24},{1,5},{5... | collective-permute-start | bytes 589832 | tf_op jit(solution)/shard_map/ppermute | solution.py:31
  88.2 9.2 %collective-permute-start.36 = (bf16[256,512]{1,0:T(8,128)(2,1)S(1)}, bf16[256,512]{1,0:T(8,128)(2,1)S(1)}, u32[]{:S(2)}, u32[]{:S(2)}) collective-permute-start(bf16[256,512]{1,0:T(8,128)(2,1)S(1)} %get-tuple-element.115), channel_id=1, source_target_pairs={{0,1},{1,0},{2,3},{3,2},{4,5},{5,4},{6,7},{7,6},{8,9},{9,8},{10,11... | collective-permute-start | bytes 786440 | tf_op jit(solution)/shard_map/ppermute | solution.py:31
  89.1 12.2 %collective-permute-start.37 = (bf16[256,512]{1,0:T(8,128)(2,1)S(1)}, bf16[256,512]{1,0:T(8,128)(2,1)S(1)}, u32[]{:S(2)}, u32[]{:S(2)}) collective-permute-start(bf16[256,512]{1,0:T(8,128)(2,1)S(1)} %get-tuple-element.116), channel_id=1, source_target_pairs={{0,2},{1,3},{2,0},{3,1},{4,6},{5,7},{6,4},{7,5},{8,10},{9,11},{10,... | collective-permute-start | bytes 786440 | tf_op jit(solution)/shard_map/ppermute | solution.py:31
  90.0 13.1 %collective-permute-start.38 = (bf16[256,512]{1,0:T(8,128)(2,1)S(1)}, bf16[256,512]{1,0:T(8,128)(2,1)S(1)}, u32[]{:S(2)}, u32[]{:S(2)}) collective-permute-start(bf16[256,512]{1,0:T(8,128)(2,1)S(1)} %get-tuple-element.117), channel_id=1, source_target_pairs={{0,3},{1,2},{2,1},{3,0},{4,7},{5,6},{6,5},{7,4},{8,11},{9,10},{10,... | collective-permute-start | bytes 786440 | tf_op jit(solution)/shard_map/ppermute | solution.py:31
  91.9 15.9 %collective-permute-start.30 = (bf16[80,512]{1,0:T(8,128)(2,1)S(1)}, bf16[80,512]{1,0:T(8,128)(2,1)S(1)}, u32[]{:S(2)}, u32[]{:S(2)}) collective-permute-start(bf16[80,512]{1,0:T(8,128)(2,1)S(1)} %get-tuple-element.105), channel_id=1, source_target_pairs={{0,8},{4,12},{8,0},{12,4},{16,24},{20,28},{24,16},{28,20},{1,9},{5... | collective-permute-start | bytes 245768 | tf_op jit(solution)/shard_map/ppermute | solution.py:31
  92.0 15.8 %collective-permute-start.31 = (bf16[80,512]{1,0:T(8,128)(2,1)S(1)}, bf16[80,512]{1,0:T(8,128)(2,1)S(1)}, u32[]{:S(2)}, u32[]{:S(2)}) collective-permute-start(bf16[80,512]{1,0:T(8,128)(2,1)S(1)} %get-tuple-element.106), channel_id=1, source_target_pairs={{0,16},{4,20},{8,24},{12,28},{16,0},{20,4},{24,8},{28,12},{1,17},{... | collective-permute-start | bytes 245768 | tf_op jit(solution)/shard_map/ppermute | solution.py:31
  97.4 10.4 %collective-permute-start.32 = (bf16[80,512]{1,0:T(8,128)(2,1)S(1)}, bf16[80,512]{1,0:T(8,128)(2,1)S(1)}, u32[]{:S(2)}, u32[]{:S(2)}) collective-permute-start(bf16[80,512]{1,0:T(8,128)(2,1)S(1)} %get-tuple-element.107), channel_id=1, source_target_pairs={{0,24},{4,28},{8,16},{12,20},{16,8},{20,12},{24,0},{28,4},{1,25},{... | collective-permute-start | bytes 245768 | tf_op jit(solution)/shard_map/ppermute | solution.py:31
  103.3 4.5 %collective-permute-start.39 = (bf16[64,512]{1,0:T(8,128)(2,1)S(1)}, bf16[64,512]{1,0:T(8,128)(2,1)S(1)}, u32[]{:S(2)}, u32[]{:S(2)}) collective-permute-start(bf16[64,512]{1,0:T(8,128)(2,1)S(1)} %get-tuple-element.119), channel_id=1, source_target_pairs={{0,8},{4,12},{8,0},{12,4},{16,24},{20,28},{24,16},{28,20},{1,9},{5... | collective-permute-start | bytes 196616 | tf_op jit(solution)/shard_map/ppermute | solution.py:31
  103.4 8.7 %collective-permute-start.40 = (bf16[64,512]{1,0:T(8,128)(2,1)S(1)}, bf16[64,512]{1,0:T(8,128)(2,1)S(1)}, u32[]{:S(2)}, u32[]{:S(2)}) collective-permute-start(bf16[64,512]{1,0:T(8,128)(2,1)S(1)} %get-tuple-element.120), channel_id=1, source_target_pairs={{0,16},{4,20},{8,24},{12,28},{16,0},{20,4},{24,8},{28,12},{1,17},{... | collective-permute-start | bytes 196616 | tf_op jit(solution)/shard_map/ppermute | solution.py:31
  107.8 6.1 %collective-permute-start.41 = (bf16[64,512]{1,0:T(8,128)(2,1)S(1)}, bf16[64,512]{1,0:T(8,128)(2,1)S(1)}, u32[]{:S(2)}, u32[]{:S(2)}) collective-permute-start(bf16[64,512]{1,0:T(8,128)(2,1)S(1)} %get-tuple-element.121), channel_id=1, source_target_pairs={{0,24},{4,28},{8,16},{12,20},{16,8},{20,12},{24,0},{28,4},{1,25},{... | collective-permute-start | bytes 196616 | tf_op jit(solution)/shard_map/ppermute | solution.py:31
  113.9 10.2 %collective-permute-start.44 = (bf16[112,512]{1,0:T(8,128)(2,1)S(1)}, bf16[112,512]{1,0:T(8,128)(2,1)S(1)}, u32[]{:S(2)}, u32[]{:S(2)}) collective-permute-start(bf16[112,512]{1,0:T(8,128)(2,1)S(1)} %shard_map.197.refs_0_), channel_id=1, source_target_pairs={{0,24},{4,28},{8,16},{12,20},{16,8},{20,12},{24,0},{28,4},{1,25},{... | collective-permute-start | bytes 344072 | tf_op jit(solution)/shard_map/ppermute | solution.py:31
  115.4 9.3 %collective-permute-start.43 = (bf16[112,512]{1,0:T(8,128)(2,1)S(1)}, bf16[112,512]{1,0:T(8,128)(2,1)S(1)}, u32[]{:S(2)}, u32[]{:S(2)}) collective-permute-start(bf16[112,512]{1,0:T(8,128)(2,1)S(1)} %shard_map.197.refs_0_), channel_id=1, source_target_pairs={{0,16},{4,20},{8,24},{12,28},{16,0},{20,4},{24,8},{28,12},{1,17},{... | collective-permute-start | bytes 344072 | tf_op jit(solution)/shard_map/ppermute | solution.py:31
  115.4 9.3 %collective-permute-start.42 = (bf16[112,512]{1,0:T(8,128)(2,1)S(1)}, bf16[112,512]{1,0:T(8,128)(2,1)S(1)}, u32[]{:S(2)}, u32[]{:S(2)}) collective-permute-start(bf16[112,512]{1,0:T(8,128)(2,1)S(1)} %shard_map.197.refs_0_), channel_id=1, source_target_pairs={{0,8},{4,12},{8,0},{12,4},{16,24},{20,28},{24,16},{28,20},{1,9},{5... | collective-permute-start | bytes 344072 | tf_op jit(solution)/shard_map/ppermute | solution.py:31
  119.4 4.7 %collective-permute-start.33 = (bf16[96,512]{1,0:T(8,128)(2,1)S(1)}, bf16[96,512]{1,0:T(8,128)(2,1)S(1)}, u32[]{:S(2)}, u32[]{:S(2)}) collective-permute-start(bf16[96,512]{1,0:T(8,128)(2,1)S(1)} %get-tuple-element.109), channel_id=1, source_target_pairs={{0,1},{1,0},{2,3},{3,2},{4,5},{5,4},{6,7},{7,6},{8,9},{9,8},{10,11... | collective-permute-start | bytes 294920 | tf_op jit(solution)/shard_map/ppermute | solution.py:31
  120.8 4.6 %collective-permute-start.34 = (bf16[96,512]{1,0:T(8,128)(2,1)S(1)}, bf16[96,512]{1,0:T(8,128)(2,1)S(1)}, u32[]{:S(2)}, u32[]{:S(2)}) collective-permute-start(bf16[96,512]{1,0:T(8,128)(2,1)S(1)} %get-tuple-element.110), channel_id=1, source_target_pairs={{0,2},{1,3},{2,0},{3,1},{4,6},{5,7},{6,4},{7,5},{8,10},{9,11},{10,... | collective-permute-start | bytes 294920 | tf_op jit(solution)/shard_map/ppermute | solution.py:31
  124.0 7.7 %collective-permute-start.45 = (bf16[112,512]{1,0:T(8,128)(2,1)S(1)}, bf16[112,512]{1,0:T(8,128)(2,1)S(1)}, u32[]{:S(2)}, u32[]{:S(2)}) collective-permute-start(bf16[112,512]{1,0:T(8,128)(2,1)S(1)} %shard_map.197.refs_0_), channel_id=1, source_target_pairs={{0,4},{4,0},{8,12},{12,8},{16,20},{20,16},{24,28},{28,24},{1,5},{5... | collective-permute-start | bytes 344072 | tf_op jit(solution)/shard_map/ppermute | solution.py:31
  124.0 7.7 %collective-permute-start.48 = (bf16[112,512]{1,0:T(8,128)(2,1)S(1)}, bf16[112,512]{1,0:T(8,128)(2,1)S(1)}, u32[]{:S(2)}, u32[]{:S(2)}) collective-permute-start(bf16[112,512]{1,0:T(8,128)(2,1)S(1)} %collective-permute-done.44.refs_3_), channel_id=1, source_target_pairs={{0,4},{4,0},{8,12},{12,8},{16,20},{20,16},{24,28},{28,24},{1,5},{5... | collective-permute-start | bytes 344072 | tf_op jit(solution)/shard_map/ppermute | solution.py:31
  124.8 6.9 %collective-permute-start.47 = (bf16[112,512]{1,0:T(8,128)(2,1)S(1)}, bf16[112,512]{1,0:T(8,128)(2,1)S(1)}, u32[]{:S(2)}, u32[]{:S(2)}) collective-permute-start(bf16[112,512]{1,0:T(8,128)(2,1)S(1)} %collective-permute-done.43.refs_2_), channel_id=1, source_target_pairs={{0,4},{4,0},{8,12},{12,8},{16,20},{20,16},{24,28},{28,24},{1,5},{5... | collective-permute-start | bytes 344072 | tf_op jit(solution)/shard_map/ppermute | solution.py:31
  124.8 6.9 %collective-permute-start.46 = (bf16[112,512]{1,0:T(8,128)(2,1)S(1)}, bf16[112,512]{1,0:T(8,128)(2,1)S(1)}, u32[]{:S(2)}, u32[]{:S(2)}) collective-permute-start(bf16[112,512]{1,0:T(8,128)(2,1)S(1)} %collective-permute-done.42.refs_1_), channel_id=1, source_target_pairs={{0,4},{4,0},{8,12},{12,8},{16,20},{20,16},{24,28},{28,24},{1,5},{5... | collective-permute-start | bytes 344072 | tf_op jit(solution)/shard_map/ppermute | solution.py:31
  125.4 5.6 %collective-permute-start.35 = (bf16[96,512]{1,0:T(8,128)(2,1)S(1)}, bf16[96,512]{1,0:T(8,128)(2,1)S(1)}, u32[]{:S(2)}, u32[]{:S(2)}) collective-permute-start(bf16[96,512]{1,0:T(8,128)(2,1)S(1)} %get-tuple-element.111), channel_id=1, source_target_pairs={{0,3},{1,2},{2,1},{3,0},{4,7},{5,6},{6,5},{7,4},{8,11},{9,10},{10,... | collective-permute-start | bytes 294920 | tf_op jit(solution)/shard_map/ppermute | solution.py:31
  (11 other events, 301.3 us)
